TPU v7x, 512 devices: a whole 4x4x16 slice. The times are simulated.
512 devices in a mesh: seq: 128 (over z, y, core), head: 4 (over x).
Axes of the slice: x: 4, y: 4, z: 16, core: 2. Of those that a mesh axis runs over, the one named last changes fastest.
Arguments:
- queries: bfloat16 [65536, 2048], P('seq', 'head'), may hold values from -6 to 6
- key_vectors: bfloat16 [65536, 2048], P('seq', 'head'), may hold values from -6 to 6
- value_vectors: bfloat16 [65536, 2048], P('seq', 'head'), may hold values from -6 to 6
- gate_input: bfloat16 [65536, 2048], P('seq', 'head'), may hold values from -6 to 6
- out_weight: bfloat16 [2048, 4096], P('seq', 'head'), may hold values from -0.125 to 0.125
Outputs:
- layer_output: bfloat16 [65536, 4096], P('seq', 'head')
All inputs are finite; a program needn't handle non-finite values.
Results may differ from a plain program's by a relative error of at most 0.0057.
Values may be sent and summed in bfloat16 or wider, within the bound.
No kernel may reach another device: no remote copies, remote signals or barrier semaphores. Data moves between devices by JAX's collectives and lax.ppermute only.
A program may use at most 64 MiB of HBM per device.

v0:
```python
import jax
import jax.numpy as jnp
from jax import lax
from jax.sharding import Mesh
from jax.sharding import PartitionSpec as P

HD = 128
SEQ = ("seq_0", "seq_1", "seq_2")


def nothing_yet(shard, identity):
    return jnp.broadcast_to(jnp.asarray(identity, shard.dtype), shard.shape)


def carried_in(shard, axes, combine, identity):
    before = start = nothing_yet(shard, identity)
    total = shard
    for axis in reversed(axes):
        count, position = (lax.axis_size(axis), lax.axis_index(axis))
        pieces = lax.all_gather(total, axis)
        inside, total = (start, start)
        for k in range(count):
            passed = k < position
            total = combine(total, pieces[k])
            inside = jnp.where(passed, total, inside)
        before = combine(inside, before)
    return before


def sent_to_all(shard, axis):
    count = lax.axis_size(axis)
    return lax.all_to_all(
        jnp.broadcast_to(shard[None], (count, *shard.shape)), axis, 0, 0, tiled=True
    )


def of_everyone(shard, axis):
    everything = sent_to_all(shard, axis)
    return jnp.sum(everything, axis=0)


def in_order(blocks, dim):
    shape = list(blocks.shape[1:])
    shape[dim] *= blocks.shape[0]
    return jnp.moveaxis(blocks, 0, dim).reshape(shape)


def gather_directly(shard, axis, dim):
    blocks = sent_to_all(shard, axis)
    return in_order(blocks, dim)


def stacked_from(shard, axes, sequence):
    blocks = shard[None]
    for k in sequence:
        blocks = lax.all_gather(blocks, axes[k], axis=0, tiled=True)
    block = [lax.axis_size(axes[k]) for k in reversed(sequence)]
    blocks = blocks.reshape(*block, *shard.shape)
    turned = sorted(range(len(sequence)), key=lambda place: sequence[len(sequence) - 1 - place])
    return blocks.transpose(*turned, *range(len(sequence), blocks.ndim)).reshape(-1, *shard.shape)


def gathered_by_axis(shard, axes, sequence, dim):
    return in_order(stacked_from(shard, axes, sequence), dim)


def add_states(earlier, later):
    return earlier + later


def carried(own_state):
    return carried_in(own_state, SEQ, add_states, jnp.zeros_like(own_state))


def in_shard(qhead, khead, vhead, scale):
    rows = qhead.shape[0]
    step = min(rows, 512)
    scores = jnp.einsum("thd,shd->hts", qhead, khead, preferred_element_type=jnp.float32) * scale
    rowpos = 0 + lax.broadcasted_iota(jnp.int32, (step, step), 0)
    colpos = lax.broadcasted_iota(jnp.int32, (step, step), 1)
    scores = jnp.where((colpos <= rowpos)[None, :, :], scores, 0.0).astype(jnp.bfloat16)
    pieces = jnp.einsum("hts,she->the", scores, vhead, preferred_element_type=jnp.float32)
    return pieces


def per_device(queries, key_vectors, value_vectors, gate_input, out_weight):
    rows, width = queries.shape
    heads = width // HD
    scale = HD ** (-0.5)
    qhead = queries.reshape(rows, heads, HD)
    khead = key_vectors.reshape(rows, heads, HD)
    vhead = value_vectors.reshape(rows, heads, HD)
    own_state = jnp.einsum("thd,the->hde", khead, vhead, preferred_element_type=jnp.float32)
    local = in_shard(qhead, khead, vhead, scale)
    prefix = carried(own_state)
    inter = (
        jnp.einsum(
            "thd,hde->the", qhead, prefix.astype(jnp.bfloat16), preferred_element_type=jnp.float32
        )
        * scale
    )
    attn = (local + inter).reshape(rows, width)
    squares = jnp.sum(attn * attn, axis=1)
    hidden = (attn * jax.nn.silu(gate_input.astype(jnp.float32))).astype(jnp.bfloat16)
    total = of_everyone(squares, "head")
    features = gather_directly(hidden, "head", 1)
    full_block = gathered_by_axis(out_weight, SEQ, (1, 0, 2), 0)
    projected = jnp.dot(features, full_block, preferred_element_type=jnp.float32)
    mean_square = total / features.shape[1]
    return (projected * lax.rsqrt(mean_square + 1e-06)[:, None]).astype(jnp.bfloat16)


def solution(mesh):
    torus = Mesh(
        mesh.devices.reshape(16, 4, 2, mesh.shape["head"]), ("seq_0", "seq_1", "seq_2", "head")
    )
    return jax.shard_map(
        per_device,
        mesh=torus,
        in_specs=(P(SEQ, "head"), P(SEQ, "head"), P(SEQ, "head"), P(SEQ, "head"), P(SEQ, "head")),
        out_specs=P(SEQ, "head"),
        check_vma=False,
    )
```

profile of v0, /device:TPU:8, one launch (start us, length us, event | category | flops | bytes accessed | tf_op | source)
XLA Modules:
  0.0 251.4 jit_solution(18268697951905926214)
XLA Ops:
  6.5 1.3 copy.62
  7.9 1.3 fusion.10
  9.2 2.2 all-gather
  11.4 0.7 slice_add_fusion.18
  12.1 0.0 all-gather.14.cloned.1.call-update
  12.1 0.0 all-gather.10.cloned.1.call-start
  12.2 15.3 %all-gather.1 = bf16[64,1024]{1,0:T(8,128)(2,1)} all-gather(bf16[16,1024]{1,0:T(8,128)(2,1)S(1)} %copy-done.3), channel_id=3, replica_groups=mesh['seq_0'=16,'seq_1'=4,'seq_2'=2,'head'=4] {'seq_1'}, dimensions={0}, use_global_device_ids=true | all-gather | bytes 163840 | tf_op jit(solution)/shard_map/all_gather | solution.py:56
  27.5 0.0 all-gather.10.cloned.1.call-update
  27.5 0.0 all-gather.8.cloned.1.call-start
  27.6 19.7 %all-gather.14.cloned.1.call-done = f32[16,128,128]{2,1,0:T(8,128)} async-done(((f32[4,128,128]{2,1,0:T(8,128)}), f32[16,128,128]{2,1,0:T(8,128)}) %all-gather.14.cloned.1.call-update) | async-done | bytes 1048592 | tf_op jit(solution)/shard_map/all_gather | solution.py:20
  47.3 1.9 fusion.24
  49.2 0.0 all-gather.8.cloned.1.call-update
  49.3 0.0 copy-start.2
  49.3 0.0 all-gather.12.cloned.1.call-start
  49.3 74.3 %all-gather.10.cloned.1.call-done = bf16[64,16,1024]{2,1,0:T(8,128)(2,1)} async-done(((bf16[4,16,1024]{2,1,0:T(8,128)(2,1)}), bf16[64,16,1024]{2,1,0:T(8,128)(2,1)}) %all-gather.10.cloned.1.call-update) | async-done | bytes 2097168 | tf_op jit(solution)/shard_map/all_gather | solution.py:56
  123.6 0.0 all-gather.12.cloned.1.call-update
  123.7 0.1 iota_compare_fusion
  123.8 76.8 %all-gather.8.cloned.1.call-done = f32[16,4,128,128]{3,2,1,0:T(8,128)} async-done(((f32[1,4,128,128]{3,2,1,0:T(8,128)}), f32[16,4,128,128]{3,2,1,0:T(8,128)}) %all-gather.8.cloned.1.call-update) | async-done | bytes 4194320 | tf_op jit(solution)/shard_map/all_gather | solution.py:20
  200.6 4.0 %fusion.3 = f32[512,4,128]{0,2,1:T(8,128)} fusion(f32[16,4,128,128]{3,2,1,0:T(8,128)} %all-gather.8.cloned.1.call-done, f32[1,4,128,128]{3,2,1,0:T(8,128)} %fusion.24, f32[4,128,128]{2,1,0:T(8,128)S(1)} %copy-done.1, f32[16,128,128]{2,1,0:T(8,128)} %all-gather.14.cloned.1.call-done, f32[8,128,128]{2,1,0:T(8,128)S(1)} %all-gather, pred[]{:T(512)S(6)} %gt.66, ...), kind=kOutput, calls=%fused_computation.6 | convolution fusion | flops 70123520 | bytes 7340054 | tf_op jit(solution)/shard_map/thd,hde->the/dot_general | solution.py:97
  204.6 2.6 %multiply_reduce_fusion = (f32[512]{0:T(512)S(1)}, f32[512,4,128]{0,2,1:T(8,128)S(1)}) fusion(f32[512,4,128]{0,2,1:T(8,128)} %fusion.3, bf16[512,4,128]{0,2,1:T(8,128)(2,1)S(1)} %bitcast.76, pred[512,512]{1,0:T(8,128)(4,1)S(1)} %iota_compare_fusion, bf16[512,512]{1,0:T(8,128)(2,1)S(1)} %copy-done.2, bf16[512,512]{1,0:T(8,128)(2,1)S(1)} %copy-done), kind=kOutput, calls=%fused_computation.13 | convolution fusion | flops 540802560 | bytes 3934208 | tf_op jit(solution)/shard_map/hts,she->the/dot_general | solution.py:82
  207.2 0.3 copy.56
  207.6 0.6 broadcast_in_dim.37
  208.2 4.3 %all-to-all-start.1 = ((f32[4,1,512]{2,1,0:T(1,128)}), f32[4,1,512]{2,1,0:T(1,128)S(1)}, u32[]{:S(2)}, u32[]{:S(2)}) async-start(f32[4,1,512]{2,1,0:T(1,128)} %broadcast_in_dim.37), calls=%async_computation.1 | async-start | bytes 16384 | tf_op jit(solution)/shard_map/all_to_all | solution.py:32
  212.4 1.4 fusion.8
  213.8 0.2 copy.57
  214.0 3.8 %all-to-all-done.1 = f32[4,1,512]{2,1,0:T(1,128)S(1)} async-done(((f32[4,1,512]{2,1,0:T(1,128)}), f32[4,1,512]{2,1,0:T(1,128)S(1)}, u32[]{:S(2)}, u32[]{:S(2)}) %all-to-all-start.1) | async-done | bytes 8224 | tf_op jit(solution)/shard_map/all_to_all | solution.py:32
  217.8 1.5 broadcast_in_dim.35
  219.3 3.6 %all-to-all-start = ((bf16[4,512,512]{1,2,0:T(8,128)(2,1)}), bf16[4,512,512]{1,2,0:T(8,128)(2,1)S(1)}, u32[]{:S(2)}, u32[]{:S(2)}) async-start(bf16[4,512,512]{1,2,0:T(8,128)(2,1)} %broadcast_in_dim.35), calls=%async_computation | async-start | bytes 4194304 | tf_op jit(solution)/shard_map/all_to_all | solution.py:32
  222.9 0.3 all-gather.12.cloned.1.call-done
  223.2 5.0 %copy.58 = bf16[16,4,2,16,1024]{4,3,2,1,0:T(8,128)(2,1)} copy(bf16[16,4,2,16,1024]{4,3,1,0,2:T(8,128)(2,1)} %bitcast.72) | data formatting | bytes 8388608 | tf_op jit(solution)/shard_map/transpose | solution.py:60
  228.2 11.2 %all-to-all-done = bf16[4,512,512]{1,2,0:T(8,128)(2,1)S(1)} async-done(((bf16[4,512,512]{1,2,0:T(8,128)(2,1)}), bf16[4,512,512]{1,2,0:T(8,128)(2,1)S(1)}, u32[]{:S(2)}, u32[]{:S(2)}) %all-to-all-start) | async-done | bytes 2097184 | tf_op jit(solution)/shard_map/all_to_all | solution.py:32
  239.4 5.5 %multiply_convert_fusion = bf16[512,1024]{1,0:T(8,128)(2,1)} fusion(bf16[512,2048]{0,1:T(8,128)(2,1)S(1)} %bitcast.74, bf16[2048,1024]{1,0:T(8,128)(2,1)} %bitcast.73, f32[512]{0:T(512)S(1)} %add_rsqrt_fusion), kind=kOutput, calls=%fused_computation.1 | convolution fusion | flops 2148532224 | bytes 7342080 | tf_op jit(solution)/shard_map/dot_general | solution.py:108
  (10 shorter events, 0.0 us)
Async XLA Ops:
  6.5 194.1 %copy-start = (bf16[512,512]{1,0:T(8,128)(2,1)S(1)}, bf16[512,512]{1,0:T(8,128)(2,1)}, u32[]{:S(2)}) copy-start(bf16[512,512]{1,0:T(8,128)(2,1)} %param.5) | copy-start | bytes 1572868
  6.5 5.7 %copy-start.3 = (bf16[16,1024]{1,0:T(8,128)(2,1)S(1)}, bf16[16,1024]{1,0:T(8,128)(2,1)}, u32[]{:S(2)}) copy-start(bf16[16,1024]{1,0:T(8,128)(2,1)} %param.9) | copy-start | bytes 98308
  6.5 40.8 %all-gather.14.cloned.1.call-start = ((), (), s32[]{:S(2)}) async-start(), calls=%async_computation.5 | async-start | bytes 1310720 | tf_op jit(solution)/shard_map/all_gather | solution.py:20
  12.1 188.5 %copy-start.1 = (f32[4,128,128]{2,1,0:T(8,128)S(1)}, f32[4,128,128]{2,1,0:T(8,128)}, u32[]{:S(2)}) copy-start(f32[4,128,128]{2,1,0:T(8,128)} %slice_add_fusion.18) | copy-start | bytes 786436
  12.1 111.5 %all-gather.10.cloned.1.call-start = ((), (), s32[]{:S(2)}) async-start(), calls=%async_computation.3 | async-start | bytes 2228224 | tf_op jit(solution)/shard_map/all_gather | solution.py:56
  27.5 173.1 %all-gather.8.cloned.1.call-start = ((), (), s32[]{:S(2)}) async-start(), calls=%async_computation.2 | async-start | bytes 4456448 | tf_op jit(solution)/shard_map/all_gather | solution.py:20
  49.3 155.4 %copy-start.2 = (bf16[512,512]{1,0:T(8,128)(2,1)S(1)}, bf16[512,512]{1,0:T(8,128)(2,1)}, u32[]{:S(2)}) copy-start(bf16[512,512]{1,0:T(8,128)(2,1)} %param.7) | copy-start | bytes 1572868
  49.3 173.9 %all-gather.12.cloned.1.call-start = ((), (), s32[]{:S(2)}) async-start(), calls=%async_computation.4 | async-start | bytes 6291456 | tf_op jit(solution)/shard_map/all_gather | solution.py:56
  208.2 9.6 %all-to-all-start.1 = ((f32[4,1,512]{2,1,0:T(1,128)}), f32[4,1,512]{2,1,0:T(1,128)S(1)}, u32[]{:S(2)}, u32[]{:S(2)}) async-start(f32[4,1,512]{2,1,0:T(1,128)} %broadcast_in_dim.37), calls=%async_computation.1 | async-start | bytes 16384 | tf_op jit(solution)/shard_map/all_to_all | solution.py:32
  219.3 20.1 %all-to-all-start = ((bf16[4,512,512]{1,2,0:T(8,128)(2,1)}), bf16[4,512,512]{1,2,0:T(8,128)(2,1)S(1)}, u32[]{:S(2)}, u32[]{:S(2)}) async-start(bf16[4,512,512]{1,2,0:T(8,128)(2,1)} %broadcast_in_dim.35), calls=%async_computation | async-start | bytes 4194304 | tf_op jit(solution)/shard_map/all_to_all | solution.py:32
Sparse Core Ops, SparseCore 0:
  12.3 34.9 all-gather.13
  49.4 74.1 all-gather.9
  125.7 74.8 all-gather.7
  202.6 20.5 all-gather.11
where the time goes:
time: 252 us; the launch traced here: 251 us
  waiting for transfers between devices  186 us (74%)
  blocking collectives  17.5 us (7%)
  matrix products  13.4 us (5%)
  between operations  13.2 us (5%)
  local copies, waits for them, and re-layouts  8.97 us (4%)
  starting transfers between devices  8 us (3%)
  other arithmetic  4.14 us (2%)
    all_gather x2, waiting for transfers between devices, carried_in(): pieces = lax.all_gather(total, axis)  96.6 us
    all_gather x2, waiting for transfers between devices, stacked_from(): blocks = lax.all_gather(blocks, axes[k], axis=0, tiled=True)  74.5 us
    all_gather x1, blocking collectives, stacked_from(): blocks = lax.all_gather(blocks, axes[k], axis=0, tiled=True)  15.3 us
    all_to_all x2, waiting for transfers between devices, sent_to_all(): lax.all_to_all(jnp.broadcast_to(shard[None], (count, *shard.shape)), axis...  15 us
    all_to_all x2, starting transfers between devices, sent_to_all(): lax.all_to_all(jnp.broadcast_to(shard[None], (count, *shard.shape)), axis...  7.87 us
    dot_general x1, matrix products, per_device(): jnp.dot(features, full_block, preferred_element_type=jnp.float32)  5.51 us
  transfers between devices with their start and end apart: 6, of which 6 were waited for; matrix products, arithmetic and copies ran while one was open for 7% of the time, Pallas kernels for 0%

commit v1 on v0

v1 whole, which is shorter than its diff:
```python
import functools

import jax
import jax.numpy as jnp
from jax import lax
from jax.experimental import pallas as pl
from jax.experimental.pallas import tpu as pltpu
from jax.sharding import Mesh
from jax.sharding import PartitionSpec as P

HD = 128
ZH, ZL, Y, C, X = "zh", "zl", "y", "c", "x"
SEQ = (ZH, ZL, Y, C)
NEAR = (ZL, Y, C)
F32 = jnp.float32
BF16 = jnp.bfloat16
VMEM = pl.BlockSpec(memory_space=pltpu.VMEM)
ANY = pl.BlockSpec(memory_space=pl.ANY)


def call(body, outs, n_in, flops, nbytes, in_specs=None, scratch=()):
    return pl.pallas_call(
        body,
        out_shape=outs,
        in_specs=in_specs or [VMEM] * n_in,
        out_specs=jax.tree.map(lambda _: VMEM, outs),
        scratch_shapes=list(scratch),
        cost_estimate=pl.CostEstimate(
            flops=flops, bytes_accessed=nbytes, transcendentals=0
        ),
        compiler_params=pltpu.CompilerParams(vmem_limit_bytes=40 * 2**20),
    )


def state_body(k_ref, v_ref, s_ref):
    for h in range(k_ref.shape[1] // HD):
        cols = slice(h * HD, (h + 1) * HD)
        s_ref[h] = lax.dot_general(
            k_ref[:, cols], v_ref[:, cols], (((0,), (0,)), ((), ())),
            preferred_element_type=F32,
        )


def local_body(q_ref, k_ref, v_ref, o_ref):
    rows = q_ref.shape[0]
    blk = 256
    scale = HD ** (-0.5)
    for h in range(q_ref.shape[1] // HD):
        cols = slice(h * HD, (h + 1) * HD)
        for i in range(rows // blk):
            r = slice(i * blk, (i + 1) * blk)
            seen = slice(0, (i + 1) * blk)
            s = lax.dot_general(
                q_ref[r, cols], k_ref[seen, cols], (((1,), (1,)), ((), ())),
                preferred_element_type=F32,
            ) * scale
            t_pos = i * blk + lax.broadcasted_iota(jnp.int32, s.shape, 0)
            s_pos = lax.broadcasted_iota(jnp.int32, s.shape, 1)
            s = jnp.where(s_pos <= t_pos, s, 0.0).astype(BF16)
            o_ref[r, cols] = jnp.dot(s, v_ref[seen, cols], preferred_element_type=F32)


def near_prefix_body(r_ref, e_ref, t_ref):
    acc = jnp.zeros(r_ref.shape[1:], F32)
    for j in range(r_ref.shape[0]):
        e_ref[j] = acc
        acc = acc + r_ref[j]
    for j in range(t_ref.shape[0]):
        t_ref[j] = acc


def far_prefix_body(e_ref, t_ref, p_ref):
    me = lax.axis_index(ZH)
    base = jnp.zeros(t_ref.shape[1:], F32)
    for j in range(t_ref.shape[0]):
        base = base + jnp.where(j < me, t_ref[j], 0.0)
    for j in range(e_ref.shape[0]):
        p_ref[j] = (e_ref[j] + base).astype(BF16)


def hidden_body(q_ref, p_ref, l_ref, g_ref, o_ref):
    rows, width = q_ref.shape
    scale = HD ** (-0.5)
    squares = jnp.zeros((rows, HD), F32)
    for h in range(width // HD):
        cols = slice(h * HD, (h + 1) * HD)
        inter = jnp.dot(q_ref[:, cols], p_ref[h], preferred_element_type=F32)
        attn = l_ref[:, cols] + inter * scale
        squares = squares + attn * attn
        gate = g_ref[:, cols].astype(F32)
        hid = (attn * (gate / (1.0 + jnp.exp(-gate)))).astype(BF16)
        for j in range(o_ref.shape[0]):
            o_ref[j, :rows, cols] = hid
    row = jnp.sum(squares.T, axis=0, keepdims=True)
    hi = row.astype(BF16).astype(F32)
    mid = (row - hi).astype(BF16).astype(F32)
    lo = row - hi - mid
    place = lax.broadcasted_iota(jnp.int32, (16, rows), 0)
    extra = jnp.where(place == 0, hi, jnp.where(place == 1, mid, jnp.where(place == 2, lo, 0.0)))
    for j in range(o_ref.shape[0]):
        o_ref[j, rows:, :] = extra.astype(BF16)


def project_body(h_ref, mine_ref, other_ref, o_ref, w_ref, sem):
    me = lax.axis_index(C)
    copies = []
    for y in range(mine_ref.shape[0]):
        for n, (src, core) in enumerate(((mine_ref, me), (other_ref, 1 - me))):
            copies.append(pltpu.make_async_copy(src.at[y], w_ref.at[:, y, core], sem.at[y, n]))
    for copy in copies:
        copy.start()
    rows, width = o_ref.shape
    parts = h_ref.shape[0]
    each = h_ref.shape[2]
    heads = each // HD
    row = jnp.zeros((1, rows), F32)
    for s in range(parts):
        for j in range(3):
            row = row + h_ref[s, rows + j : rows + j + 1, :].astype(F32)
    inv = lax.rsqrt(row / (parts * each) + 1e-06)
    inv = jnp.broadcast_to(inv, (HD, rows)).T
    for copy in copies:
        copy.wait()
    blk = 256
    for i in range(rows // blk):
        r = slice(i * blk, (i + 1) * blk)
        for n in range(width // 256):
            c = slice(n * 256, (n + 1) * 256)
            acc = jnp.zeros((blk, 256), F32)
            for s in range(parts):
                w = w_ref[s * heads : (s + 1) * heads, :, :, :, c].reshape(each, 256)
                acc = acc + jnp.dot(h_ref[s, r, :], w, preferred_element_type=F32)
            o_ref[r, c] = (acc * inv[r, :1]).astype(BF16)


def spread(block, axes):
    n = 1
    for a in axes:
        n *= lax.axis_size(a)
    return jnp.broadcast_to(block[None], (n, *block.shape))


def swap(array, axes):
    return lax.all_to_all(array, axes, 0, 0, tiled=True)


def per_device(queries, key_vectors, value_vectors, gate_input, out_weight):
    rows, width = queries.shape
    heads = width // HD
    near = lax.axis_size(ZL) * lax.axis_size(Y) * lax.axis_size(C)
    far = lax.axis_size(ZH)
    group = lax.axis_size(X)
    cols = out_weight.shape[1]
    piece = (heads * HD // near, HD)
    f32 = functools.partial(jax.ShapeDtypeStruct, dtype=F32)
    bf16 = functools.partial(jax.ShapeDtypeStruct, dtype=BF16)

    by_z = swap(spread(out_weight, (ZH, ZL)), (ZH, ZL))
    by_z = by_z.reshape(-1, *out_weight.shape)
    state = call(state_body, f32((heads, HD, HD)), 2, 10**8, 2**20)(key_vectors, value_vectors)
    local = call(local_body, f32((rows, width)), 3, 5 * 10**8, 2**21)(
        queries, key_vectors, value_vectors
    )
    pieces = swap(state.reshape(near, *piece), NEAR)
    earlier, total = call(
        near_prefix_body, (f32((near, *piece)), f32((far, *piece))), 1, 10**6, 2**19
    )(pieces)
    totals = swap(total, (ZH,))
    prefix = call(far_prefix_body, bf16((near, *piece)), 2, 10**6, 2**19)(earlier, totals)
    prefix = swap(prefix, NEAR).reshape(heads, HD, HD)
    hidden = call(
        hidden_body, bf16((group, rows + 16, width)), 4, 10**8, 2**22
    )(queries, prefix, local, gate_input)
    features = swap(hidden, (X,))
    by_y = swap(spread(by_z, (Y,)), (Y,)).reshape(-1, *by_z.shape)
    other = lax.ppermute(by_y, C, ((0, 1), (1, 0)))
    full = (by_z.shape[0], by_y.shape[0], 2, *out_weight.shape)
    return call(
        project_body, bf16((rows, cols)), 3, 2 * 10**9, 8 * 2**20,
        in_specs=[VMEM, ANY, ANY],
        scratch=[pltpu.VMEM(full, BF16), pltpu.SemaphoreType.DMA((by_y.shape[0], 2))],
    )(features, by_y, other)


def solution(mesh):
    torus = Mesh(
        mesh.devices.reshape(4, 4, 4, 2, mesh.shape["head"]), (ZH, ZL, Y, C, X)
    )
    return jax.shard_map(
        per_device,
        mesh=torus,
        in_specs=(P(SEQ, X),) * 5,
        out_specs=P(SEQ, X),
        check_vma=False,
    )
```

time: 252 us -> 161 us (0.64)
  the two profiles are of different devices: /device:TPU:8 before, /device:TPU:1 now
where the time goes in v1:
time: 161 us; the launch traced here: 160 us
  blocking collectives  100 us (62%)
  starting transfers between devices  21.7 us (13%)
  waiting for transfers between devices  20.4 us (13%)
  local copies, waits for them, and re-layouts  8.95 us (6%)
  Pallas kernels  8.18 us (5%)
    all_to_all x4, blocking collectives, swap(): return lax.all_to_all(array, axes, 0, 0, tiled=True)  100 us
    all_to_all x2, waiting for transfers between devices, swap(): return lax.all_to_all(array, axes, 0, 0, tiled=True)  20.4 us
    all_to_all x2, starting transfers between devices, swap(): return lax.all_to_all(array, axes, 0, 0, tiled=True)  19.5 us
    unnamed x16, local copies, waits for them, and re-layouts  7.29 us
    pallas_call x1, Pallas kernels, per_device(): call(project_body, bf16((rows, cols)), 3, 2 * 10 ** 9, 8 * 2 ** 20, in_sp...  4.95 us
  transfers between devices with their start and end apart: 3, of which 2 were waited for; matrix products, arithmetic and copies ran while one was open for 0% of the time, Pallas kernels for 2%

profile of v1, /device:TPU:1, one launch (start us, length us, event | category | flops | bytes accessed | tf_op | source)
XLA Modules:
  0.0 159.8 jit_solution(4213377866736670464)
XLA Ops:
  0.0 0.0 copy-start.2
  0.0 1.0 copy-done.2
  1.0 0.0 copy-start.4
  1.0 1.0 copy-done.4
  2.1 0.0 copy-start.7
  2.1 0.3 shard_map.55
  2.4 21.1 %all_to_all.30.r_ref = f32[32,16,128]{2,1,0:T(8,128)S(1)} all-to-all(f32[32,16,128]{2,1,0:T(8,128)S(1)} %bitcast.2), channel_id=1, replica_groups=mesh['zh'=4,'zl'=4,'y'=4,'c'=2,'x'=4] {'zl','y','c'}, dimensions={0} | all-to-all | bytes 524288 | tf_op jit(solution)/shard_map/all_to_all | solution.py:144
  23.5 23.4 %all_to_all.31.t_ref = f32[4,16,128]{2,1,0:T(8,128)S(1)} all-to-all(f32[4,16,128]{2,1,0:T(8,128)S(1)} %get-tuple-element.8), channel_id=1, replica_groups=mesh['zh'=4,'zl'=4,'y'=4,'c'=2,'x'=4] {'zh'}, dimensions={0} | all-to-all | bytes 65536 | tf_op jit(solution)/shard_map/all_to_all | solution.py:144
  47.0 0.0 copy-done.7
  47.0 25.6 %all_to_all.32 = bf16[16,16,1024]{2,1,0:T(8,128)(2,1)S(1)} all-to-all(bf16[16,16,1024]{2,1,0:T(8,128)(2,1)S(1)} %broadcast_in_dim.4), channel_id=1, replica_groups=mesh['zh'=4,'zl'=4,'y'=4,'c'=2,'x'=4] {'zh','zl'}, dimensions={0} | all-to-all | bytes 1048576 | tf_op jit(solution)/shard_map/all_to_all | solution.py:144
  72.7 1.6 %broadcast_in_dim.5 = bf16[4,16,16,1024]{3,2,1,0:T(8,128)(2,1)} broadcast(bf16[16,16,1024]{2,1,0:T(8,128)(2,1)S(1)} %all_to_all.32), dimensions={1,2,3} | broadcast | bytes 2621440 | tf_op jit(solution)/shard_map/broadcast_in_dim | solution.py:140
  74.3 3.6 %all-to-all-start.5 = ((bf16[4,16,16,1024]{3,2,1,0:T(8,128)(2,1)}), bf16[4,16,16,1024]{3,2,1,0:T(8,128)(2,1)S(1)}, u32[]{:S(2)}, u32[]{:S(2)}) async-start(bf16[4,16,16,1024]{3,2,1,0:T(8,128)(2,1)} %broadcast_in_dim.5), calls=%async_computation.5 | async-start | bytes 4194304 | tf_op jit(solution)/shard_map/all_to_all | solution.py:144
  77.9 0.7 shard_map.57
  78.6 18.7 %all-to-all-done.5.mine_ref = bf16[4,16,16,1024]{3,2,1,0:T(8,128)(2,1)S(1)} async-done(((bf16[4,16,16,1024]{3,2,1,0:T(8,128)(2,1)}), bf16[4,16,16,1024]{3,2,1,0:T(8,128)(2,1)S(1)}, u32[]{:S(2)}, u32[]{:S(2)}) %all-to-all-start.5) | async-done | bytes 2097184 | tf_op jit(solution)/shard_map/all_to_all | solution.py:144
  97.2 15.9 %all-to-all-start.2 = ((bf16[32,16,128]{2,1,0:T(8,128)(2,1)}), bf16[32,16,128]{2,1,0:T(8,128)(2,1)S(1)}, u32[]{:S(2)}, u32[]{:S(2)}) async-start(bf16[32,16,128]{2,1,0:T(8,128)(2,1)} %shard_map.57), calls=%async_computation.2 | async-start | bytes 262144 | tf_op jit(solution)/shard_map/all_to_all | solution.py:144
  113.1 2.1 %collective-permute-start = (bf16[4,16,16,1024]{3,2,1,0:T(8,128)(2,1)S(1)}, bf16[4,16,16,1024]{3,2,1,0:T(8,128)(2,1)}, u32[]{:S(2)}, u32[]{:S(2)}) collective-permute-start(bf16[4,16,16,1024]{3,2,1,0:T(8,128)(2,1)S(1)} %all-to-all-done.5.mine_ref), channel_id=1, source_target_pairs={{0,4},{4,0},{1,5},{5,1},{2,6},{6,2},{3,7},{7,3},{8,12},{12,8},{9,1... | collective-permute-start | bytes 6291464 | tf_op jit(solution)/shard_map/ppermute | solution.py:176
  115.3 0.0 copy-start
  115.3 1.0 copy-done
  116.3 0.0 copy-start.3
  116.3 1.0 copy-done.3
  117.4 0.0 copy-start.5
  117.4 1.0 copy-done.5
  118.4 1.4 shard_map.58.l_ref
  119.9 1.8 %all-to-all-done.2 = bf16[32,16,128]{2,1,0:T(8,128)(2,1)S(1)} async-done(((bf16[32,16,128]{2,1,0:T(8,128)(2,1)}), bf16[32,16,128]{2,1,0:T(8,128)(2,1)S(1)}, u32[]{:S(2)}, u32[]{:S(2)}) %all-to-all-start.2) | async-done | bytes 131104 | tf_op jit(solution)/shard_map/all_to_all | solution.py:144
  121.7 0.0 copy-start.1
  121.7 1.0 copy-done.1
  122.7 0.0 copy-start.6
  122.7 1.0 copy-done.6
  123.8 0.7 shard_map.59
  124.5 30.3 %all_to_all.33.h_ref = bf16[4,528,512]{2,1,0:T(8,128)(2,1)S(1)} all-to-all(bf16[4,528,512]{2,1,0:T(8,128)(2,1)S(1)} %shard_map.59), channel_id=1, replica_groups=mesh['zh'=4,'zl'=4,'y'=4,'c'=2,'x'=4] {'x'}, dimensions={0} | all-to-all | bytes 4325376 | tf_op jit(solution)/shard_map/all_to_all | solution.py:144
  154.8 0.0 collective-permute-done.other_ref
  154.8 4.9 %shard_map.60 = bf16[512,1024]{1,0:T(8,128)(2,1)} custom-call(bf16[4,528,512]{2,1,0:T(8,128)(2,1)S(1)} %all_to_all.33.h_ref, bf16[4,16,16,1024]{3,2,1,0:T(8,128)(2,1)S(1)} %all-to-all-done.5.mine_ref, bf16[4,16,16,1024]{3,2,1,0:T(8,128)(2,1)} %collective-permute-done.other_ref), custom_call_target="tpu_custom_call" | custom-call | flops 2000000000 | bytes 8388608 | tf_op jit(solution)/shard_map/pallas_call | solution.py:178
  (2 shorter events, 0.1 us)
Async XLA Ops:
  0.0 1.0 copy-start.2
  1.0 1.0 copy-start.4
  2.1 44.9 %copy-start.7 = (bf16[16,1024]{1,0:T(8,128)(2,1)S(1)}, bf16[16,1024]{1,0:T(8,128)(2,1)}, u32[]{:S(2)}) copy-start(bf16[16,1024]{1,0:T(8,128)(2,1)} %param.9) | copy-start | bytes 98308
  74.3 23.0 %all-to-all-start.5 = ((bf16[4,16,16,1024]{3,2,1,0:T(8,128)(2,1)}), bf16[4,16,16,1024]{3,2,1,0:T(8,128)(2,1)S(1)}, u32[]{:S(2)}, u32[]{:S(2)}) async-start(bf16[4,16,16,1024]{3,2,1,0:T(8,128)(2,1)} %broadcast_in_dim.5), calls=%async_computation.5 | async-start | bytes 4194304 | tf_op jit(solution)/shard_map/all_to_all | solution.py:144
  97.2 24.4 %all-to-all-start.2 = ((bf16[32,16,128]{2,1,0:T(8,128)(2,1)}), bf16[32,16,128]{2,1,0:T(8,128)(2,1)S(1)}, u32[]{:S(2)}, u32[]{:S(2)}) async-start(bf16[32,16,128]{2,1,0:T(8,128)(2,1)} %shard_map.57), calls=%async_computation.2 | async-start | bytes 262144 | tf_op jit(solution)/shard_map/all_to_all | solution.py:144
  113.1 41.7 %collective-permute-start = (bf16[4,16,16,1024]{3,2,1,0:T(8,128)(2,1)S(1)}, bf16[4,16,16,1024]{3,2,1,0:T(8,128)(2,1)}, u32[]{:S(2)}, u32[]{:S(2)}) collective-permute-start(bf16[4,16,16,1024]{3,2,1,0:T(8,128)(2,1)S(1)} %all-to-all-done.5.mine_ref), channel_id=1, source_target_pairs={{0,4},{4,0},{1,5},{5,1},{2,6},{6,2},{3,7},{7,3},{8,12},{12,8},{9,1... | collective-permute-start | bytes 6291464 | tf_op jit(solution)/shard_map/ppermute | solution.py:176
  115.3 1.0 copy-start
  116.3 1.0 copy-start.3
  117.4 1.0 copy-start.5
  121.7 1.0 copy-start.1
  122.7 1.0 copy-start.6

commit v2 on v1

--- a/solution.py
+++ b/solution.py
@@ -8,17 +8,22 @@
 from jax.sharding import Mesh
 from jax.sharding import PartitionSpec as P
 
+
 HD = 128
 ZH, ZL, Y, C, X = "zh", "zl", "y", "c", "x"
 SEQ = (ZH, ZL, Y, C)
 NEAR = (ZL, Y, C)
+STEPS = (1, -1, 2)
+NEXT = (0, 3, 1, 2)
+
+
 F32 = jnp.float32
 BF16 = jnp.bfloat16
 VMEM = pl.BlockSpec(memory_space=pltpu.VMEM)
 ANY = pl.BlockSpec(memory_space=pl.ANY)
 
 
-def call(body, outs, n_in, flops, nbytes, in_specs=None, scratch=()):
+def call(body, outs, n_in, flops, nbytes, in_specs=None, scratch=(), grant=16):
     return pl.pallas_call(
         body,
         out_shape=outs,
@@ -28,7 +33,7 @@
         cost_estimate=pl.CostEstimate(
             flops=flops, bytes_accessed=nbytes, transcendentals=0
         ),
-        compiler_params=pltpu.CompilerParams(vmem_limit_bytes=40 * 2**20),
+        compiler_params=pltpu.CompilerParams(vmem_limit_bytes=grant * 2**20),
     )
 
 
@@ -60,20 +65,29 @@
             o_ref[r, cols] = jnp.dot(s, v_ref[seen, cols], preferred_element_type=F32)
 
 
-def near_prefix_body(r_ref, e_ref, t_ref):
+def near_prefix_body(r_ref, w_ref, e_ref, t_ref):
     acc = jnp.zeros(r_ref.shape[1:], F32)
     for j in range(r_ref.shape[0]):
         e_ref[j] = acc
         acc = acc + r_ref[j]
+    hi = acc.astype(BF16)
+    lo = (acc - hi.astype(F32)).astype(BF16)
+    cols = w_ref.shape[1]
     for j in range(t_ref.shape[0]):
-        t_ref[j] = acc
-
-
-def far_prefix_body(e_ref, t_ref, p_ref):
+        t_ref[j, :, :cols] = w_ref[...]
+        t_ref[j, :, cols : cols + HD] = hi
+        t_ref[j, :, cols + HD :] = lo
+
+
+def far_prefix_body(e_ref, t_ref, p_ref, w_ref):
     me = lax.axis_index(ZH)
-    base = jnp.zeros(t_ref.shape[1:], F32)
+    cols = w_ref.shape[2]
+    base = jnp.zeros(e_ref.shape[1:], F32)
     for j in range(t_ref.shape[0]):
-        base = base + jnp.where(j < me, t_ref[j], 0.0)
+        hi = t_ref[j, :, cols : cols + HD].astype(F32)
+        lo = t_ref[j, :, cols + HD :].astype(F32)
+        base = base + jnp.where(j < me, hi + lo, 0.0)
+        w_ref[j] = t_ref[j, :, :cols]
     for j in range(e_ref.shape[0]):
         p_ref[j] = (e_ref[j] + base).astype(BF16)
 
@@ -101,18 +115,26 @@
         o_ref[j, rows:, :] = extra.astype(BF16)
 
 
-def project_body(h_ref, mine_ref, other_ref, o_ref, w_ref, sem):
-    me = lax.axis_index(C)
+def project_body(h_ref, *refs):
+    blocks = refs[:8]
+    o_ref, w_ref, sem = refs[8:]
+    core = lax.axis_index(C)
+    zl = lax.axis_index(ZL)
+    y = lax.axis_index(Y)
     copies = []
-    for y in range(mine_ref.shape[0]):
-        for n, (src, core) in enumerate(((mine_ref, me), (other_ref, 1 - me))):
-            copies.append(pltpu.make_async_copy(src.at[y], w_ref.at[:, y, core], sem.at[y, n]))
+    for n, block in enumerate(blocks):
+        owner = core if n < 4 else 1 - core
+        for k in range(4):
+            outer, inner = NEXT[n % 4], NEXT[k]
+            by_z = jnp.where(owner == 0, inner, outer)
+            by_y = jnp.where(owner == 0, outer, inner)
+            to = w_ref.at[:, lax.rem(zl + by_z, 4), lax.rem(y + by_y, 4), owner]
+            copies.append(pltpu.make_async_copy(block.at[k], to, sem.at[n, k]))
     for copy in copies:
         copy.start()
     rows, width = o_ref.shape
     parts = h_ref.shape[0]
     each = h_ref.shape[2]
-    heads = each // HD
     row = jnp.zeros((1, rows), F32)
     for s in range(parts):
         for j in range(3):
@@ -128,20 +150,30 @@
             c = slice(n * 256, (n + 1) * 256)
             acc = jnp.zeros((blk, 256), F32)
             for s in range(parts):
-                w = w_ref[s * heads : (s + 1) * heads, :, :, :, c].reshape(each, 256)
+                w = w_ref[s, :, :, :, :, c].reshape(each, 256)
                 acc = acc + jnp.dot(h_ref[s, r, :], w, preferred_element_type=F32)
             o_ref[r, c] = (acc * inv[r, :1]).astype(BF16)
 
 
-def spread(block, axes):
-    n = 1
-    for a in axes:
-        n *= lax.axis_size(a)
-    return jnp.broadcast_to(block[None], (n, *block.shape))
-
-
 def swap(array, axes):
     return lax.all_to_all(array, axes, 0, 0, tiled=True)
+
+
+def moved(array, first, second, step):
+    pairs = []
+    n = {a: lax.axis_size(a) for a in SEQ}
+    ring = n[ZH] * n[ZL]
+    for z in range(ring):
+        for y in range(n[Y]):
+            for c in range(n[C]):
+                to_z, to_y = z, y
+                if (first, second)[c] == "z":
+                    hop = step if step != 2 or z % 2 == 0 else -2
+                    to_z = (z + hop) % ring
+                else:
+                    to_y = (y + step) % n[Y]
+                pairs.append(((z * n[Y] + y) * n[C] + c, (to_z * n[Y] + to_y) * n[C] + c))
+    return lax.ppermute(array, SEQ, pairs)
 
 
 def per_device(queries, key_vectors, value_vectors, gate_input, out_weight):
@@ -155,31 +187,46 @@
     f32 = functools.partial(jax.ShapeDtypeStruct, dtype=F32)
     bf16 = functools.partial(jax.ShapeDtypeStruct, dtype=BF16)
 
-    by_z = swap(spread(out_weight, (ZH, ZL)), (ZH, ZL))
-    by_z = by_z.reshape(-1, *out_weight.shape)
-    state = call(state_body, f32((heads, HD, HD)), 2, 10**8, 2**20)(key_vectors, value_vectors)
+    state = call(state_body, f32((heads, HD, HD)), 2, 10**8, 2**20)(
+        key_vectors, value_vectors
+    )
     local = call(local_body, f32((rows, width)), 3, 5 * 10**8, 2**21)(
         queries, key_vectors, value_vectors
     )
     pieces = swap(state.reshape(near, *piece), NEAR)
     earlier, total = call(
-        near_prefix_body, (f32((near, *piece)), f32((far, *piece))), 1, 10**6, 2**19
-    )(pieces)
+        near_prefix_body,
+        (f32((near, *piece)), bf16((far, piece[0], cols + 2 * HD))),
+        2, 10**6, 2**19,
+    )(pieces, out_weight)
     totals = swap(total, (ZH,))
-    prefix = call(far_prefix_body, bf16((near, *piece)), 2, 10**6, 2**19)(earlier, totals)
+    prefix, w_far = call(
+        far_prefix_body,
+        (bf16((near, *piece)), bf16((far, *out_weight.shape))),
+        2, 10**6, 2**19,
+    )(earlier, totals)
     prefix = swap(prefix, NEAR).reshape(heads, HD, HD)
     hidden = call(
         hidden_body, bf16((group, rows + 16, width)), 4, 10**8, 2**22
     )(queries, prefix, local, gate_input)
     features = swap(hidden, (X,))
-    by_y = swap(spread(by_z, (Y,)), (Y,)).reshape(-1, *by_z.shape)
-    other = lax.ppermute(by_y, C, ((0, 1), (1, 0)))
-    full = (by_z.shape[0], by_y.shape[0], 2, *out_weight.shape)
+    first = [w_far]
+    for step in STEPS:
+        first.append(moved(w_far, "z", "y", step))
+    first = jnp.stack(first)
+    mine = [first]
+    for step in STEPS:
+        mine.append(moved(first, "y", "z", step))
+    other = []
+    for block in mine:
+        other.append(lax.ppermute(block, C, ((0, 1), (1, 0))))
+    full = (far, lax.axis_size(ZL), lax.axis_size(Y), 2, *out_weight.shape)
     return call(
         project_body, bf16((rows, cols)), 3, 2 * 10**9, 8 * 2**20,
-        in_specs=[VMEM, ANY, ANY],
-        scratch=[pltpu.VMEM(full, BF16), pltpu.SemaphoreType.DMA((by_y.shape[0], 2))],
-    )(features, by_y, other)
+        in_specs=[VMEM] + [ANY] * 8,
+        grant=60,
+        scratch=[pltpu.VMEM(full, BF16), pltpu.SemaphoreType.DMA((8, 4))],
+    )(features, *mine, *other)
 
 
 def solution(mesh):

time: 161 us -> 122 us (0.76)
  the two profiles are of different devices: /device:TPU:1 before, /device:TPU:27 now
where the time goes in v2:
time: 122 us
  starting transfers between devices  49.4 us (40%)
  blocking collectives  43.8 us (36%)
  Pallas kernels  12.1 us (10%)
  waiting for transfers between devices  10 us (8%)
  local copies, waits for them, and re-layouts  6.08 us (5%)
    all_to_all x2, blocking collectives, swap(): return lax.all_to_all(array, axes, 0, 0, tiled=True)  43.8 us
    ppermute x6, starting transfers between devices, moved(): return lax.ppermute(array, SEQ, pairs)  18.5 us
    ppermute x4, starting transfers between devices, per_device(): other.append(lax.ppermute(block, C, ((0, 1), (1, 0))))  16.8 us
    all_to_all x2, starting transfers between devices, swap(): return lax.all_to_all(array, axes, 0, 0, tiled=True)  14.1 us
    pallas_call x1, Pallas kernels, per_device(): call(project_body, bf16((rows, cols)), 3, 2 * 10 ** 9, 8 * 2 ** 20, in_sp...  7.48 us
    unnamed x30, local copies, waits for them, and re-layouts  6.08 us
    all_to_all x2, waiting for transfers between devices, swap(): return lax.all_to_all(array, axes, 0, 0, tiled=True)  5.44 us
    ppermute x6, waiting for transfers between devices, moved(): return lax.ppermute(array, SEQ, pairs)  4.44 us
  transfers between devices with their start and end apart: 12, of which 5 were waited for; matrix products, arithmetic and copies ran while one was open for 0% of the time, Pallas kernels for 1%

profile of v2, /device:TPU:27, one launch (start us, length us, event | category | flops | bytes accessed | tf_op | source)
XLA Modules:
  0.0 121.7 jit_solution(7252571693741425650)
XLA Ops:
  0.0 1.1 copy-done.1
  1.1 1.0 copy-done.3
  2.1 0.3 shard_map.55
  2.5 18.7 %all_to_all.20.r_ref = f32[32,16,128]{2,1,0:T(8,128)S(1)} all-to-all(f32[32,16,128]{2,1,0:T(8,128)S(1)} %bitcast.6), channel_id=1, replica_groups=mesh['zh'=4,'zl'=4,'y'=4,'c'=2,'x'=4] {'zl','y','c'}, dimensions={0} | all-to-all | bytes 524288 | tf_op jit(solution)/shard_map/all_to_all | solution.py:159
  21.2 0.8 copy-done.6
  22.0 25.1 %all_to_all.21.t_ref = bf16[4,16,1280]{2,1,0:T(8,128)(2,1)S(1)} all-to-all(bf16[4,16,1280]{2,1,0:T(8,128)(2,1)S(1)} %get-tuple-element.10), channel_id=1, replica_groups=mesh['zh'=4,'zl'=4,'y'=4,'c'=2,'x'=4] {'zh'}, dimensions={0} | all-to-all | bytes 327680 | tf_op jit(solution)/shard_map/all_to_all | solution.py:159
  47.1 0.7 shard_map.57
  47.8 9.8 %all-to-all-start.2 = ((bf16[32,16,128]{2,1,0:T(8,128)(2,1)}), bf16[32,16,128]{2,1,0:T(8,128)(2,1)S(1)}, u32[]{:S(2)}, u32[]{:S(2)}) async-start(bf16[32,16,128]{2,1,0:T(8,128)(2,1)} %get-tuple-element.11), calls=%async_computation.2 | async-start | bytes 262144 | tf_op jit(solution)/shard_map/all_to_all | solution.py:159
  57.6 1.4 %shard_map.58.l_ref = f32[512,512]{1,0:T(8,128)S(1)} custom-call(bf16[512,512]{1,0:T(8,128)(2,1)S(1)} %copy-done, bf16[512,512]{1,0:T(8,128)(2,1)S(1)} %copy-done.2, bf16[512,512]{1,0:T(8,128)(2,1)S(1)} %copy-done.4), custom_call_target="tpu_custom_call" | custom-call | flops 500000000 | bytes 2097152 | tf_op jit(solution)/shard_map/pallas_call | solution.py:193
  59.1 5.4 %all-to-all-done.2 = bf16[32,16,128]{2,1,0:T(8,128)(2,1)S(1)} async-done(((bf16[32,16,128]{2,1,0:T(8,128)(2,1)}), bf16[32,16,128]{2,1,0:T(8,128)(2,1)S(1)}, u32[]{:S(2)}, u32[]{:S(2)}) %all-to-all-start.2) | async-done | bytes 131104 | tf_op jit(solution)/shard_map/all_to_all | solution.py:159
  64.5 2.1 %shard_map.59 = bf16[4,528,512]{2,1,0:T(8,128)(2,1)} custom-call(bf16[512,512]{1,0:T(8,128)(2,1)S(1)} %copy-done, bf16[4,128,128]{2,1,0:T(8,128)(2,1)S(1)} %bitcast.7, f32[512,512]{1,0:T(8,128)S(1)} %shard_map.58.l_ref, bf16[512,512]{1,0:T(8,128)(2,1)S(1)} %copy-done.5), custom_call_target="tpu_custom_call" | custom-call | flops 100000000 | bytes 4194304 | tf_op jit(solution)/shard_map/pallas_call | solution.py:209
  66.6 4.3 %all-to-all-start.3 = ((bf16[4,528,512]{2,1,0:T(8,128)(2,1)}), bf16[4,528,512]{2,1,0:T(8,128)(2,1)S(1)}, u32[]{:S(2)}, u32[]{:S(2)}) async-start(bf16[4,528,512]{2,1,0:T(8,128)(2,1)} %shard_map.59), calls=%async_computation.3 | async-start | bytes 4325376 | tf_op jit(solution)/shard_map/all_to_all | solution.py:159
  70.9 3.6 %collective-permute-start.2 = (bf16[4,16,1024]{2,1,0:T(8,128)(2,1)S(1)}, bf16[4,16,1024]{2,1,0:T(8,128)(2,1)S(1)}, u32[]{:S(2)}, u32[]{:S(2)}) collective-permute-start(bf16[4,16,1024]{2,1,0:T(8,128)(2,1)S(1)} %get-tuple-element.12), channel_id=1, source_target_pairs={{0,64},{4,20},{8,72},{12,28},{16,80},{20,4},{24,88},{28,12},{32,48... | collective-permute-start | bytes 393224 | tf_op jit(solution)/shard_map/ppermute | solution.py:176
  74.5 2.5 %collective-permute-start.1 = (bf16[4,16,1024]{2,1,0:T(8,128)(2,1)S(1)}, bf16[4,16,1024]{2,1,0:T(8,128)(2,1)S(1)}, u32[]{:S(2)}, u32[]{:S(2)}) collective-permute-start(bf16[4,16,1024]{2,1,0:T(8,128)(2,1)S(1)} %get-tuple-element.12), channel_id=1, source_target_pairs={{0,480},{4,28},{8,488},{12,4},{16,496},{20,12},{24,504},{28,20},{3... | collective-permute-start | bytes 393224 | tf_op jit(solution)/shard_map/ppermute | solution.py:176
  77.0 4.0 %collective-permute-start = (bf16[4,16,1024]{2,1,0:T(8,128)(2,1)S(1)}, bf16[4,16,1024]{2,1,0:T(8,128)(2,1)S(1)}, u32[]{:S(2)}, u32[]{:S(2)}) collective-permute-start(bf16[4,16,1024]{2,1,0:T(8,128)(2,1)S(1)} %get-tuple-element.12), channel_id=1, source_target_pairs={{0,32},{4,12},{8,40},{12,20},{16,48},{20,28},{24,56},{28,4},{32,64... | collective-permute-start | bytes 393224 | tf_op jit(solution)/shard_map/ppermute | solution.py:176
  81.0 0.4 collective-permute-done.1
  81.4 1.6 %collective-permute-done = bf16[4,16,1024]{2,1,0:T(8,128)(2,1)S(1)} collective-permute-done((bf16[4,16,1024]{2,1,0:T(8,128)(2,1)S(1)}, bf16[4,16,1024]{2,1,0:T(8,128)(2,1)S(1)}, u32[]{:S(2)}, u32[]{:S(2)}) %collective-permute-start) | collective-permute-done | bytes 131104 | tf_op jit(solution)/shard_map/ppermute | solution.py:176
  83.0 0.1 pad_maximum_fusion.refs_0_
  83.1 2.3 %collective-permute-start.3 = (bf16[4,4,16,1024]{3,2,1,0:T(8,128)(2,1)S(1)}, bf16[4,4,16,1024]{3,2,1,0:T(8,128)(2,1)S(1)}, u32[]{:S(2)}, u32[]{:S(2)}) collective-permute-start(bf16[4,4,16,1024]{3,2,1,0:T(8,128)(2,1)S(1)} %pad_maximum_fusion.refs_0_), channel_id=1, source_target_pairs={{0,8},{4,36},{8,16},{12,44},{16,24},{20,52},{24,0},{28,60},{32,40}... | collective-permute-start | bytes 1572872 | tf_op jit(solution)/shard_map/ppermute | solution.py:176
  85.4 4.2 %collective-permute-start.4 = (bf16[4,4,16,1024]{3,2,1,0:T(8,128)(2,1)S(1)}, bf16[4,4,16,1024]{3,2,1,0:T(8,128)(2,1)S(1)}, u32[]{:S(2)}, u32[]{:S(2)}) collective-permute-start(bf16[4,4,16,1024]{3,2,1,0:T(8,128)(2,1)S(1)} %pad_maximum_fusion.refs_0_), channel_id=1, source_target_pairs={{0,24},{4,484},{8,0},{12,492},{16,8},{20,500},{24,16},{28,508},{32... | collective-permute-start | bytes 1572872 | tf_op jit(solution)/shard_map/ppermute | solution.py:176
  89.6 1.9 %collective-permute-start.5 = (bf16[4,4,16,1024]{3,2,1,0:T(8,128)(2,1)S(1)}, bf16[4,4,16,1024]{3,2,1,0:T(8,128)(2,1)S(1)}, u32[]{:S(2)}, u32[]{:S(2)}) collective-permute-start(bf16[4,4,16,1024]{3,2,1,0:T(8,128)(2,1)S(1)} %pad_maximum_fusion.refs_0_), channel_id=1, source_target_pairs={{0,16},{4,68},{8,24},{12,76},{16,0},{20,84},{24,8},{28,92},{32,48}... | collective-permute-start | bytes 1572872 | tf_op jit(solution)/shard_map/ppermute | solution.py:176
  91.5 5.4 %collective-permute-start.6 = (bf16[4,4,16,1024]{3,2,1,0:T(8,128)(2,1)S(1)}, bf16[4,4,16,1024]{3,2,1,0:T(8,128)(2,1)S(1)}, u32[]{:S(2)}, u32[]{:S(2)}) collective-permute-start(bf16[4,4,16,1024]{3,2,1,0:T(8,128)(2,1)S(1)} %pad_maximum_fusion.refs_0_), channel_id=1, source_target_pairs={{0,4},{4,0},{1,5},{5,1},{2,6},{6,2},{3,7},{7,3},{8,12},{12,8},{9,1... | collective-permute-start | bytes 1572872 | tf_op jit(solution)/shard_map/ppermute | solution.py:222
  96.9 1.9 %collective-permute-start.7 = (bf16[4,4,16,1024]{3,2,1,0:T(8,128)(2,1)S(1)}, bf16[4,4,16,1024]{3,2,1,0:T(8,128)(2,1)S(1)}, u32[]{:S(2)}, u32[]{:S(2)}) collective-permute-start(bf16[4,4,16,1024]{3,2,1,0:T(8,128)(2,1)S(1)} %collective-permute-done.3.refs_1_), channel_id=1, source_target_pairs={{0,4},{4,0},{1,5},{5,1},{2,6},{6,2},{3,7},{7,3},{8,12},{12,8},{9,1... | collective-permute-start | bytes 1572872 | tf_op jit(solution)/shard_map/ppermute | solution.py:222
  98.8 2.5 %collective-permute-done.4.refs_2_ = bf16[4,4,16,1024]{3,2,1,0:T(8,128)(2,1)S(1)} collective-permute-done((bf16[4,4,16,1024]{3,2,1,0:T(8,128)(2,1)S(1)}, bf16[4,4,16,1024]{3,2,1,0:T(8,128)(2,1)S(1)}, u32[]{:S(2)}, u32[]{:S(2)}) %collective-permute-start.4) | collective-permute-done | bytes 524320 | tf_op jit(solution)/shard_map/ppermute | solution.py:176
  101.3 7.6 %collective-permute-start.8 = (bf16[4,4,16,1024]{3,2,1,0:T(8,128)(2,1)S(1)}, bf16[4,4,16,1024]{3,2,1,0:T(8,128)(2,1)S(1)}, u32[]{:S(2)}, u32[]{:S(2)}) collective-permute-start(bf16[4,4,16,1024]{3,2,1,0:T(8,128)(2,1)S(1)} %collective-permute-done.4.refs_2_), channel_id=1, source_target_pairs={{0,4},{4,0},{1,5},{5,1},{2,6},{6,2},{3,7},{7,3},{8,12},{12,8},{9,1... | collective-permute-start | bytes 1572872 | tf_op jit(solution)/shard_map/ppermute | solution.py:222
  108.9 1.9 %collective-permute-start.9 = (bf16[4,4,16,1024]{3,2,1,0:T(8,128)(2,1)S(1)}, bf16[4,4,16,1024]{3,2,1,0:T(8,128)(2,1)}, u32[]{:S(2)}, u32[]{:S(2)}) collective-permute-start(bf16[4,4,16,1024]{3,2,1,0:T(8,128)(2,1)S(1)} %collective-permute-done.5.refs_3_), channel_id=1, source_target_pairs={{0,4},{4,0},{1,5},{5,1},{2,6},{6,2},{3,7},{7,3},{8,12},{12,8},{9,1... | collective-permute-start | bytes 1572872 | tf_op jit(solution)/shard_map/ppermute | solution.py:222
  110.9 0.8 copy-done.12
  111.7 0.2 copy-done.13
  111.9 0.8 copy-done.14
  112.7 0.2 collective-permute-done.9.refs_7_
  112.9 1.4 %copy-done.7 = bf16[4,528,512]{2,1,0:T(8,128)(2,1)} copy-done((bf16[4,528,512]{2,1,0:T(8,128)(2,1)}, bf16[4,528,512]{2,1,0:T(8,128)(2,1)S(1)}, u32[]{:S(2)}) %copy-start.7) | copy-done | bytes 2162712
  114.2 7.5 %shard_map.60 = bf16[512,1024]{1,0:T(8,128)(2,1)} custom-call(bf16[4,528,512]{2,1,0:T(8,128)(2,1)} %copy-done.7, bf16[4,4,16,1024]{3,2,1,0:T(8,128)(2,1)} %copy-done.8, bf16[4,4,16,1024]{3,2,1,0:T(8,128)(2,1)} %copy-done.9, bf16[4,4,16,1024]{3,2,1,0:T(8,128)(2,1)} %copy-done.10, bf16[4,4,16,1024]{3,2,1,0:T(8,128)(2,1)} %copy-done.11, ...), custom_call_target="tpu_custom_call" | custom-call | flops 2000000000 | bytes 8388608 | tf_op jit(solution)/shard_map/pallas_call | solution.py:224
  (31 shorter events, 0.1 us)
Async XLA Ops:
  0.0 57.6 %copy-start = (bf16[512,512]{1,0:T(8,128)(2,1)S(1)}, bf16[512,512]{1,0:T(8,128)(2,1)}, u32[]{:S(2)}) copy-start(bf16[512,512]{1,0:T(8,128)(2,1)} %q_ref.3) | copy-start | bytes 1572868
  0.0 1.1 copy-start.1
  1.1 1.0 copy-start.3
  2.1 55.5 %copy-start.2 = (bf16[512,512]{1,0:T(8,128)(2,1)S(1)}, bf16[512,512]{1,0:T(8,128)(2,1)}, u32[]{:S(2)}) copy-start(bf16[512,512]{1,0:T(8,128)(2,1)} %k_ref.3) | copy-start | bytes 1572868
  2.1 55.5 %copy-start.4 = (bf16[512,512]{1,0:T(8,128)(2,1)S(1)}, bf16[512,512]{1,0:T(8,128)(2,1)}, u32[]{:S(2)}) copy-start(bf16[512,512]{1,0:T(8,128)(2,1)} %v_ref.3) | copy-start | bytes 1572868
  2.5 62.0 %copy-start.5 = (bf16[512,512]{1,0:T(8,128)(2,1)S(1)}, bf16[512,512]{1,0:T(8,128)(2,1)}, u32[]{:S(2)}) copy-start(bf16[512,512]{1,0:T(8,128)(2,1)} %g_ref.1) | copy-start | bytes 1572868
  21.2 0.8 copy-start.6
  47.8 16.7 %all-to-all-start.2 = ((bf16[32,16,128]{2,1,0:T(8,128)(2,1)}), bf16[32,16,128]{2,1,0:T(8,128)(2,1)S(1)}, u32[]{:S(2)}, u32[]{:S(2)}) async-start(bf16[32,16,128]{2,1,0:T(8,128)(2,1)} %get-tuple-element.11), calls=%async_computation.2 | async-start | bytes 262144 | tf_op jit(solution)/shard_map/all_to_all | solution.py:159
  66.6 46.3 %all-to-all-start.3 = ((bf16[4,528,512]{2,1,0:T(8,128)(2,1)}), bf16[4,528,512]{2,1,0:T(8,128)(2,1)S(1)}, u32[]{:S(2)}, u32[]{:S(2)}) async-start(bf16[4,528,512]{2,1,0:T(8,128)(2,1)} %shard_map.59), calls=%async_computation.3 | async-start | bytes 4325376 | tf_op jit(solution)/shard_map/all_to_all | solution.py:159
  70.9 10.1 %collective-permute-start.2 = (bf16[4,16,1024]{2,1,0:T(8,128)(2,1)S(1)}, bf16[4,16,1024]{2,1,0:T(8,128)(2,1)S(1)}, u32[]{:S(2)}, u32[]{:S(2)}) collective-permute-start(bf16[4,16,1024]{2,1,0:T(8,128)(2,1)S(1)} %get-tuple-element.12), channel_id=1, source_target_pairs={{0,64},{4,20},{8,72},{12,28},{16,80},{20,4},{24,88},{28,12},{32,48... | collective-permute-start | bytes 393224 | tf_op jit(solution)/shard_map/ppermute | solution.py:176
  74.5 6.9 %collective-permute-start.1 = (bf16[4,16,1024]{2,1,0:T(8,128)(2,1)S(1)}, bf16[4,16,1024]{2,1,0:T(8,128)(2,1)S(1)}, u32[]{:S(2)}, u32[]{:S(2)}) collective-permute-start(bf16[4,16,1024]{2,1,0:T(8,128)(2,1)S(1)} %get-tuple-element.12), channel_id=1, source_target_pairs={{0,480},{4,28},{8,488},{12,4},{16,496},{20,12},{24,504},{28,20},{3... | collective-permute-start | bytes 393224 | tf_op jit(solution)/shard_map/ppermute | solution.py:176
  77.0 6.0 %collective-permute-start = (bf16[4,16,1024]{2,1,0:T(8,128)(2,1)S(1)}, bf16[4,16,1024]{2,1,0:T(8,128)(2,1)S(1)}, u32[]{:S(2)}, u32[]{:S(2)}) collective-permute-start(bf16[4,16,1024]{2,1,0:T(8,128)(2,1)S(1)} %get-tuple-element.12), channel_id=1, source_target_pairs={{0,32},{4,12},{8,40},{12,20},{16,48},{20,28},{24,56},{28,4},{32,64... | collective-permute-start | bytes 393224 | tf_op jit(solution)/shard_map/ppermute | solution.py:176
  83.1 29.8 %copy-start.8 = (bf16[4,4,16,1024]{3,2,1,0:T(8,128)(2,1)}, bf16[4,4,16,1024]{3,2,1,0:T(8,128)(2,1)S(1)}, u32[]{:S(2)}) copy-start(bf16[4,4,16,1024]{3,2,1,0:T(8,128)(2,1)S(1)} %pad_maximum_fusion.refs_0_) | copy-start | bytes 1572868
  83.1 13.8 %collective-permute-start.3 = (bf16[4,4,16,1024]{3,2,1,0:T(8,128)(2,1)S(1)}, bf16[4,4,16,1024]{3,2,1,0:T(8,128)(2,1)S(1)}, u32[]{:S(2)}, u32[]{:S(2)}) collective-permute-start(bf16[4,4,16,1024]{3,2,1,0:T(8,128)(2,1)S(1)} %pad_maximum_fusion.refs_0_), channel_id=1, source_target_pairs={{0,8},{4,36},{8,16},{12,44},{16,24},{20,52},{24,0},{28,60},{32,40}... | collective-permute-start | bytes 1572872 | tf_op jit(solution)/shard_map/ppermute | solution.py:176
  85.4 15.9 %collective-permute-start.4 = (bf16[4,4,16,1024]{3,2,1,0:T(8,128)(2,1)S(1)}, bf16[4,4,16,1024]{3,2,1,0:T(8,128)(2,1)S(1)}, u32[]{:S(2)}, u32[]{:S(2)}) collective-permute-start(bf16[4,4,16,1024]{3,2,1,0:T(8,128)(2,1)S(1)} %pad_maximum_fusion.refs_0_), channel_id=1, source_target_pairs={{0,24},{4,484},{8,0},{12,492},{16,8},{20,500},{24,16},{28,508},{32... | collective-permute-start | bytes 1572872 | tf_op jit(solution)/shard_map/ppermute | solution.py:176
  89.6 19.3 %collective-permute-start.5 = (bf16[4,4,16,1024]{3,2,1,0:T(8,128)(2,1)S(1)}, bf16[4,4,16,1024]{3,2,1,0:T(8,128)(2,1)S(1)}, u32[]{:S(2)}, u32[]{:S(2)}) collective-permute-start(bf16[4,4,16,1024]{3,2,1,0:T(8,128)(2,1)S(1)} %pad_maximum_fusion.refs_0_), channel_id=1, source_target_pairs={{0,16},{4,68},{8,24},{12,76},{16,0},{20,84},{24,8},{28,92},{32,48}... | collective-permute-start | bytes 1572872 | tf_op jit(solution)/shard_map/ppermute | solution.py:176
  91.5 19.3 %collective-permute-start.6 = (bf16[4,4,16,1024]{3,2,1,0:T(8,128)(2,1)S(1)}, bf16[4,4,16,1024]{3,2,1,0:T(8,128)(2,1)S(1)}, u32[]{:S(2)}, u32[]{:S(2)}) collective-permute-start(bf16[4,4,16,1024]{3,2,1,0:T(8,128)(2,1)S(1)} %pad_maximum_fusion.refs_0_), channel_id=1, source_target_pairs={{0,4},{4,0},{1,5},{5,1},{2,6},{6,2},{3,7},{7,3},{8,12},{12,8},{9,1... | collective-permute-start | bytes 1572872 | tf_op jit(solution)/shard_map/ppermute | solution.py:222
  96.9 16.0 %copy-start.9 = (bf16[4,4,16,1024]{3,2,1,0:T(8,128)(2,1)}, bf16[4,4,16,1024]{3,2,1,0:T(8,128)(2,1)S(1)}, u32[]{:S(2)}) copy-start(bf16[4,4,16,1024]{3,2,1,0:T(8,128)(2,1)S(1)} %collective-permute-done.3.refs_1_) | copy-start | bytes 1572868
  96.9 14.0 %collective-permute-start.7 = (bf16[4,4,16,1024]{3,2,1,0:T(8,128)(2,1)S(1)}, bf16[4,4,16,1024]{3,2,1,0:T(8,128)(2,1)S(1)}, u32[]{:S(2)}, u32[]{:S(2)}) collective-permute-start(bf16[4,4,16,1024]{3,2,1,0:T(8,128)(2,1)S(1)} %collective-permute-done.3.refs_1_), channel_id=1, source_target_pairs={{0,4},{4,0},{1,5},{5,1},{2,6},{6,2},{3,7},{7,3},{8,12},{12,8},{9,1... | collective-permute-start | bytes 1572872 | tf_op jit(solution)/shard_map/ppermute | solution.py:222
  101.3 9.6 %copy-start.10 = (bf16[4,4,16,1024]{3,2,1,0:T(8,128)(2,1)}, bf16[4,4,16,1024]{3,2,1,0:T(8,128)(2,1)S(1)}, u32[]{:S(2)}) copy-start(bf16[4,4,16,1024]{3,2,1,0:T(8,128)(2,1)S(1)} %collective-permute-done.4.refs_2_) | copy-start | bytes 1572868
  101.3 9.6 %collective-permute-start.8 = (bf16[4,4,16,1024]{3,2,1,0:T(8,128)(2,1)S(1)}, bf16[4,4,16,1024]{3,2,1,0:T(8,128)(2,1)S(1)}, u32[]{:S(2)}, u32[]{:S(2)}) collective-permute-start(bf16[4,4,16,1024]{3,2,1,0:T(8,128)(2,1)S(1)} %collective-permute-done.4.refs_2_), channel_id=1, source_target_pairs={{0,4},{4,0},{1,5},{5,1},{2,6},{6,2},{3,7},{7,3},{8,12},{12,8},{9,1... | collective-permute-start | bytes 1572872 | tf_op jit(solution)/shard_map/ppermute | solution.py:222
  108.9 2.0 %copy-start.11 = (bf16[4,4,16,1024]{3,2,1,0:T(8,128)(2,1)}, bf16[4,4,16,1024]{3,2,1,0:T(8,128)(2,1)S(1)}, u32[]{:S(2)}) copy-start(bf16[4,4,16,1024]{3,2,1,0:T(8,128)(2,1)S(1)} %collective-permute-done.5.refs_3_) | copy-start | bytes 1572868
  108.9 3.9 %collective-permute-start.9 = (bf16[4,4,16,1024]{3,2,1,0:T(8,128)(2,1)S(1)}, bf16[4,4,16,1024]{3,2,1,0:T(8,128)(2,1)}, u32[]{:S(2)}, u32[]{:S(2)}) collective-permute-start(bf16[4,4,16,1024]{3,2,1,0:T(8,128)(2,1)S(1)} %collective-permute-done.5.refs_3_), channel_id=1, source_target_pairs={{0,4},{4,0},{1,5},{5,1},{2,6},{6,2},{3,7},{7,3},{8,12},{12,8},{9,1... | collective-permute-start | bytes 1572872 | tf_op jit(solution)/shard_map/ppermute | solution.py:222
  110.9 0.8 copy-start.12
  110.9 1.0 copy-start.13
  111.9 0.8 copy-start.14
  112.9 1.4 %copy-start.7 = (bf16[4,528,512]{2,1,0:T(8,128)(2,1)}, bf16[4,528,512]{2,1,0:T(8,128)(2,1)S(1)}, u32[]{:S(2)}) copy-start(bf16[4,528,512]{2,1,0:T(8,128)(2,1)S(1)} %all-to-all-done.3.h_ref) | copy-start | bytes 6488068

commit v3 on v2

--- a/solution.py
+++ b/solution.py
@@ -115,9 +115,9 @@
         o_ref[j, rows:, :] = extra.astype(BF16)
 
 
-def project_body(h_ref, *refs):
+def assemble_body(*refs):
     blocks = refs[:8]
-    o_ref, w_ref, sem = refs[8:]
+    w_ref, sem = refs[8:]
     core = lax.axis_index(C)
     zl = lax.axis_index(ZL)
     y = lax.axis_index(Y)
@@ -132,6 +132,11 @@
             copies.append(pltpu.make_async_copy(block.at[k], to, sem.at[n, k]))
     for copy in copies:
         copy.start()
+    for copy in copies:
+        copy.wait()
+
+
+def project_body(h_ref, w_ref, o_ref):
     rows, width = o_ref.shape
     parts = h_ref.shape[0]
     each = h_ref.shape[2]
@@ -141,8 +146,6 @@
             row = row + h_ref[s, rows + j : rows + j + 1, :].astype(F32)
     inv = lax.rsqrt(row / (parts * each) + 1e-06)
     inv = jnp.broadcast_to(inv, (HD, rows)).T
-    for copy in copies:
-        copy.wait()
     blk = 256
     for i in range(rows // blk):
         r = slice(i * blk, (i + 1) * blk)
@@ -221,12 +224,14 @@
     for block in mine:
         other.append(lax.ppermute(block, C, ((0, 1), (1, 0))))
     full = (far, lax.axis_size(ZL), lax.axis_size(Y), 2, *out_weight.shape)
+    weight = call(
+        assemble_body, bf16(full), 8, 10**6, 8 * 2**20,
+        in_specs=[ANY] * 8,
+        scratch=[pltpu.SemaphoreType.DMA((8, 4))],
+    )(*mine, *other)
     return call(
-        project_body, bf16((rows, cols)), 3, 2 * 10**9, 8 * 2**20,
-        in_specs=[VMEM] + [ANY] * 8,
-        grant=60,
-        scratch=[pltpu.VMEM(full, BF16), pltpu.SemaphoreType.DMA((8, 4))],
-    )(features, *mine, *other)
+        project_body, bf16((rows, cols)), 2, 2 * 10**9, 8 * 2**20
+    )(features, weight)
 
 
 def solution(mesh):

time: 122 us -> 122 us (level)
  the two profiles are of different devices: /device:TPU:27 before, /device:TPU:1 now
where the time goes in v3:
time: 122 us
  blocking collectives  45.7 us (37%)
  starting transfers between devices  41.4 us (34%)
  waiting for transfers between devices  14.1 us (12%)
  local copies, waits for them, and re-layouts  11.5 us (9%)
  Pallas kernels  8.59 us (7%)
    all_to_all x2, blocking collectives, swap(): return lax.all_to_all(array, axes, 0, 0, tiled=True)  45.7 us
    ppermute x6, starting transfers between devices, moved(): return lax.ppermute(array, SEQ, pairs)  16.1 us
    all_to_all x2, starting transfers between devices, swap(): return lax.all_to_all(array, axes, 0, 0, tiled=True)  12.9 us
    ppermute x4, starting transfers between devices, per_device(): other.append(lax.ppermute(block, C, ((0, 1), (1, 0))))  12.4 us
    unnamed x22, local copies, waits for them, and re-layouts  11.5 us
    ppermute x6, waiting for transfers between devices, moved(): return lax.ppermute(array, SEQ, pairs)  6.61 us
    all_to_all x2, waiting for transfers between devices, swap(): return lax.all_to_all(array, axes, 0, 0, tiled=True)  6 us
    pallas_call x1, Pallas kernels, per_device(): call(project_body, bf16((rows, cols)), 2, 2 * 10 ** 9, 8 * 2 ** 20)  3.3 us
  transfers between devices with their start and end apart: 12, of which 6 were waited for; matrix products, arithmetic and copies ran while one was open for 0% of the time, Pallas kernels for 3%

profile of v3, /device:TPU:1, one launch (start us, length us, event | category | flops | bytes accessed | tf_op | source)
XLA Modules:
  0.0 121.5 jit_solution(13029033341391218660)
XLA Ops:
  0.0 1.0 copy-done.5
  1.0 1.0 copy-done.7
  2.5 21.2 %all_to_all.20.r_ref = f32[32,16,128]{2,1,0:T(8,128)S(1)} all-to-all(f32[32,16,128]{2,1,0:T(8,128)S(1)} %bitcast.6), channel_id=1, replica_groups=mesh['zh'=4,'zl'=4,'y'=4,'c'=2,'x'=4] {'zl','y','c'}, dimensions={0} | all-to-all | bytes 524288 | tf_op jit(solution)/shard_map/all_to_all | solution.py:162
  23.6 0.8 copy-done.10
  24.4 24.5 %all_to_all.21.t_ref = bf16[4,16,1280]{2,1,0:T(8,128)(2,1)S(1)} all-to-all(bf16[4,16,1280]{2,1,0:T(8,128)(2,1)S(1)} %get-tuple-element.10), channel_id=1, replica_groups=mesh['zh'=4,'zl'=4,'y'=4,'c'=2,'x'=4] {'zh'}, dimensions={0} | all-to-all | bytes 327680 | tf_op jit(solution)/shard_map/all_to_all | solution.py:162
  48.9 0.7 shard_map.57
  49.6 8.9 %all-to-all-start.2 = ((bf16[32,16,128]{2,1,0:T(8,128)(2,1)}), bf16[32,16,128]{2,1,0:T(8,128)(2,1)S(1)}, u32[]{:S(2)}, u32[]{:S(2)}) async-start(bf16[32,16,128]{2,1,0:T(8,128)(2,1)} %get-tuple-element.11), calls=%async_computation.2 | async-start | bytes 262144 | tf_op jit(solution)/shard_map/all_to_all | solution.py:162
  58.5 1.0 copy-done.3
  59.6 1.4 %shard_map.58.l_ref = f32[512,512]{1,0:T(8,128)S(1)} custom-call(bf16[512,512]{1,0:T(8,128)(2,1)S(1)} %copy-done.3, bf16[512,512]{1,0:T(8,128)(2,1)S(1)} %copy-done.6, bf16[512,512]{1,0:T(8,128)(2,1)S(1)} %copy-done.8), custom_call_target="tpu_custom_call" | custom-call | flops 500000000 | bytes 2097152 | tf_op jit(solution)/shard_map/pallas_call | solution.py:196
  61.0 6.0 %all-to-all-done.2 = bf16[32,16,128]{2,1,0:T(8,128)(2,1)S(1)} async-done(((bf16[32,16,128]{2,1,0:T(8,128)(2,1)}), bf16[32,16,128]{2,1,0:T(8,128)(2,1)S(1)}, u32[]{:S(2)}, u32[]{:S(2)}) %all-to-all-start.2) | async-done | bytes 131104 | tf_op jit(solution)/shard_map/all_to_all | solution.py:162
  67.0 1.0 copy-done.4
  68.1 1.0 copy-done.9
  69.1 0.7 shard_map.59
  69.9 1.4 %copy-done.2 = bf16[4,528,512]{2,1,0:T(8,128)(2,1)} copy-done((bf16[4,528,512]{2,1,0:T(8,128)(2,1)}, bf16[4,528,512]{2,1,0:T(8,128)(2,1)S(1)}, u32[]{:S(2)}) %copy-start.2) | copy-done | bytes 2162712
  71.2 4.0 %all-to-all-start.3 = ((bf16[4,528,512]{2,1,0:T(8,128)(2,1)}), bf16[4,528,512]{2,1,0:T(8,128)(2,1)S(1)}, u32[]{:S(2)}, u32[]{:S(2)}) async-start(bf16[4,528,512]{2,1,0:T(8,128)(2,1)} %copy-done.2), calls=%async_computation.3 | async-start | bytes 4325376 | tf_op jit(solution)/shard_map/all_to_all | solution.py:162
  75.2 2.5 %collective-permute-start.2 = (bf16[4,16,1024]{2,1,0:T(8,128)(2,1)S(1)}, bf16[4,16,1024]{2,1,0:T(8,128)(2,1)S(1)}, u32[]{:S(2)}, u32[]{:S(2)}) collective-permute-start(bf16[4,16,1024]{2,1,0:T(8,128)(2,1)S(1)} %get-tuple-element.12), channel_id=1, source_target_pairs={{0,64},{4,20},{8,72},{12,28},{16,80},{20,4},{24,88},{28,12},{32,48... | collective-permute-start | bytes 393224 | tf_op jit(solution)/shard_map/ppermute | solution.py:179
  77.8 4.0 %collective-permute-start.1 = (bf16[4,16,1024]{2,1,0:T(8,128)(2,1)S(1)}, bf16[4,16,1024]{2,1,0:T(8,128)(2,1)S(1)}, u32[]{:S(2)}, u32[]{:S(2)}) collective-permute-start(bf16[4,16,1024]{2,1,0:T(8,128)(2,1)S(1)} %get-tuple-element.12), channel_id=1, source_target_pairs={{0,480},{4,28},{8,488},{12,4},{16,496},{20,12},{24,504},{28,20},{3... | collective-permute-start | bytes 393224 | tf_op jit(solution)/shard_map/ppermute | solution.py:179
  81.7 1.9 %collective-permute-start = (bf16[4,16,1024]{2,1,0:T(8,128)(2,1)S(1)}, bf16[4,16,1024]{2,1,0:T(8,128)(2,1)S(1)}, u32[]{:S(2)}, u32[]{:S(2)}) collective-permute-start(bf16[4,16,1024]{2,1,0:T(8,128)(2,1)S(1)} %get-tuple-element.12), channel_id=1, source_target_pairs={{0,32},{4,12},{8,40},{12,20},{16,48},{20,28},{24,56},{28,4},{32,64... | collective-permute-start | bytes 393224 | tf_op jit(solution)/shard_map/ppermute | solution.py:179
  83.8 5.2 %collective-permute-done = bf16[4,16,1024]{2,1,0:T(8,128)(2,1)S(1)} collective-permute-done((bf16[4,16,1024]{2,1,0:T(8,128)(2,1)S(1)}, bf16[4,16,1024]{2,1,0:T(8,128)(2,1)S(1)}, u32[]{:S(2)}, u32[]{:S(2)}) %collective-permute-start) | collective-permute-done | bytes 131104 | tf_op jit(solution)/shard_map/ppermute | solution.py:179
  89.0 2.4 %collective-permute-start.5 = (bf16[4,4,16,1024]{3,2,1,0:T(8,128)(2,1)S(1)}, bf16[4,4,16,1024]{3,2,1,0:T(8,128)(2,1)S(1)}, u32[]{:S(2)}, u32[]{:S(2)}) collective-permute-start(bf16[4,4,16,1024]{3,2,1,0:T(8,128)(2,1)S(1)} %pad_maximum_fusion.refs_0_), channel_id=1, source_target_pairs={{0,16},{4,68},{8,24},{12,76},{16,0},{20,84},{24,8},{28,92},{32,48}... | collective-permute-start | bytes 1572872 | tf_op jit(solution)/shard_map/ppermute | solution.py:179
  91.4 2.1 %collective-permute-start.4 = (bf16[4,4,16,1024]{3,2,1,0:T(8,128)(2,1)S(1)}, bf16[4,4,16,1024]{3,2,1,0:T(8,128)(2,1)S(1)}, u32[]{:S(2)}, u32[]{:S(2)}) collective-permute-start(bf16[4,4,16,1024]{3,2,1,0:T(8,128)(2,1)S(1)} %pad_maximum_fusion.refs_0_), channel_id=1, source_target_pairs={{0,24},{4,484},{8,0},{12,492},{16,8},{20,500},{24,16},{28,508},{32... | collective-permute-start | bytes 1572872 | tf_op jit(solution)/shard_map/ppermute | solution.py:179
  93.5 3.2 %collective-permute-start.3 = (bf16[4,4,16,1024]{3,2,1,0:T(8,128)(2,1)S(1)}, bf16[4,4,16,1024]{3,2,1,0:T(8,128)(2,1)S(1)}, u32[]{:S(2)}, u32[]{:S(2)}) collective-permute-start(bf16[4,4,16,1024]{3,2,1,0:T(8,128)(2,1)S(1)} %pad_maximum_fusion.refs_0_), channel_id=1, source_target_pairs={{0,8},{4,36},{8,16},{12,44},{16,24},{20,52},{24,0},{28,60},{32,40}... | collective-permute-start | bytes 1572872 | tf_op jit(solution)/shard_map/ppermute | solution.py:179
  96.7 3.5 %collective-permute-start.6 = (bf16[4,4,16,1024]{3,2,1,0:T(8,128)(2,1)S(1)}, bf16[4,4,16,1024]{3,2,1,0:T(8,128)(2,1)S(1)}, u32[]{:S(2)}, u32[]{:S(2)}) collective-permute-start(bf16[4,4,16,1024]{3,2,1,0:T(8,128)(2,1)S(1)} %pad_maximum_fusion.refs_0_), channel_id=1, source_target_pairs={{0,4},{4,0},{1,5},{5,1},{2,6},{6,2},{3,7},{7,3},{8,12},{12,8},{9,1... | collective-permute-start | bytes 1572872 | tf_op jit(solution)/shard_map/ppermute | solution.py:225
  100.2 1.2 collective-permute-done.5.refs_3_
  101.4 2.4 %collective-permute-start.9 = (bf16[4,4,16,1024]{3,2,1,0:T(8,128)(2,1)S(1)}, bf16[4,4,16,1024]{3,2,1,0:T(8,128)(2,1)S(1)}, u32[]{:S(2)}, u32[]{:S(2)}) collective-permute-start(bf16[4,4,16,1024]{3,2,1,0:T(8,128)(2,1)S(1)} %collective-permute-done.5.refs_3_), channel_id=1, source_target_pairs={{0,4},{4,0},{1,5},{5,1},{2,6},{6,2},{3,7},{7,3},{8,12},{12,8},{9,1... | collective-permute-start | bytes 1572872 | tf_op jit(solution)/shard_map/ppermute | solution.py:225
  103.9 4.1 %collective-permute-start.8 = (bf16[4,4,16,1024]{3,2,1,0:T(8,128)(2,1)S(1)}, bf16[4,4,16,1024]{3,2,1,0:T(8,128)(2,1)S(1)}, u32[]{:S(2)}, u32[]{:S(2)}) collective-permute-start(bf16[4,4,16,1024]{3,2,1,0:T(8,128)(2,1)S(1)} %collective-permute-done.4.refs_2_), channel_id=1, source_target_pairs={{0,4},{4,0},{1,5},{5,1},{2,6},{6,2},{3,7},{7,3},{8,12},{12,8},{9,1... | collective-permute-start | bytes 1572872 | tf_op jit(solution)/shard_map/ppermute | solution.py:225
  108.0 2.5 %collective-permute-start.7 = (bf16[4,4,16,1024]{3,2,1,0:T(8,128)(2,1)S(1)}, bf16[4,4,16,1024]{3,2,1,0:T(8,128)(2,1)S(1)}, u32[]{:S(2)}, u32[]{:S(2)}) collective-permute-start(bf16[4,4,16,1024]{3,2,1,0:T(8,128)(2,1)S(1)} %collective-permute-done.3.refs_1_), channel_id=1, source_target_pairs={{0,4},{4,0},{1,5},{5,1},{2,6},{6,2},{3,7},{7,3},{8,12},{12,8},{9,1... | collective-permute-start | bytes 1572872 | tf_op jit(solution)/shard_map/ppermute | solution.py:225
  110.6 1.5 %collective-permute-done.7.refs_5_ = bf16[4,4,16,1024]{3,2,1,0:T(8,128)(2,1)S(1)} collective-permute-done((bf16[4,4,16,1024]{3,2,1,0:T(8,128)(2,1)S(1)}, bf16[4,4,16,1024]{3,2,1,0:T(8,128)(2,1)S(1)}, u32[]{:S(2)}, u32[]{:S(2)}) %collective-permute-start.7) | collective-permute-done | bytes 524320 | tf_op jit(solution)/shard_map/ppermute | solution.py:225
  112.0 2.0 %shard_map.60.w_ref = bf16[4,4,4,2,16,1024]{5,4,3,2,1,0:T(8,128)(2,1)S(1)} custom-call(bf16[4,4,16,1024]{3,2,1,0:T(8,128)(2,1)S(1)} %pad_maximum_fusion.refs_0_, bf16[4,4,16,1024]{3,2,1,0:T(8,128)(2,1)S(1)} %collective-permute-done.3.refs_1_, bf16[4,4,16,1024]{3,2,1,0:T(8,128)(2,1)S(1)} %collective-permute-done.4.refs_2_, ...), custom_call_target="tpu_custom_call" | custom-call | flops 1000000 | bytes 8388608 | tf_op jit(solution)/shard_map/pallas_call | solution.py:227
  114.1 1.9 %copy-done = bf16[4,4,4,2,16,1024]{5,4,3,2,1,0:T(8,128)(2,1)} copy-done((bf16[4,4,4,2,16,1024]{5,4,3,2,1,0:T(8,128)(2,1)}, bf16[4,4,4,2,16,1024]{5,4,3,2,1,0:T(8,128)(2,1)S(1)}, u32[]{:S(2)}) %copy-start) | copy-done | bytes 4194328
  116.0 2.2 %copy-done.1 = bf16[4,4,4,2,16,1024]{5,4,3,2,1,0:T(8,128)(2,1)S(1)} copy-done((bf16[4,4,4,2,16,1024]{5,4,3,2,1,0:T(8,128)(2,1)S(1)}, bf16[4,4,4,2,16,1024]{5,4,3,2,1,0:T(8,128)(2,1)}, u32[]{:S(2)}) %copy-start.1) | copy-done | bytes 4194328
  118.2 3.3 %shard_map.61 = bf16[512,1024]{1,0:T(8,128)(2,1)} custom-call(bf16[4,528,512]{2,1,0:T(8,128)(2,1)S(1)} %all-to-all-done.3.h_ref, bf16[4,4,4,2,16,1024]{5,4,3,2,1,0:T(8,128)(2,1)S(1)} %copy-done.1), custom_call_target="tpu_custom_call" | custom-call | flops 2000000000 | bytes 8388608 | tf_op jit(solution)/shard_map/pallas_call | solution.py:232
  (24 shorter events, 0.7 us)
Async XLA Ops:
  0.0 1.0 copy-start.5
  1.0 1.0 copy-start.7
  2.1 56.4 %copy-start.8 = (bf16[512,512]{1,0:T(8,128)(2,1)S(1)}, bf16[512,512]{1,0:T(8,128)(2,1)}, u32[]{:S(2)}) copy-start(bf16[512,512]{1,0:T(8,128)(2,1)} %v_ref.3) | copy-start | bytes 1572868
  2.4 56.1 %copy-start.6 = (bf16[512,512]{1,0:T(8,128)(2,1)S(1)}, bf16[512,512]{1,0:T(8,128)(2,1)}, u32[]{:S(2)}) copy-start(bf16[512,512]{1,0:T(8,128)(2,1)} %k_ref.3) | copy-start | bytes 1572868
  23.6 0.8 copy-start.10
  49.6 17.4 %all-to-all-start.2 = ((bf16[32,16,128]{2,1,0:T(8,128)(2,1)}), bf16[32,16,128]{2,1,0:T(8,128)(2,1)S(1)}, u32[]{:S(2)}, u32[]{:S(2)}) async-start(bf16[32,16,128]{2,1,0:T(8,128)(2,1)} %get-tuple-element.11), calls=%async_computation.2 | async-start | bytes 262144 | tf_op jit(solution)/shard_map/all_to_all | solution.py:162
  58.5 1.0 copy-start.3
  67.0 1.0 copy-start.4
  68.1 1.0 copy-start.9
  69.8 1.4 %copy-start.2 = (bf16[4,528,512]{2,1,0:T(8,128)(2,1)}, bf16[4,528,512]{2,1,0:T(8,128)(2,1)S(1)}, u32[]{:S(2)}) copy-start(bf16[4,528,512]{2,1,0:T(8,128)(2,1)S(1)} %shard_map.59) | copy-start | bytes 6488068
  71.2 44.8 %all-to-all-start.3 = ((bf16[4,528,512]{2,1,0:T(8,128)(2,1)}), bf16[4,528,512]{2,1,0:T(8,128)(2,1)S(1)}, u32[]{:S(2)}, u32[]{:S(2)}) async-start(bf16[4,528,512]{2,1,0:T(8,128)(2,1)} %copy-done.2), calls=%async_computation.3 | async-start | bytes 4325376 | tf_op jit(solution)/shard_map/all_to_all | solution.py:162
  75.2 8.4 %collective-permute-start.2 = (bf16[4,16,1024]{2,1,0:T(8,128)(2,1)S(1)}, bf16[4,16,1024]{2,1,0:T(8,128)(2,1)S(1)}, u32[]{:S(2)}, u32[]{:S(2)}) collective-permute-start(bf16[4,16,1024]{2,1,0:T(8,128)(2,1)S(1)} %get-tuple-element.12), channel_id=1, source_target_pairs={{0,64},{4,20},{8,72},{12,28},{16,80},{20,4},{24,88},{28,12},{32,48... | collective-permute-start | bytes 393224 | tf_op jit(solution)/shard_map/ppermute | solution.py:179
  77.8 6.0 %collective-permute-start.1 = (bf16[4,16,1024]{2,1,0:T(8,128)(2,1)S(1)}, bf16[4,16,1024]{2,1,0:T(8,128)(2,1)S(1)}, u32[]{:S(2)}, u32[]{:S(2)}) collective-permute-start(bf16[4,16,1024]{2,1,0:T(8,128)(2,1)S(1)} %get-tuple-element.12), channel_id=1, source_target_pairs={{0,480},{4,28},{8,488},{12,4},{16,496},{20,12},{24,504},{28,20},{3... | collective-permute-start | bytes 393224 | tf_op jit(solution)/shard_map/ppermute | solution.py:179
  81.7 7.2 %collective-permute-start = (bf16[4,16,1024]{2,1,0:T(8,128)(2,1)S(1)}, bf16[4,16,1024]{2,1,0:T(8,128)(2,1)S(1)}, u32[]{:S(2)}, u32[]{:S(2)}) collective-permute-start(bf16[4,16,1024]{2,1,0:T(8,128)(2,1)S(1)} %get-tuple-element.12), channel_id=1, source_target_pairs={{0,32},{4,12},{8,40},{12,20},{16,48},{20,28},{24,56},{28,4},{32,64... | collective-permute-start | bytes 393224 | tf_op jit(solution)/shard_map/ppermute | solution.py:179
  89.0 12.3 %collective-permute-start.5 = (bf16[4,4,16,1024]{3,2,1,0:T(8,128)(2,1)S(1)}, bf16[4,4,16,1024]{3,2,1,0:T(8,128)(2,1)S(1)}, u32[]{:S(2)}, u32[]{:S(2)}) collective-permute-start(bf16[4,4,16,1024]{3,2,1,0:T(8,128)(2,1)S(1)} %pad_maximum_fusion.refs_0_), channel_id=1, source_target_pairs={{0,16},{4,68},{8,24},{12,76},{16,0},{20,84},{24,8},{28,92},{32,48}... | collective-permute-start | bytes 1572872 | tf_op jit(solution)/shard_map/ppermute | solution.py:179
  91.4 12.5 %collective-permute-start.4 = (bf16[4,4,16,1024]{3,2,1,0:T(8,128)(2,1)S(1)}, bf16[4,4,16,1024]{3,2,1,0:T(8,128)(2,1)S(1)}, u32[]{:S(2)}, u32[]{:S(2)}) collective-permute-start(bf16[4,4,16,1024]{3,2,1,0:T(8,128)(2,1)S(1)} %pad_maximum_fusion.refs_0_), channel_id=1, source_target_pairs={{0,24},{4,484},{8,0},{12,492},{16,8},{20,500},{24,16},{28,508},{32... | collective-permute-start | bytes 1572872 | tf_op jit(solution)/shard_map/ppermute | solution.py:179
  93.5 14.4 %collective-permute-start.3 = (bf16[4,4,16,1024]{3,2,1,0:T(8,128)(2,1)S(1)}, bf16[4,4,16,1024]{3,2,1,0:T(8,128)(2,1)S(1)}, u32[]{:S(2)}, u32[]{:S(2)}) collective-permute-start(bf16[4,4,16,1024]{3,2,1,0:T(8,128)(2,1)S(1)} %pad_maximum_fusion.refs_0_), channel_id=1, source_target_pairs={{0,8},{4,36},{8,16},{12,44},{16,24},{20,52},{24,0},{28,60},{32,40}... | collective-permute-start | bytes 1572872 | tf_op jit(solution)/shard_map/ppermute | solution.py:179
  96.7 13.8 %collective-permute-start.6 = (bf16[4,4,16,1024]{3,2,1,0:T(8,128)(2,1)S(1)}, bf16[4,4,16,1024]{3,2,1,0:T(8,128)(2,1)S(1)}, u32[]{:S(2)}, u32[]{:S(2)}) collective-permute-start(bf16[4,4,16,1024]{3,2,1,0:T(8,128)(2,1)S(1)} %pad_maximum_fusion.refs_0_), channel_id=1, source_target_pairs={{0,4},{4,0},{1,5},{5,1},{2,6},{6,2},{3,7},{7,3},{8,12},{12,8},{9,1... | collective-permute-start | bytes 1572872 | tf_op jit(solution)/shard_map/ppermute | solution.py:225
  101.4 9.2 %collective-permute-start.9 = (bf16[4,4,16,1024]{3,2,1,0:T(8,128)(2,1)S(1)}, bf16[4,4,16,1024]{3,2,1,0:T(8,128)(2,1)S(1)}, u32[]{:S(2)}, u32[]{:S(2)}) collective-permute-start(bf16[4,4,16,1024]{3,2,1,0:T(8,128)(2,1)S(1)} %collective-permute-done.5.refs_3_), channel_id=1, source_target_pairs={{0,4},{4,0},{1,5},{5,1},{2,6},{6,2},{3,7},{7,3},{8,12},{12,8},{9,1... | collective-permute-start | bytes 1572872 | tf_op jit(solution)/shard_map/ppermute | solution.py:225
  103.9 6.7 %collective-permute-start.8 = (bf16[4,4,16,1024]{3,2,1,0:T(8,128)(2,1)S(1)}, bf16[4,4,16,1024]{3,2,1,0:T(8,128)(2,1)S(1)}, u32[]{:S(2)}, u32[]{:S(2)}) collective-permute-start(bf16[4,4,16,1024]{3,2,1,0:T(8,128)(2,1)S(1)} %collective-permute-done.4.refs_2_), channel_id=1, source_target_pairs={{0,4},{4,0},{1,5},{5,1},{2,6},{6,2},{3,7},{7,3},{8,12},{12,8},{9,1... | collective-permute-start | bytes 1572872 | tf_op jit(solution)/shard_map/ppermute | solution.py:225
  108.0 4.1 %collective-permute-start.7 = (bf16[4,4,16,1024]{3,2,1,0:T(8,128)(2,1)S(1)}, bf16[4,4,16,1024]{3,2,1,0:T(8,128)(2,1)S(1)}, u32[]{:S(2)}, u32[]{:S(2)}) collective-permute-start(bf16[4,4,16,1024]{3,2,1,0:T(8,128)(2,1)S(1)} %collective-permute-done.3.refs_1_), channel_id=1, source_target_pairs={{0,4},{4,0},{1,5},{5,1},{2,6},{6,2},{3,7},{7,3},{8,12},{12,8},{9,1... | collective-permute-start | bytes 1572872 | tf_op jit(solution)/shard_map/ppermute | solution.py:225
  114.1 1.9 %copy-start = (bf16[4,4,4,2,16,1024]{5,4,3,2,1,0:T(8,128)(2,1)}, bf16[4,4,4,2,16,1024]{5,4,3,2,1,0:T(8,128)(2,1)S(1)}, u32[]{:S(2)}) copy-start(bf16[4,4,4,2,16,1024]{5,4,3,2,1,0:T(8,128)(2,1)S(1)} %shard_map.60.w_ref) | copy-start | bytes 12582916
  116.0 2.2 %copy-start.1 = (bf16[4,4,4,2,16,1024]{5,4,3,2,1,0:T(8,128)(2,1)S(1)}, bf16[4,4,4,2,16,1024]{5,4,3,2,1,0:T(8,128)(2,1)}, u32[]{:S(2)}) copy-start(bf16[4,4,4,2,16,1024]{5,4,3,2,1,0:T(8,128)(2,1)} %copy-done) | copy-start | bytes 12582916

commit v4 on v3

--- a/solution.py
+++ b/solution.py
@@ -23,12 +23,12 @@
 ANY = pl.BlockSpec(memory_space=pl.ANY)
 
 
-def call(body, outs, n_in, flops, nbytes, in_specs=None, scratch=(), grant=16):
+def call(body, outs, n_in, flops, nbytes, in_specs=None, out_spec=VMEM, scratch=(), grant=16):
     return pl.pallas_call(
         body,
         out_shape=outs,
         in_specs=in_specs or [VMEM] * n_in,
-        out_specs=jax.tree.map(lambda _: VMEM, outs),
+        out_specs=jax.tree.map(lambda _: out_spec, outs),
         scratch_shapes=list(scratch),
         cost_estimate=pl.CostEstimate(
             flops=flops, bytes_accessed=nbytes, transcendentals=0
@@ -37,13 +37,23 @@
     )
 
 
-def state_body(k_ref, v_ref, s_ref):
+def state_body(k_hbm, v_hbm, w_hbm, s_ref, w_ref, k_ref, v_ref, sem):
+    copies = [
+        pltpu.make_async_copy(k_hbm, k_ref, sem.at[0]),
+        pltpu.make_async_copy(v_hbm, v_ref, sem.at[1]),
+        pltpu.make_async_copy(w_hbm, w_ref, sem.at[2]),
+    ]
+    for copy in copies:
+        copy.start()
+    copies[0].wait()
+    copies[1].wait()
     for h in range(k_ref.shape[1] // HD):
         cols = slice(h * HD, (h + 1) * HD)
         s_ref[h] = lax.dot_general(
             k_ref[:, cols], v_ref[:, cols], (((0,), (0,)), ((), ())),
             preferred_element_type=F32,
         )
+    copies[2].wait()
 
 
 def local_body(q_ref, k_ref, v_ref, o_ref):
@@ -101,8 +111,7 @@
         inter = jnp.dot(q_ref[:, cols], p_ref[h], preferred_element_type=F32)
         attn = l_ref[:, cols] + inter * scale
         squares = squares + attn * attn
-        gate = g_ref[:, cols].astype(F32)
-        hid = (attn * (gate / (1.0 + jnp.exp(-gate)))).astype(BF16)
+        hid = (attn * g_ref[:, cols]).astype(BF16)
         for j in range(o_ref.shape[0]):
             o_ref[j, :rows, cols] = hid
     row = jnp.sum(squares.T, axis=0, keepdims=True)
@@ -116,19 +125,18 @@
 
 
 def assemble_body(*refs):
-    blocks = refs[:8]
-    w_ref, sem = refs[8:]
+    blocks = refs[:4]
+    w_ref, sem = refs[4:]
     core = lax.axis_index(C)
     zl = lax.axis_index(ZL)
     y = lax.axis_index(Y)
     copies = []
     for n, block in enumerate(blocks):
-        owner = core if n < 4 else 1 - core
         for k in range(4):
-            outer, inner = NEXT[n % 4], NEXT[k]
-            by_z = jnp.where(owner == 0, inner, outer)
-            by_y = jnp.where(owner == 0, outer, inner)
-            to = w_ref.at[:, lax.rem(zl + by_z, 4), lax.rem(y + by_y, 4), owner]
+            outer, inner = NEXT[n], NEXT[k]
+            by_z = jnp.where(core == 0, inner, outer)
+            by_y = jnp.where(core == 0, outer, inner)
+            to = w_ref.at[:, lax.rem(zl + by_z, 4), lax.rem(y + by_y, 4)]
             copies.append(pltpu.make_async_copy(block.at[k], to, sem.at[n, k]))
     for copy in copies:
         copy.start()
@@ -136,26 +144,59 @@
         copy.wait()
 
 
-def project_body(h_ref, w_ref, o_ref):
+def project_body(h_hbm, mine_ref, other_ref, out_ref, h_ref, w_ref, acc_ref, o_ref, sem, out_sem):
     rows, width = o_ref.shape
     parts = h_ref.shape[0]
     each = h_ref.shape[2]
-    row = jnp.zeros((1, rows), F32)
+    core = lax.axis_index(C)
+    span = w_ref.shape[0] // parts
+    tile = 256
+    copies = []
     for s in range(parts):
-        for j in range(3):
-            row = row + h_ref[s, rows + j : rows + j + 1, :].astype(F32)
-    inv = lax.rsqrt(row / (parts * each) + 1e-06)
-    inv = jnp.broadcast_to(inv, (HD, rows)).T
-    blk = 256
-    for i in range(rows // blk):
-        r = slice(i * blk, (i + 1) * blk)
-        for n in range(width // 256):
-            c = slice(n * 256, (n + 1) * 256)
-            acc = jnp.zeros((blk, 256), F32)
-            for s in range(parts):
-                w = w_ref[s, :, :, :, :, c].reshape(each, 256)
-                acc = acc + jnp.dot(h_ref[s, r, :], w, preferred_element_type=F32)
-            o_ref[r, c] = (acc * inv[r, :1]).astype(BF16)
+        part = slice(s * span, (s + 1) * span)
+        copies.append(
+            [
+                pltpu.make_async_copy(h_hbm.at[s], h_ref.at[s], sem.at[s, 0]),
+                pltpu.make_async_copy(mine_ref.at[part], w_ref.at[part, core], sem.at[s, 1]),
+                pltpu.make_async_copy(other_ref.at[part], w_ref.at[part, 1 - core], sem.at[s, 2]),
+            ]
+        )
+        for copy in copies[s]:
+            copy.start()
+    for s in range(parts):
+        for copy in copies[s]:
+            copy.wait()
+        last = s == parts - 1
+        if last:
+            row = jnp.zeros((1, rows), F32)
+            for p in range(parts):
+                for j in range(3):
+                    row = row + h_ref[p, rows + j : rows + j + 1, :].astype(F32)
+            inv = lax.rsqrt(row / (parts * each) + 1e-06)
+            inv = jnp.broadcast_to(inv, (HD, rows)).T
+        block = rows // 2 if last else rows
+        for i in range(rows // block):
+            r = slice(i * block, (i + 1) * block)
+            for n in range(width // tile):
+                c = slice(n * tile, (n + 1) * tile)
+                w = w_ref[s * span : (s + 1) * span, :, :, c].reshape(each, tile)
+                acc = jnp.dot(h_ref[s, r, :], w, preferred_element_type=F32)
+                if s > 0:
+                    acc = acc + acc_ref[r, c]
+                if last:
+                    o_ref[r, c] = (acc * inv[r, :1]).astype(BF16)
+                else:
+                    acc_ref[r, c] = acc
+            if last:
+                pltpu.make_async_copy(o_ref.at[r], out_ref.at[r], out_sem.at[i]).start()
+    for i in range(2):
+        r = slice(i * (rows // 2), (i + 1) * (rows // 2))
+        pltpu.make_async_copy(o_ref.at[r], out_ref.at[r], out_sem.at[i]).wait()
+
+
+def gate_body(g_ref, o_ref):
+    gate = g_ref[...].astype(F32)
+    o_ref[...] = gate / (1.0 + jnp.exp(-gate))
 
 
 def swap(array, axes):
@@ -190,18 +231,22 @@
     f32 = functools.partial(jax.ShapeDtypeStruct, dtype=F32)
     bf16 = functools.partial(jax.ShapeDtypeStruct, dtype=BF16)
 
-    state = call(state_body, f32((heads, HD, HD)), 2, 10**8, 2**20)(
-        key_vectors, value_vectors
-    )
+    state, w_own = call(
+        state_body, (f32((heads, HD, HD)), bf16(out_weight.shape)), 3, 10**8, 2**20,
+        in_specs=[ANY] * 3,
+        scratch=[pltpu.VMEM((rows, width), BF16)] * 2 + [pltpu.SemaphoreType.DMA((3,))],
+        grant=58,
+    )(key_vectors, value_vectors, out_weight)
     local = call(local_body, f32((rows, width)), 3, 5 * 10**8, 2**21)(
         queries, key_vectors, value_vectors
     )
+    gate = call(gate_body, f32((rows, width)), 1, 10**6, 2**20)(gate_input)
     pieces = swap(state.reshape(near, *piece), NEAR)
     earlier, total = call(
         near_prefix_body,
         (f32((near, *piece)), bf16((far, piece[0], cols + 2 * HD))),
         2, 10**6, 2**19,
-    )(pieces, out_weight)
+    )(pieces, w_own)
     totals = swap(total, (ZH,))
     prefix, w_far = call(
         far_prefix_body,
@@ -211,27 +256,40 @@
     prefix = swap(prefix, NEAR).reshape(heads, HD, HD)
     hidden = call(
         hidden_body, bf16((group, rows + 16, width)), 4, 10**8, 2**22
-    )(queries, prefix, local, gate_input)
+    )(queries, prefix, local, gate)
     features = swap(hidden, (X,))
     first = [w_far]
     for step in STEPS:
         first.append(moved(w_far, "z", "y", step))
+    *first, _ = lax.optimization_barrier((*first, hidden))
     first = jnp.stack(first)
     mine = [first]
     for step in STEPS:
         mine.append(moved(first, "y", "z", step))
-    other = []
-    for block in mine:
-        other.append(lax.ppermute(block, C, ((0, 1), (1, 0))))
-    full = (far, lax.axis_size(ZL), lax.axis_size(Y), 2, *out_weight.shape)
+    half = (far, lax.axis_size(ZL), lax.axis_size(Y), *out_weight.shape)
     weight = call(
-        assemble_body, bf16(full), 8, 10**6, 8 * 2**20,
-        in_specs=[ANY] * 8,
-        scratch=[pltpu.SemaphoreType.DMA((8, 4))],
-    )(*mine, *other)
+        assemble_body, bf16(half), 4, 10**6, 4 * 2**20,
+        in_specs=[ANY] * 4,
+        out_spec=ANY,
+        scratch=[pltpu.SemaphoreType.DMA((4, 4))],
+    )(*mine)
+    other = lax.ppermute(weight, C, ((0, 1), (1, 0)))
+    flat = (-1, *out_weight.shape)
+    count = half[0] * half[1] * half[2]
     return call(
-        project_body, bf16((rows, cols)), 2, 2 * 10**9, 8 * 2**20
-    )(features, weight)
+        project_body, bf16((rows, cols)), 3, 2 * 10**9, 8 * 2**20,
+        in_specs=[ANY] * 3,
+        out_spec=ANY,
+        scratch=[
+            pltpu.VMEM((group, rows + 16, width), BF16),
+            pltpu.VMEM((count, 2, *out_weight.shape), BF16),
+            pltpu.VMEM((rows, cols), F32),
+            pltpu.VMEM((rows, cols), BF16),
+            pltpu.SemaphoreType.DMA((group, 3)),
+            pltpu.SemaphoreType.DMA((2,)),
+        ],
+        grant=60,
+    )(features, weight.reshape(flat), other.reshape(flat))
 
 
 def solution(mesh):

time: 122 us -> 135 us (1.11)
  blocking collectives: 45.7 us -> 76.2 us
  starting transfers between devices: 41.4 us -> 32.8 us
  local copies, waits for them, and re-layouts: 11.5 us -> 3.16 us
  waiting for transfers between devices: 14.1 us -> 9.71 us
  Pallas kernels: 8.59 us -> 11.3 us
    all_to_all x2 -> x3, blocking collectives: 45.7 us -> 76.2 us  [swap(): return lax.all_to_all(array, axes, 0, 0, tiled=True)]
    unnamed x22 -> x14, local copies, waits for them, and re-layouts: 11.5 us -> 3.16 us
    ppermute x4 -> x1, starting transfers between devices: 12.4 us -> 4.56 us  [per_device(): other = lax.ppermute(weight, C, ((0, 1), (1, 0)))]
    all_to_all x2 -> x1, waiting for transfers between devices: 6 us -> 0.01 us  [swap(): return lax.all_to_all(array, axes, 0, 0, tiled=True)]
    all_to_all x2 -> x1, starting transfers between devices: 12.9 us -> 8.87 us  [swap(): return lax.all_to_all(array, axes, 0, 0, tiled=True)]
    ppermute x6, starting transfers between devices: 16.1 us -> 19.3 us  [moved(): return lax.ppermute(array, SEQ, pairs)]
    ppermute x6, waiting for transfers between devices: 6.61 us -> 9.7 us  [moved(): return lax.ppermute(array, SEQ, pairs)]
    pallas_call x3 -> x4, Pallas kernels: 5.69 us -> 8.46 us  [the longest x1 4.79 us: per_device(): call(project_body, bf16((rows, cols)), 3, 2 * 10 ** 9, 8 * 2 ** 20, in_sp...]
  transfers between devices with their start and end apart: 12 -> 8, of which waited for: 6 -> 4; matrix products, arithmetic and copies ran while one was open for 0% -> 0% of each run, Pallas kernels for 3% -> 2%
where the time goes in v4:
time: 135 us; the launch traced here: 134 us
  blocking collectives  76.2 us (56%)
  starting transfers between devices  32.8 us (24%)
  Pallas kernels  11.3 us (8%)
  waiting for transfers between devices  9.71 us (7%)
  local copies, waits for them, and re-layouts  3.16 us (2%)
    all_to_all x3, blocking collectives, swap(): return lax.all_to_all(array, axes, 0, 0, tiled=True)  76.2 us
    ppermute x6, starting transfers between devices, moved(): return lax.ppermute(array, SEQ, pairs)  19.3 us
    ppermute x6, waiting for transfers between devices, moved(): return lax.ppermute(array, SEQ, pairs)  9.7 us
    all_to_all x1, starting transfers between devices, swap(): return lax.all_to_all(array, axes, 0, 0, tiled=True)  8.87 us
    pallas_call x1, Pallas kernels, per_device(): call(project_body, bf16((rows, cols)), 3, 2 * 10 ** 9, 8 * 2 ** 20, in_sp...  4.79 us
    ppermute x1, starting transfers between devices, per_device(): other = lax.ppermute(weight, C, ((0, 1), (1, 0)))  4.56 us
    unnamed x14, local copies, waits for them, and re-layouts  3.16 us
  transfers between devices with their start and end apart: 8, of which 4 were waited for; matrix products, arithmetic and copies ran while one was open for 0% of the time, Pallas kernels for 2%

profile of v4, /device:TPU:1, one launch (start us, length us, event | category | flops | bytes accessed | tf_op | source)
XLA Modules:
  0.0 134.3 jit_solution(11057022087206232398)
XLA Ops:
  0.0 2.4 %shard_map.55 = (f32[4,128,128]{2,1,0:T(8,128)}, bf16[16,1024]{1,0:T(8,128)(2,1)}) custom-call(bf16[512,512]{1,0:T(8,128)(2,1)} %k_ref.1, bf16[512,512]{1,0:T(8,128)(2,1)} %v_ref.1, bf16[16,1024]{1,0:T(8,128)(2,1)} %w_hbm.1), custom_call_target="tpu_custom_call" | custom-call | flops 100000000 | bytes 1048576 | tf_op jit(solution)/shard_map/pallas_call | solution.py:234
  2.4 21.5 %all_to_all.20.r_ref = f32[32,16,128]{2,1,0:T(8,128)S(1)} all-to-all(f32[32,16,128]{2,1,0:T(8,128)} %bitcast.12), channel_id=1, replica_groups=mesh['zh'=4,'zl'=4,'y'=4,'c'=2,'x'=4] {'zl','y','c'}, dimensions={0} | all-to-all | bytes 524288 | tf_op jit(solution)/shard_map/all_to_all | solution.py:203
  24.0 0.8 copy-done.5
  24.8 24.2 %all_to_all.21.t_ref = bf16[4,16,1280]{2,1,0:T(8,128)(2,1)S(1)} all-to-all(bf16[4,16,1280]{2,1,0:T(8,128)(2,1)S(1)} %get-tuple-element.18), channel_id=1, replica_groups=mesh['zh'=4,'zl'=4,'y'=4,'c'=2,'x'=4] {'zh'}, dimensions={0} | all-to-all | bytes 327680 | tf_op jit(solution)/shard_map/all_to_all | solution.py:203
  49.0 0.7 shard_map.57
  49.7 8.9 %all-to-all-start.2 = ((bf16[32,16,128]{2,1,0:T(8,128)(2,1)}), bf16[32,16,128]{2,1,0:T(8,128)(2,1)S(1)}, u32[]{:S(2)}, u32[]{:S(2)}) async-start(bf16[32,16,128]{2,1,0:T(8,128)(2,1)} %get-tuple-element.19), calls=%async_computation.2 | async-start | bytes 262144 | tf_op jit(solution)/shard_map/all_to_all | solution.py:203
  58.6 4.8 %collective-permute-start.2 = (bf16[4,16,1024]{2,1,0:T(8,128)(2,1)S(1)}, bf16[4,16,1024]{2,1,0:T(8,128)(2,1)S(1)}, u32[]{:S(2)}, u32[]{:S(2)}) collective-permute-start(bf16[4,16,1024]{2,1,0:T(8,128)(2,1)S(1)} %get-tuple-element.21), channel_id=1, source_target_pairs={{0,64},{4,20},{8,72},{12,28},{16,80},{20,4},{24,88},{28,12},{32,48... | collective-permute-start | bytes 393224 | tf_op jit(solution)/shard_map/ppermute | solution.py:220
  63.3 2.8 %collective-permute-start.1 = (bf16[4,16,1024]{2,1,0:T(8,128)(2,1)S(1)}, bf16[4,16,1024]{2,1,0:T(8,128)(2,1)}, u32[]{:S(2)}, u32[]{:S(2)}) collective-permute-start(bf16[4,16,1024]{2,1,0:T(8,128)(2,1)S(1)} %get-tuple-element.21), channel_id=1, source_target_pairs={{0,480},{4,28},{8,488},{12,4},{16,496},{20,12},{24,504},{28,20},{3... | collective-permute-start | bytes 393224 | tf_op jit(solution)/shard_map/ppermute | solution.py:220
  66.1 2.5 %collective-permute-start = (bf16[4,16,1024]{2,1,0:T(8,128)(2,1)S(1)}, bf16[4,16,1024]{2,1,0:T(8,128)(2,1)}, u32[]{:S(2)}, u32[]{:S(2)}) collective-permute-start(bf16[4,16,1024]{2,1,0:T(8,128)(2,1)S(1)} %get-tuple-element.21), channel_id=1, source_target_pairs={{0,32},{4,12},{8,40},{12,20},{16,48},{20,28},{24,56},{28,4},{32,64... | collective-permute-start | bytes 393224 | tf_op jit(solution)/shard_map/ppermute | solution.py:220
  68.6 0.0 copy-done.4
  68.6 0.3 shard_map.59.g_ref
  69.0 0.0 copy-start.3
  69.0 1.0 copy-done.3
  70.0 1.4 %shard_map.58.l_ref = f32[512,512]{1,0:T(8,128)S(1)} custom-call(bf16[512,512]{1,0:T(8,128)(2,1)S(1)} %copy-done.1, bf16[512,512]{1,0:T(8,128)(2,1)S(1)} %copy-done.2, bf16[512,512]{1,0:T(8,128)(2,1)S(1)} %copy-done.3), custom_call_target="tpu_custom_call" | custom-call | flops 500000000 | bytes 2097152 | tf_op jit(solution)/shard_map/pallas_call | solution.py:240
  71.5 0.0 all-to-all-done.2
  71.5 0.6 shard_map.60
  72.1 0.0 collective-permute-done.2
  72.1 0.0 collective-permute-done.1
  72.1 1.1 collective-permute-done
  73.2 1.0 pad_maximum_fusion.refs_0_
  74.2 4.0 %collective-permute-start.5 = (bf16[4,4,16,1024]{3,2,1,0:T(8,128)(2,1)S(1)}, bf16[4,4,16,1024]{3,2,1,0:T(8,128)(2,1)S(1)}, u32[]{:S(2)}, u32[]{:S(2)}) collective-permute-start(bf16[4,4,16,1024]{3,2,1,0:T(8,128)(2,1)S(1)} %pad_maximum_fusion.refs_0_), channel_id=1, source_target_pairs={{0,16},{4,68},{8,24},{12,76},{16,0},{20,84},{24,8},{28,92},{32,48}... | collective-permute-start | bytes 1572872 | tf_op jit(solution)/shard_map/ppermute | solution.py:220
  78.2 1.9 %collective-permute-start.4 = (bf16[4,4,16,1024]{3,2,1,0:T(8,128)(2,1)S(1)}, bf16[4,4,16,1024]{3,2,1,0:T(8,128)(2,1)S(1)}, u32[]{:S(2)}, u32[]{:S(2)}) collective-permute-start(bf16[4,4,16,1024]{3,2,1,0:T(8,128)(2,1)S(1)} %pad_maximum_fusion.refs_0_), channel_id=1, source_target_pairs={{0,24},{4,484},{8,0},{12,492},{16,8},{20,500},{24,16},{28,508},{32... | collective-permute-start | bytes 1572872 | tf_op jit(solution)/shard_map/ppermute | solution.py:220
  80.1 3.4 %collective-permute-start.3 = (bf16[4,4,16,1024]{3,2,1,0:T(8,128)(2,1)S(1)}, bf16[4,4,16,1024]{3,2,1,0:T(8,128)(2,1)S(1)}, u32[]{:S(2)}, u32[]{:S(2)}) collective-permute-start(bf16[4,4,16,1024]{3,2,1,0:T(8,128)(2,1)S(1)} %pad_maximum_fusion.refs_0_), channel_id=1, source_target_pairs={{0,8},{4,36},{8,16},{12,44},{16,24},{20,52},{24,0},{28,60},{32,40}... | collective-permute-start | bytes 1572872 | tf_op jit(solution)/shard_map/ppermute | solution.py:220
  83.5 3.0 %collective-permute-done.5.refs_3_ = bf16[4,4,16,1024]{3,2,1,0:T(8,128)(2,1)S(1)} collective-permute-done((bf16[4,4,16,1024]{3,2,1,0:T(8,128)(2,1)S(1)}, bf16[4,4,16,1024]{3,2,1,0:T(8,128)(2,1)S(1)}, u32[]{:S(2)}, u32[]{:S(2)}) %collective-permute-start.5) | collective-permute-done | bytes 524320 | tf_op jit(solution)/shard_map/ppermute | solution.py:220
  86.5 4.5 %collective-permute-done.4.refs_2_ = bf16[4,4,16,1024]{3,2,1,0:T(8,128)(2,1)S(1)} collective-permute-done((bf16[4,4,16,1024]{3,2,1,0:T(8,128)(2,1)S(1)}, bf16[4,4,16,1024]{3,2,1,0:T(8,128)(2,1)S(1)}, u32[]{:S(2)}, u32[]{:S(2)}) %collective-permute-start.4) | collective-permute-done | bytes 524320 | tf_op jit(solution)/shard_map/ppermute | solution.py:220
  91.1 1.1 collective-permute-done.3.refs_1_
  92.2 1.0 shard_map.61
  93.2 4.6 %collective-permute-start.6 = (bf16[4,4,4,16,1024]{4,3,2,1,0:T(8,128)(2,1)S(1)}, bf16[4,4,4,16,1024]{4,3,2,1,0:T(8,128)(2,1)S(1)}, u32[]{:S(2)}, u32[]{:S(2)}) collective-permute-start(bf16[4,4,4,16,1024]{4,3,2,1,0:T(8,128)(2,1)S(1)} %shard_map.61), channel_id=1, source_target_pairs={{0,4},{4,0},{1,5},{5,1},{2,6},{6,2},{3,7},{7,3},{8,12},{12,8},{9,1... | collective-permute-start | bytes 6291464 | tf_op jit(solution)/shard_map/ppermute | solution.py:276
  97.7 30.5 %all_to_all.22.h_hbm = bf16[4,528,512]{2,1,0:T(8,128)(2,1)} all-to-all(bf16[4,528,512]{2,1,0:T(8,128)(2,1)S(1)} %shard_map.60), channel_id=1, replica_groups=mesh['zh'=4,'zl'=4,'y'=4,'c'=2,'x'=4] {'x'}, dimensions={0} | all-to-all | bytes 4325376 | tf_op jit(solution)/shard_map/all_to_all | solution.py:203
  128.2 0.0 collective-permute-done.6
  128.2 1.3 %copy-done.6 = bf16[4,4,4,16,1024]{4,3,2,1,0:T(8,128)(2,1)} copy-done((bf16[4,4,4,16,1024]{4,3,2,1,0:T(8,128)(2,1)}, bf16[4,4,4,16,1024]{4,3,2,1,0:T(8,128)(2,1)S(1)}, u32[]{:S(2)}) %copy-start.6) | copy-done | bytes 2097176
  129.5 4.8 %shard_map.62 = bf16[512,1024]{1,0:T(8,128)(2,1)} custom-call(bf16[4,528,512]{2,1,0:T(8,128)(2,1)} %all_to_all.22.h_hbm, bf16[64,16,1024]{2,1,0:T(8,128)(2,1)} %bitcast.8, bf16[64,16,1024]{2,1,0:T(8,128)(2,1)} %bitcast.11), custom_call_target="tpu_custom_call" | custom-call | flops 2000000000 | bytes 8388608 | tf_op jit(solution)/shard_map/pallas_call | solution.py:279
  (10 shorter events, 0.1 us)
Async XLA Ops:
  0.0 68.9 %copy-start.2 = (bf16[512,512]{1,0:T(8,128)(2,1)S(1)}, bf16[512,512]{1,0:T(8,128)(2,1)}, u32[]{:S(2)}) copy-start(bf16[512,512]{1,0:T(8,128)(2,1)} %k_ref.1) | copy-start | bytes 1572868
  0.0 68.6 %copy-start.4 = (bf16[512,512]{1,0:T(8,128)(2,1)S(1)}, bf16[512,512]{1,0:T(8,128)(2,1)}, u32[]{:S(2)}) copy-start(bf16[512,512]{1,0:T(8,128)(2,1)} %g_ref.1) | copy-start | bytes 1572868
  0.0 68.9 %copy-start.1 = (bf16[512,512]{1,0:T(8,128)(2,1)S(1)}, bf16[512,512]{1,0:T(8,128)(2,1)}, u32[]{:S(2)}) copy-start(bf16[512,512]{1,0:T(8,128)(2,1)} %q_ref.3) | copy-start | bytes 1572868
  24.0 0.8 copy-start.5
  49.7 21.8 %all-to-all-start.2 = ((bf16[32,16,128]{2,1,0:T(8,128)(2,1)}), bf16[32,16,128]{2,1,0:T(8,128)(2,1)S(1)}, u32[]{:S(2)}, u32[]{:S(2)}) async-start(bf16[32,16,128]{2,1,0:T(8,128)(2,1)} %get-tuple-element.19), calls=%async_computation.2 | async-start | bytes 262144 | tf_op jit(solution)/shard_map/all_to_all | solution.py:203
  58.6 13.5 %collective-permute-start.2 = (bf16[4,16,1024]{2,1,0:T(8,128)(2,1)S(1)}, bf16[4,16,1024]{2,1,0:T(8,128)(2,1)S(1)}, u32[]{:S(2)}, u32[]{:S(2)}) collective-permute-start(bf16[4,16,1024]{2,1,0:T(8,128)(2,1)S(1)} %get-tuple-element.21), channel_id=1, source_target_pairs={{0,64},{4,20},{8,72},{12,28},{16,80},{20,4},{24,88},{28,12},{32,48... | collective-permute-start | bytes 393224 | tf_op jit(solution)/shard_map/ppermute | solution.py:220
  63.3 8.8 %collective-permute-start.1 = (bf16[4,16,1024]{2,1,0:T(8,128)(2,1)S(1)}, bf16[4,16,1024]{2,1,0:T(8,128)(2,1)}, u32[]{:S(2)}, u32[]{:S(2)}) collective-permute-start(bf16[4,16,1024]{2,1,0:T(8,128)(2,1)S(1)} %get-tuple-element.21), channel_id=1, source_target_pairs={{0,480},{4,28},{8,488},{12,4},{16,496},{20,12},{24,504},{28,20},{3... | collective-permute-start | bytes 393224 | tf_op jit(solution)/shard_map/ppermute | solution.py:220
  66.1 7.0 %collective-permute-start = (bf16[4,16,1024]{2,1,0:T(8,128)(2,1)S(1)}, bf16[4,16,1024]{2,1,0:T(8,128)(2,1)}, u32[]{:S(2)}, u32[]{:S(2)}) collective-permute-start(bf16[4,16,1024]{2,1,0:T(8,128)(2,1)S(1)} %get-tuple-element.21), channel_id=1, source_target_pairs={{0,32},{4,12},{8,40},{12,20},{16,48},{20,28},{24,56},{28,4},{32,64... | collective-permute-start | bytes 393224 | tf_op jit(solution)/shard_map/ppermute | solution.py:220
  69.0 1.0 copy-start.3
  74.2 12.3 %collective-permute-start.5 = (bf16[4,4,16,1024]{3,2,1,0:T(8,128)(2,1)S(1)}, bf16[4,4,16,1024]{3,2,1,0:T(8,128)(2,1)S(1)}, u32[]{:S(2)}, u32[]{:S(2)}) collective-permute-start(bf16[4,4,16,1024]{3,2,1,0:T(8,128)(2,1)S(1)} %pad_maximum_fusion.refs_0_), channel_id=1, source_target_pairs={{0,16},{4,68},{8,24},{12,76},{16,0},{20,84},{24,8},{28,92},{32,48}... | collective-permute-start | bytes 1572872 | tf_op jit(solution)/shard_map/ppermute | solution.py:220
  78.2 12.9 %collective-permute-start.4 = (bf16[4,4,16,1024]{3,2,1,0:T(8,128)(2,1)S(1)}, bf16[4,4,16,1024]{3,2,1,0:T(8,128)(2,1)S(1)}, u32[]{:S(2)}, u32[]{:S(2)}) collective-permute-start(bf16[4,4,16,1024]{3,2,1,0:T(8,128)(2,1)S(1)} %pad_maximum_fusion.refs_0_), channel_id=1, source_target_pairs={{0,24},{4,484},{8,0},{12,492},{16,8},{20,500},{24,16},{28,508},{32... | collective-permute-start | bytes 1572872 | tf_op jit(solution)/shard_map/ppermute | solution.py:220
  80.1 12.0 %collective-permute-start.3 = (bf16[4,4,16,1024]{3,2,1,0:T(8,128)(2,1)S(1)}, bf16[4,4,16,1024]{3,2,1,0:T(8,128)(2,1)S(1)}, u32[]{:S(2)}, u32[]{:S(2)}) collective-permute-start(bf16[4,4,16,1024]{3,2,1,0:T(8,128)(2,1)S(1)} %pad_maximum_fusion.refs_0_), channel_id=1, source_target_pairs={{0,8},{4,36},{8,16},{12,44},{16,24},{20,52},{24,0},{28,60},{32,40}... | collective-permute-start | bytes 1572872 | tf_op jit(solution)/shard_map/ppermute | solution.py:220
  93.1 36.4 %copy-start = (bf16[4,4,4,16,1024]{4,3,2,1,0:T(8,128)(2,1)}, bf16[4,4,4,16,1024]{4,3,2,1,0:T(8,128)(2,1)S(1)}, u32[]{:S(2)}) copy-start(bf16[4,4,4,16,1024]{4,3,2,1,0:T(8,128)(2,1)S(1)} %shard_map.61) | copy-start | bytes 6291460
  93.2 35.0 %collective-permute-start.6 = (bf16[4,4,4,16,1024]{4,3,2,1,0:T(8,128)(2,1)S(1)}, bf16[4,4,4,16,1024]{4,3,2,1,0:T(8,128)(2,1)S(1)}, u32[]{:S(2)}, u32[]{:S(2)}) collective-permute-start(bf16[4,4,4,16,1024]{4,3,2,1,0:T(8,128)(2,1)S(1)} %shard_map.61), channel_id=1, source_target_pairs={{0,4},{4,0},{1,5},{5,1},{2,6},{6,2},{3,7},{7,3},{8,12},{12,8},{9,1... | collective-permute-start | bytes 6291464 | tf_op jit(solution)/shard_map/ppermute | solution.py:276
  128.2 1.3 %copy-start.6 = (bf16[4,4,4,16,1024]{4,3,2,1,0:T(8,128)(2,1)}, bf16[4,4,4,16,1024]{4,3,2,1,0:T(8,128)(2,1)S(1)}, u32[]{:S(2)}) copy-start(bf16[4,4,4,16,1024]{4,3,2,1,0:T(8,128)(2,1)S(1)} %collective-permute-done.6) | copy-start | bytes 6291460

commit v5 on v4

--- a/solution.py
+++ b/solution.py
@@ -134,8 +134,8 @@
     for n, block in enumerate(blocks):
         for k in range(4):
             outer, inner = NEXT[n], NEXT[k]
-            by_z = jnp.where(core == 0, inner, outer)
-            by_y = jnp.where(core == 0, outer, inner)
+            by_z = jnp.where(core == 1, inner, outer)
+            by_y = jnp.where(core == 1, outer, inner)
             to = w_ref.at[:, lax.rem(zl + by_z, 4), lax.rem(y + by_y, 4)]
             copies.append(pltpu.make_async_copy(block.at[k], to, sem.at[n, k]))
     for copy in copies:
@@ -260,12 +260,12 @@
     features = swap(hidden, (X,))
     first = [w_far]
     for step in STEPS:
-        first.append(moved(w_far, "z", "y", step))
+        first.append(moved(w_far, "y", "z", step))
     *first, _ = lax.optimization_barrier((*first, hidden))
     first = jnp.stack(first)
     mine = [first]
     for step in STEPS:
-        mine.append(moved(first, "y", "z", step))
+        mine.append(moved(first, "z", "y", step))
     half = (far, lax.axis_size(ZL), lax.axis_size(Y), *out_weight.shape)
     weight = call(
         assemble_body, bf16(half), 4, 10**6, 4 * 2**20,

time: 135 us -> 135 us (level)
  no operation moved by 1% of the time
where the time goes in v5:
time: 135 us
  blocking collectives  76.2 us (56%)
  starting transfers between devices  33.7 us (25%)
  Pallas kernels  11.3 us (8%)
  waiting for transfers between devices  9.12 us (7%)
  local copies, waits for them, and re-layouts  3.16 us (2%)
    all_to_all x3, blocking collectives, swap(): return lax.all_to_all(array, axes, 0, 0, tiled=True)  76.2 us
    ppermute x6, starting transfers between devices, moved(): return lax.ppermute(array, SEQ, pairs)  19.3 us
    ppermute x6, waiting for transfers between devices, moved(): return lax.ppermute(array, SEQ, pairs)  9.11 us
    all_to_all x1, starting transfers between devices, swap(): return lax.all_to_all(array, axes, 0, 0, tiled=True)  8.87 us
    ppermute x1, starting transfers between devices, per_device(): other = lax.ppermute(weight, C, ((0, 1), (1, 0)))  5.45 us
    pallas_call x1, Pallas kernels, per_device(): call(project_body, bf16((rows, cols)), 3, 2 * 10 ** 9, 8 * 2 ** 20, in_sp...  4.79 us
    unnamed x14, local copies, waits for them, and re-layouts  3.16 us
  transfers between devices with their start and end apart: 8, of which 4 were waited for; matrix products, arithmetic and copies ran while one was open for 0% of the time, Pallas kernels for 2%

profile of v5, /device:TPU:1, one launch (start us, length us, event | category | flops | bytes accessed | tf_op | source)
XLA Modules:
  0.0 134.6 jit_solution(1318156544624401229)
XLA Ops:
  0.0 2.4 %shard_map.55 = (f32[4,128,128]{2,1,0:T(8,128)}, bf16[16,1024]{1,0:T(8,128)(2,1)}) custom-call(bf16[512,512]{1,0:T(8,128)(2,1)} %k_ref.1, bf16[512,512]{1,0:T(8,128)(2,1)} %v_ref.1, bf16[16,1024]{1,0:T(8,128)(2,1)} %w_hbm.1), custom_call_target="tpu_custom_call" | custom-call | flops 100000000 | bytes 1048576 | tf_op jit(solution)/shard_map/pallas_call | solution.py:234
  2.4 21.5 %all_to_all.20.r_ref = f32[32,16,128]{2,1,0:T(8,128)S(1)} all-to-all(f32[32,16,128]{2,1,0:T(8,128)} %bitcast.12), channel_id=1, replica_groups=mesh['zh'=4,'zl'=4,'y'=4,'c'=2,'x'=4] {'zl','y','c'}, dimensions={0} | all-to-all | bytes 524288 | tf_op jit(solution)/shard_map/all_to_all | solution.py:203
  24.0 0.8 copy-done.5
  24.8 24.2 %all_to_all.21.t_ref = bf16[4,16,1280]{2,1,0:T(8,128)(2,1)S(1)} all-to-all(bf16[4,16,1280]{2,1,0:T(8,128)(2,1)S(1)} %get-tuple-element.18), channel_id=1, replica_groups=mesh['zh'=4,'zl'=4,'y'=4,'c'=2,'x'=4] {'zh'}, dimensions={0} | all-to-all | bytes 327680 | tf_op jit(solution)/shard_map/all_to_all | solution.py:203
  49.0 0.7 shard_map.57
  49.7 8.9 %all-to-all-start.2 = ((bf16[32,16,128]{2,1,0:T(8,128)(2,1)}), bf16[32,16,128]{2,1,0:T(8,128)(2,1)S(1)}, u32[]{:S(2)}, u32[]{:S(2)}) async-start(bf16[32,16,128]{2,1,0:T(8,128)(2,1)} %get-tuple-element.19), calls=%async_computation.2 | async-start | bytes 262144 | tf_op jit(solution)/shard_map/all_to_all | solution.py:203
  58.6 4.2 %collective-permute-start.2 = (bf16[4,16,1024]{2,1,0:T(8,128)(2,1)S(1)}, bf16[4,16,1024]{2,1,0:T(8,128)(2,1)S(1)}, u32[]{:S(2)}, u32[]{:S(2)}) collective-permute-start(bf16[4,16,1024]{2,1,0:T(8,128)(2,1)S(1)} %get-tuple-element.21), channel_id=1, source_target_pairs={{0,16},{4,68},{8,24},{12,76},{16,0},{20,84},{24,8},{28,92},{32,48}... | collective-permute-start | bytes 393224 | tf_op jit(solution)/shard_map/ppermute | solution.py:220
  62.7 1.9 %collective-permute-start.1 = (bf16[4,16,1024]{2,1,0:T(8,128)(2,1)S(1)}, bf16[4,16,1024]{2,1,0:T(8,128)(2,1)}, u32[]{:S(2)}, u32[]{:S(2)}) collective-permute-start(bf16[4,16,1024]{2,1,0:T(8,128)(2,1)S(1)} %get-tuple-element.21), channel_id=1, source_target_pairs={{0,24},{4,484},{8,0},{12,492},{16,8},{20,500},{24,16},{28,508},{32... | collective-permute-start | bytes 393224 | tf_op jit(solution)/shard_map/ppermute | solution.py:220
  64.7 3.4 %collective-permute-start = (bf16[4,16,1024]{2,1,0:T(8,128)(2,1)S(1)}, bf16[4,16,1024]{2,1,0:T(8,128)(2,1)}, u32[]{:S(2)}, u32[]{:S(2)}) collective-permute-start(bf16[4,16,1024]{2,1,0:T(8,128)(2,1)S(1)} %get-tuple-element.21), channel_id=1, source_target_pairs={{0,8},{4,36},{8,16},{12,44},{16,24},{20,52},{24,0},{28,60},{32,40}... | collective-permute-start | bytes 393224 | tf_op jit(solution)/shard_map/ppermute | solution.py:220
  68.0 0.0 copy-done.4
  68.0 0.3 shard_map.59.g_ref
  68.4 0.0 copy-start.3
  68.4 1.0 copy-done.3
  69.4 1.4 %shard_map.58.l_ref = f32[512,512]{1,0:T(8,128)S(1)} custom-call(bf16[512,512]{1,0:T(8,128)(2,1)S(1)} %copy-done.1, bf16[512,512]{1,0:T(8,128)(2,1)S(1)} %copy-done.2, bf16[512,512]{1,0:T(8,128)(2,1)S(1)} %copy-done.3), custom_call_target="tpu_custom_call" | custom-call | flops 500000000 | bytes 2097152 | tf_op jit(solution)/shard_map/pallas_call | solution.py:240
  70.9 0.0 all-to-all-done.2
  70.9 0.6 shard_map.60
  71.5 0.0 collective-permute-done.2
  71.5 0.0 collective-permute-done.1
  71.5 0.2 collective-permute-done
  71.7 1.0 pad_maximum_fusion.refs_0_
  72.7 4.6 %collective-permute-start.5 = (bf16[4,4,16,1024]{3,2,1,0:T(8,128)(2,1)S(1)}, bf16[4,4,16,1024]{3,2,1,0:T(8,128)(2,1)S(1)}, u32[]{:S(2)}, u32[]{:S(2)}) collective-permute-start(bf16[4,4,16,1024]{3,2,1,0:T(8,128)(2,1)S(1)} %pad_maximum_fusion.refs_0_), channel_id=1, source_target_pairs={{0,64},{4,20},{8,72},{12,28},{16,80},{20,4},{24,88},{28,12},{32,48... | collective-permute-start | bytes 1572872 | tf_op jit(solution)/shard_map/ppermute | solution.py:220
  77.3 2.8 %collective-permute-start.4 = (bf16[4,4,16,1024]{3,2,1,0:T(8,128)(2,1)S(1)}, bf16[4,4,16,1024]{3,2,1,0:T(8,128)(2,1)S(1)}, u32[]{:S(2)}, u32[]{:S(2)}) collective-permute-start(bf16[4,4,16,1024]{3,2,1,0:T(8,128)(2,1)S(1)} %pad_maximum_fusion.refs_0_), channel_id=1, source_target_pairs={{0,480},{4,28},{8,488},{12,4},{16,496},{20,12},{24,504},{28,20},{3... | collective-permute-start | bytes 1572872 | tf_op jit(solution)/shard_map/ppermute | solution.py:220
  80.1 2.5 %collective-permute-start.3 = (bf16[4,4,16,1024]{3,2,1,0:T(8,128)(2,1)S(1)}, bf16[4,4,16,1024]{3,2,1,0:T(8,128)(2,1)S(1)}, u32[]{:S(2)}, u32[]{:S(2)}) collective-permute-start(bf16[4,4,16,1024]{3,2,1,0:T(8,128)(2,1)S(1)} %pad_maximum_fusion.refs_0_), channel_id=1, source_target_pairs={{0,32},{4,12},{8,40},{12,20},{16,48},{20,28},{24,56},{28,4},{32,64... | collective-permute-start | bytes 1572872 | tf_op jit(solution)/shard_map/ppermute | solution.py:220
  82.6 1.8 %collective-permute-done.5.refs_3_ = bf16[4,4,16,1024]{3,2,1,0:T(8,128)(2,1)S(1)} collective-permute-done((bf16[4,4,16,1024]{3,2,1,0:T(8,128)(2,1)S(1)}, bf16[4,4,16,1024]{3,2,1,0:T(8,128)(2,1)S(1)}, u32[]{:S(2)}, u32[]{:S(2)}) %collective-permute-start.5) | collective-permute-done | bytes 524320 | tf_op jit(solution)/shard_map/ppermute | solution.py:220
  84.5 5.7 %collective-permute-done.4.refs_2_ = bf16[4,4,16,1024]{3,2,1,0:T(8,128)(2,1)S(1)} collective-permute-done((bf16[4,4,16,1024]{3,2,1,0:T(8,128)(2,1)S(1)}, bf16[4,4,16,1024]{3,2,1,0:T(8,128)(2,1)S(1)}, u32[]{:S(2)}, u32[]{:S(2)}) %collective-permute-start.4) | collective-permute-done | bytes 524320 | tf_op jit(solution)/shard_map/ppermute | solution.py:220
  90.1 1.4 %collective-permute-done.3.refs_1_ = bf16[4,4,16,1024]{3,2,1,0:T(8,128)(2,1)S(1)} collective-permute-done((bf16[4,4,16,1024]{3,2,1,0:T(8,128)(2,1)S(1)}, bf16[4,4,16,1024]{3,2,1,0:T(8,128)(2,1)S(1)}, u32[]{:S(2)}, u32[]{:S(2)}) %collective-permute-start.3) | collective-permute-done | bytes 524320 | tf_op jit(solution)/shard_map/ppermute | solution.py:220
  91.6 1.0 shard_map.61
  92.6 5.4 %collective-permute-start.6 = (bf16[4,4,4,16,1024]{4,3,2,1,0:T(8,128)(2,1)S(1)}, bf16[4,4,4,16,1024]{4,3,2,1,0:T(8,128)(2,1)S(1)}, u32[]{:S(2)}, u32[]{:S(2)}) collective-permute-start(bf16[4,4,4,16,1024]{4,3,2,1,0:T(8,128)(2,1)S(1)} %shard_map.61), channel_id=1, source_target_pairs={{0,4},{4,0},{1,5},{5,1},{2,6},{6,2},{3,7},{7,3},{8,12},{12,8},{9,1... | collective-permute-start | bytes 6291464 | tf_op jit(solution)/shard_map/ppermute | solution.py:276
  98.0 30.5 %all_to_all.22.h_hbm = bf16[4,528,512]{2,1,0:T(8,128)(2,1)} all-to-all(bf16[4,528,512]{2,1,0:T(8,128)(2,1)S(1)} %shard_map.60), channel_id=1, replica_groups=mesh['zh'=4,'zl'=4,'y'=4,'c'=2,'x'=4] {'x'}, dimensions={0} | all-to-all | bytes 4325376 | tf_op jit(solution)/shard_map/all_to_all | solution.py:203
  128.5 0.0 collective-permute-done.6
  128.5 1.3 copy-done.6
  129.8 4.8 %shard_map.62 = bf16[512,1024]{1,0:T(8,128)(2,1)} custom-call(bf16[4,528,512]{2,1,0:T(8,128)(2,1)} %all_to_all.22.h_hbm, bf16[64,16,1024]{2,1,0:T(8,128)(2,1)} %bitcast.8, bf16[64,16,1024]{2,1,0:T(8,128)(2,1)} %bitcast.11), custom_call_target="tpu_custom_call" | custom-call | flops 2000000000 | bytes 8388608 | tf_op jit(solution)/shard_map/pallas_call | solution.py:279
  (10 shorter events, 0.1 us)
Async XLA Ops:
  0.0 68.3 %copy-start.2 = (bf16[512,512]{1,0:T(8,128)(2,1)S(1)}, bf16[512,512]{1,0:T(8,128)(2,1)}, u32[]{:S(2)}) copy-start(bf16[512,512]{1,0:T(8,128)(2,1)} %k_ref.1) | copy-start | bytes 1572868
  0.0 68.0 %copy-start.4 = (bf16[512,512]{1,0:T(8,128)(2,1)S(1)}, bf16[512,512]{1,0:T(8,128)(2,1)}, u32[]{:S(2)}) copy-start(bf16[512,512]{1,0:T(8,128)(2,1)} %g_ref.1) | copy-start | bytes 1572868
  0.0 68.3 %copy-start.1 = (bf16[512,512]{1,0:T(8,128)(2,1)S(1)}, bf16[512,512]{1,0:T(8,128)(2,1)}, u32[]{:S(2)}) copy-start(bf16[512,512]{1,0:T(8,128)(2,1)} %q_ref.3) | copy-start | bytes 1572868
  24.0 0.8 copy-start.5
  49.7 21.2 %all-to-all-start.2 = ((bf16[32,16,128]{2,1,0:T(8,128)(2,1)}), bf16[32,16,128]{2,1,0:T(8,128)(2,1)S(1)}, u32[]{:S(2)}, u32[]{:S(2)}) async-start(bf16[32,16,128]{2,1,0:T(8,128)(2,1)} %get-tuple-element.19), calls=%async_computation.2 | async-start | bytes 262144 | tf_op jit(solution)/shard_map/all_to_all | solution.py:203
  58.6 12.9 %collective-permute-start.2 = (bf16[4,16,1024]{2,1,0:T(8,128)(2,1)S(1)}, bf16[4,16,1024]{2,1,0:T(8,128)(2,1)S(1)}, u32[]{:S(2)}, u32[]{:S(2)}) collective-permute-start(bf16[4,16,1024]{2,1,0:T(8,128)(2,1)S(1)} %get-tuple-element.21), channel_id=1, source_target_pairs={{0,16},{4,68},{8,24},{12,76},{16,0},{20,84},{24,8},{28,92},{32,48}... | collective-permute-start | bytes 393224 | tf_op jit(solution)/shard_map/ppermute | solution.py:220
  62.7 8.8 %collective-permute-start.1 = (bf16[4,16,1024]{2,1,0:T(8,128)(2,1)S(1)}, bf16[4,16,1024]{2,1,0:T(8,128)(2,1)}, u32[]{:S(2)}, u32[]{:S(2)}) collective-permute-start(bf16[4,16,1024]{2,1,0:T(8,128)(2,1)S(1)} %get-tuple-element.21), channel_id=1, source_target_pairs={{0,24},{4,484},{8,0},{12,492},{16,8},{20,500},{24,16},{28,508},{32... | collective-permute-start | bytes 393224 | tf_op jit(solution)/shard_map/ppermute | solution.py:220
  64.7 7.0 %collective-permute-start = (bf16[4,16,1024]{2,1,0:T(8,128)(2,1)S(1)}, bf16[4,16,1024]{2,1,0:T(8,128)(2,1)}, u32[]{:S(2)}, u32[]{:S(2)}) collective-permute-start(bf16[4,16,1024]{2,1,0:T(8,128)(2,1)S(1)} %get-tuple-element.21), channel_id=1, source_target_pairs={{0,8},{4,36},{8,16},{12,44},{16,24},{20,52},{24,0},{28,60},{32,40}... | collective-permute-start | bytes 393224 | tf_op jit(solution)/shard_map/ppermute | solution.py:220
  68.4 1.0 copy-start.3
  72.7 11.7 %collective-permute-start.5 = (bf16[4,4,16,1024]{3,2,1,0:T(8,128)(2,1)S(1)}, bf16[4,4,16,1024]{3,2,1,0:T(8,128)(2,1)S(1)}, u32[]{:S(2)}, u32[]{:S(2)}) collective-permute-start(bf16[4,4,16,1024]{3,2,1,0:T(8,128)(2,1)S(1)} %pad_maximum_fusion.refs_0_), channel_id=1, source_target_pairs={{0,64},{4,20},{8,72},{12,28},{16,80},{20,4},{24,88},{28,12},{32,48... | collective-permute-start | bytes 1572872 | tf_op jit(solution)/shard_map/ppermute | solution.py:220
  77.3 12.8 %collective-permute-start.4 = (bf16[4,4,16,1024]{3,2,1,0:T(8,128)(2,1)S(1)}, bf16[4,4,16,1024]{3,2,1,0:T(8,128)(2,1)S(1)}, u32[]{:S(2)}, u32[]{:S(2)}) collective-permute-start(bf16[4,4,16,1024]{3,2,1,0:T(8,128)(2,1)S(1)} %pad_maximum_fusion.refs_0_), channel_id=1, source_target_pairs={{0,480},{4,28},{8,488},{12,4},{16,496},{20,12},{24,504},{28,20},{3... | collective-permute-start | bytes 1572872 | tf_op jit(solution)/shard_map/ppermute | solution.py:220
  80.1 11.4 %collective-permute-start.3 = (bf16[4,4,16,1024]{3,2,1,0:T(8,128)(2,1)S(1)}, bf16[4,4,16,1024]{3,2,1,0:T(8,128)(2,1)S(1)}, u32[]{:S(2)}, u32[]{:S(2)}) collective-permute-start(bf16[4,4,16,1024]{3,2,1,0:T(8,128)(2,1)S(1)} %pad_maximum_fusion.refs_0_), channel_id=1, source_target_pairs={{0,32},{4,12},{8,40},{12,20},{16,48},{20,28},{24,56},{28,4},{32,64... | collective-permute-start | bytes 1572872 | tf_op jit(solution)/shard_map/ppermute | solution.py:220
  92.6 37.3 %copy-start = (bf16[4,4,4,16,1024]{4,3,2,1,0:T(8,128)(2,1)}, bf16[4,4,4,16,1024]{4,3,2,1,0:T(8,128)(2,1)S(1)}, u32[]{:S(2)}) copy-start(bf16[4,4,4,16,1024]{4,3,2,1,0:T(8,128)(2,1)S(1)} %shard_map.61) | copy-start | bytes 6291460
  92.6 35.9 %collective-permute-start.6 = (bf16[4,4,4,16,1024]{4,3,2,1,0:T(8,128)(2,1)S(1)}, bf16[4,4,4,16,1024]{4,3,2,1,0:T(8,128)(2,1)S(1)}, u32[]{:S(2)}, u32[]{:S(2)}) collective-permute-start(bf16[4,4,4,16,1024]{4,3,2,1,0:T(8,128)(2,1)S(1)} %shard_map.61), channel_id=1, source_target_pairs={{0,4},{4,0},{1,5},{5,1},{2,6},{6,2},{3,7},{7,3},{8,12},{12,8},{9,1... | collective-permute-start | bytes 6291464 | tf_op jit(solution)/shard_map/ppermute | solution.py:276
  128.5 1.3 copy-start.6

commit v6 on v5

--- a/solution.py
+++ b/solution.py
@@ -14,6 +14,7 @@
 SEQ = (ZH, ZL, Y, C)
 NEAR = (ZL, Y, C)
 STEPS = (1, -1, 2)
+PLACES = ((0, 3), (1, 2))
 NEXT = (0, 3, 1, 2)
 
 
@@ -102,41 +103,48 @@
         p_ref[j] = (e_ref[j] + base).astype(BF16)
 
 
-def hidden_body(q_ref, p_ref, l_ref, g_ref, o_ref):
+def hidden_body(q_ref, p_ref, l_ref, g_ref, out_ref, o_ref, sem):
     rows, width = q_ref.shape
     scale = HD ** (-0.5)
-    squares = jnp.zeros((rows, HD), F32)
-    for h in range(width // HD):
-        cols = slice(h * HD, (h + 1) * HD)
-        inter = jnp.dot(q_ref[:, cols], p_ref[h], preferred_element_type=F32)
-        attn = l_ref[:, cols] + inter * scale
-        squares = squares + attn * attn
-        hid = (attn * g_ref[:, cols]).astype(BF16)
-        for j in range(o_ref.shape[0]):
-            o_ref[j, :rows, cols] = hid
-    row = jnp.sum(squares.T, axis=0, keepdims=True)
-    hi = row.astype(BF16).astype(F32)
-    mid = (row - hi).astype(BF16).astype(F32)
-    lo = row - hi - mid
-    place = lax.broadcasted_iota(jnp.int32, (16, rows), 0)
-    extra = jnp.where(place == 0, hi, jnp.where(place == 1, mid, jnp.where(place == 2, lo, 0.0)))
-    for j in range(o_ref.shape[0]):
-        o_ref[j, rows:, :] = extra.astype(BF16)
+    half = rows // 2
+    sums = []
+    copies = []
+    for i in range(2):
+        r = slice(i * half, (i + 1) * half)
+        squares = jnp.zeros((half, HD), F32)
+        for h in range(width // HD):
+            cols = slice(h * HD, (h + 1) * HD)
+            inter = jnp.dot(q_ref[r, cols], p_ref[h], preferred_element_type=F32)
+            attn = l_ref[r, cols] + inter * scale
+            squares = squares + attn * attn
+            o_ref[r, cols] = (attn * g_ref[r, cols]).astype(BF16)
+        sums.append(jnp.sum(squares.T, axis=0, keepdims=True))
+        if i == 1:
+            row = jnp.concatenate(sums, axis=1)
+            hi = row.astype(BF16).astype(F32)
+            mid = (row - hi).astype(BF16).astype(F32)
+            lo = row - hi - mid
+            place = lax.broadcasted_iota(jnp.int32, (16, rows), 0)
+            extra = jnp.where(
+                place == 0, hi, jnp.where(place == 1, mid, jnp.where(place == 2, lo, 0.0))
+            )
+            o_ref[rows:, :] = extra.astype(BF16)
+            r = slice(half, rows + 16)
+        for j in range(out_ref.shape[0]):
+            copies.append(pltpu.make_async_copy(o_ref.at[r], out_ref.at[j, r], sem.at[i, j]))
+            copies[-1].start()
+    for copy in copies:
+        copy.wait()
 
 
 def assemble_body(*refs):
-    blocks = refs[:4]
-    w_ref, sem = refs[4:]
-    core = lax.axis_index(C)
-    zl = lax.axis_index(ZL)
-    y = lax.axis_index(Y)
+    blocks = refs[:2]
+    w_ref, sem = refs[2:]
+    mine = jnp.where(lax.axis_index(C) == 1, lax.axis_index(ZL), lax.axis_index(Y))
     copies = []
     for n, block in enumerate(blocks):
         for k in range(4):
-            outer, inner = NEXT[n], NEXT[k]
-            by_z = jnp.where(core == 1, inner, outer)
-            by_y = jnp.where(core == 1, outer, inner)
-            to = w_ref.at[:, lax.rem(zl + by_z, 4), lax.rem(y + by_y, 4)]
+            to = w_ref.at[n, :, lax.rem(mine + NEXT[k], 4)]
             copies.append(pltpu.make_async_copy(block.at[k], to, sem.at[n, k]))
     for copy in copies:
         copy.start()
@@ -144,28 +152,49 @@
         copy.wait()
 
 
-def project_body(h_hbm, mine_ref, other_ref, out_ref, h_ref, w_ref, acc_ref, o_ref, sem, out_sem):
+def project_body(h_hbm, *refs):
+    pieces = refs[:4]
+    out_ref, h_ref, w_ref, acc_ref, o_ref, sem, out_sem = refs[4:]
     rows, width = o_ref.shape
     parts = h_ref.shape[0]
     each = h_ref.shape[2]
     core = lax.axis_index(C)
-    span = w_ref.shape[0] // parts
+    zl = lax.axis_index(ZL)
+    y = lax.axis_index(Y)
     tile = 256
     copies = []
     for s in range(parts):
-        part = slice(s * span, (s + 1) * span)
-        copies.append(
-            [
-                pltpu.make_async_copy(h_hbm.at[s], h_ref.at[s], sem.at[s, 0]),
-                pltpu.make_async_copy(mine_ref.at[part], w_ref.at[part, core], sem.at[s, 1]),
-                pltpu.make_async_copy(other_ref.at[part], w_ref.at[part, 1 - core], sem.at[s, 2]),
-            ]
-        )
-        for copy in copies[s]:
-            copy.start()
+        copies.append([pltpu.make_async_copy(h_hbm.at[s], h_ref.at[s], sem.at[s, 16])])
+        copies[s][0].start()
+        for p, piece in enumerate(pieces):
+            owner = core if p < 2 else 1 - core
+            for n in range(2):
+                step = NEXT[PLACES[p % 2][n]]
+                down = w_ref.at[s, :, lax.rem(y + step, 4), owner]
+                along = w_ref.at[s, lax.rem(zl + step, 4), :, owner]
+                by_y = pltpu.make_async_copy(piece.at[n, s], down, sem.at[s, 2 * p + n])
+                by_z = pltpu.make_async_copy(piece.at[n, s], along, sem.at[s, 8 + 2 * p + n])
+                copies[s].append((owner, by_y, by_z))
+
+                @pl.when(owner == 1)
+                def _():
+                    by_y.start()
+
+                @pl.when(owner == 0)
+                def _():
+                    by_z.start()
+
     for s in range(parts):
-        for copy in copies[s]:
-            copy.wait()
+        copies[s][0].wait()
+        for owner, by_y, by_z in copies[s][1:]:
+            @pl.when(owner == 1)
+            def _():
+                by_y.wait()
+
+            @pl.when(owner == 0)
+            def _():
+                by_z.wait()
+
         last = s == parts - 1
         if last:
             row = jnp.zeros((1, rows), F32)
@@ -179,7 +208,7 @@
             r = slice(i * block, (i + 1) * block)
             for n in range(width // tile):
                 c = slice(n * tile, (n + 1) * tile)
-                w = w_ref[s * span : (s + 1) * span, :, :, c].reshape(each, tile)
+                w = w_ref[s, :, :, :, :, c].reshape(each, tile)
                 acc = jnp.dot(h_ref[s, r, :], w, preferred_element_type=F32)
                 if s > 0:
                     acc = acc + acc_ref[r, c]
@@ -255,7 +284,12 @@
     )(earlier, totals)
     prefix = swap(prefix, NEAR).reshape(heads, HD, HD)
     hidden = call(
-        hidden_body, bf16((group, rows + 16, width)), 4, 10**8, 2**22
+        hidden_body, bf16((group, rows + 16, width)), 4, 10**8, 2**22,
+        out_spec=ANY,
+        scratch=[
+            pltpu.VMEM((rows + 16, width), BF16),
+            pltpu.SemaphoreType.DMA((2, group)),
+        ],
     )(queries, prefix, local, gate)
     features = swap(hidden, (X,))
     first = [w_far]
@@ -266,30 +300,33 @@
     mine = [first]
     for step in STEPS:
         mine.append(moved(first, "z", "y", step))
-    half = (far, lax.axis_size(ZL), lax.axis_size(Y), *out_weight.shape)
-    weight = call(
-        assemble_body, bf16(half), 4, 10**6, 4 * 2**20,
-        in_specs=[ANY] * 4,
-        out_spec=ANY,
-        scratch=[pltpu.SemaphoreType.DMA((4, 4))],
-    )(*mine)
-    other = lax.ppermute(weight, C, ((0, 1), (1, 0)))
-    flat = (-1, *out_weight.shape)
-    count = half[0] * half[1] * half[2]
+    halves = []
+    for places in PLACES:
+        halves.append(
+            call(
+                assemble_body, bf16((2, far, 4, *out_weight.shape)),
+                2, 10**6, 2 * 2**20,
+                in_specs=[ANY] * 2,
+                out_spec=ANY,
+                scratch=[pltpu.SemaphoreType.DMA((2, 4))],
+            )(*[mine[k] for k in places])
+        )
+    for n in range(2):
+        halves.append(lax.ppermute(halves[n], C, ((0, 1), (1, 0))))
     return call(
-        project_body, bf16((rows, cols)), 3, 2 * 10**9, 8 * 2**20,
-        in_specs=[ANY] * 3,
+        project_body, bf16((rows, cols)), 5, 2 * 10**9, 8 * 2**20,
+        in_specs=[ANY] * 5,
         out_spec=ANY,
         scratch=[
             pltpu.VMEM((group, rows + 16, width), BF16),
-            pltpu.VMEM((count, 2, *out_weight.shape), BF16),
+            pltpu.VMEM((far, 4, 4, 2, *out_weight.shape), BF16),
             pltpu.VMEM((rows, cols), F32),
             pltpu.VMEM((rows, cols), BF16),
-            pltpu.SemaphoreType.DMA((group, 3)),
+            pltpu.SemaphoreType.DMA((group, 17)),
             pltpu.SemaphoreType.DMA((2,)),
         ],
         grant=60,
-    )(features, weight.reshape(flat), other.reshape(flat))
+    )(features, *halves)
 
 
 def solution(mesh):

time: 135 us -> 110 us (0.81)
  the two profiles are of different devices: /device:TPU:1 before, /device:TPU:17 now
where the time goes in v6:
time: 110 us; the launch traced here: 109 us
  blocking collectives  42.6 us (39%)
  starting transfers between devices  38.2 us (35%)
  Pallas kernels  12.6 us (11%)
  waiting for transfers between devices  12.2 us (11%)
  local copies, waits for them, and re-layouts  1.82 us (2%)
    all_to_all x2, blocking collectives, swap(): return lax.all_to_all(array, axes, 0, 0, tiled=True)  42.6 us
    ppermute x6, starting transfers between devices, moved(): return lax.ppermute(array, SEQ, pairs)  17.1 us
    all_to_all x2, starting transfers between devices, swap(): return lax.all_to_all(array, axes, 0, 0, tiled=True)  15.6 us
    ppermute x6, waiting for transfers between devices, moved(): return lax.ppermute(array, SEQ, pairs)  6.42 us
    ppermute x2, starting transfers between devices, per_device(): halves.append(lax.ppermute(halves[n], C, ((0, 1), (1, 0))))  5.48 us
    pallas_call x1, Pallas kernels, per_device(): call(project_body, bf16((rows, cols)), 5, 2 * 10 ** 9, 8 * 2 ** 20, in_sp...  5.32 us
    all_to_all x2, waiting for transfers between devices, swap(): return lax.all_to_all(array, axes, 0, 0, tiled=True)  3.42 us
    pallas_call x1, Pallas kernels, per_device(): call(state_body, (f32((heads, HD, HD)), bf16(out_weight.shape)), 3, 10 **...  2.4 us
  transfers between devices with their start and end apart: 10, of which 5 were waited for; matrix products, arithmetic and copies ran while one was open for 1% of the time, Pallas kernels for 4%

profile of v6, /device:TPU:17, one launch (start us, length us, event | category | flops | bytes accessed | tf_op | source)
XLA Modules:
  0.0 108.8 jit_solution(9262265347436253551)
XLA Ops:
  0.0 2.4 %shard_map.55 = (f32[4,128,128]{2,1,0:T(8,128)}, bf16[16,1024]{1,0:T(8,128)(2,1)}) custom-call(bf16[512,512]{1,0:T(8,128)(2,1)} %k_ref.1, bf16[512,512]{1,0:T(8,128)(2,1)} %v_ref.1, bf16[16,1024]{1,0:T(8,128)(2,1)} %w_hbm.1), custom_call_target="tpu_custom_call" | custom-call | flops 100000000 | bytes 1048576 | tf_op jit(solution)/shard_map/pallas_call | solution.py:263
  2.4 18.4 %all_to_all.20.r_ref = f32[32,16,128]{2,1,0:T(8,128)S(1)} all-to-all(f32[32,16,128]{2,1,0:T(8,128)} %bitcast.8), channel_id=1, replica_groups=mesh['zh'=4,'zl'=4,'y'=4,'c'=2,'x'=4] {'zl','y','c'}, dimensions={0} | all-to-all | bytes 524288 | tf_op jit(solution)/shard_map/all_to_all | solution.py:232
  20.8 0.8 copy-done.6
  21.6 24.3 %all_to_all.21.t_ref = bf16[4,16,1280]{2,1,0:T(8,128)(2,1)S(1)} all-to-all(bf16[4,16,1280]{2,1,0:T(8,128)(2,1)S(1)} %get-tuple-element.18), channel_id=1, replica_groups=mesh['zh'=4,'zl'=4,'y'=4,'c'=2,'x'=4] {'zh'}, dimensions={0} | all-to-all | bytes 327680 | tf_op jit(solution)/shard_map/all_to_all | solution.py:232
  45.9 0.7 shard_map.57
  46.5 11.1 %all-to-all-start.2 = ((bf16[32,16,128]{2,1,0:T(8,128)(2,1)}), bf16[32,16,128]{2,1,0:T(8,128)(2,1)S(1)}, u32[]{:S(2)}, u32[]{:S(2)}) async-start(bf16[32,16,128]{2,1,0:T(8,128)(2,1)} %get-tuple-element.19), calls=%async_computation.2 | async-start | bytes 262144 | tf_op jit(solution)/shard_map/all_to_all | solution.py:232
  57.7 4.0 %collective-permute-start.2 = (bf16[4,16,1024]{2,1,0:T(8,128)(2,1)S(1)}, bf16[4,16,1024]{2,1,0:T(8,128)(2,1)S(1)}, u32[]{:S(2)}, u32[]{:S(2)}) collective-permute-start(bf16[4,16,1024]{2,1,0:T(8,128)(2,1)S(1)} %get-tuple-element.21), channel_id=1, source_target_pairs={{0,16},{4,68},{8,24},{12,76},{16,0},{20,84},{24,8},{28,92},{32,48}... | collective-permute-start | bytes 393224 | tf_op jit(solution)/shard_map/ppermute | solution.py:249
  61.7 1.9 %collective-permute-start.1 = (bf16[4,16,1024]{2,1,0:T(8,128)(2,1)S(1)}, bf16[4,16,1024]{2,1,0:T(8,128)(2,1)}, u32[]{:S(2)}, u32[]{:S(2)}) collective-permute-start(bf16[4,16,1024]{2,1,0:T(8,128)(2,1)S(1)} %get-tuple-element.21), channel_id=1, source_target_pairs={{0,24},{4,484},{8,0},{12,492},{16,8},{20,500},{24,16},{28,508},{32... | collective-permute-start | bytes 393224 | tf_op jit(solution)/shard_map/ppermute | solution.py:249
  63.6 3.4 %collective-permute-start = (bf16[4,16,1024]{2,1,0:T(8,128)(2,1)S(1)}, bf16[4,16,1024]{2,1,0:T(8,128)(2,1)}, u32[]{:S(2)}, u32[]{:S(2)}) collective-permute-start(bf16[4,16,1024]{2,1,0:T(8,128)(2,1)S(1)} %get-tuple-element.21), channel_id=1, source_target_pairs={{0,8},{4,36},{8,16},{12,44},{16,24},{20,52},{24,0},{28,60},{32,40}... | collective-permute-start | bytes 393224 | tf_op jit(solution)/shard_map/ppermute | solution.py:249
  67.0 0.3 shard_map.59.g_ref
  67.3 0.0 copy-start.4
  67.3 1.0 copy-done.4
  68.4 1.4 %shard_map.58.l_ref = f32[512,512]{1,0:T(8,128)S(1)} custom-call(bf16[512,512]{1,0:T(8,128)(2,1)S(1)} %copy-done.2, bf16[512,512]{1,0:T(8,128)(2,1)S(1)} %copy-done.3, bf16[512,512]{1,0:T(8,128)(2,1)S(1)} %copy-done.4), custom_call_target="tpu_custom_call" | custom-call | flops 500000000 | bytes 2097152 | tf_op jit(solution)/shard_map/pallas_call | solution.py:269
  69.8 0.0 all-to-all-done.2
  69.8 1.6 %shard_map.60 = bf16[4,528,512]{2,1,0:T(8,128)(2,1)} custom-call(bf16[512,512]{1,0:T(8,128)(2,1)S(1)} %copy-done.2, bf16[4,128,128]{2,1,0:T(8,128)(2,1)S(1)} %bitcast.6, f32[512,512]{1,0:T(8,128)S(1)} %shard_map.58.l_ref, f32[512,512]{1,0:T(8,128)S(1)} %shard_map.59.g_ref), custom_call_target="tpu_custom_call" | custom-call | flops 100000000 | bytes 4194304 | tf_op jit(solution)/shard_map/pallas_call | solution.py:286
  71.5 4.5 %all-to-all-start.3 = ((bf16[4,528,512]{2,1,0:T(8,128)(2,1)}), bf16[4,528,512]{2,1,0:T(8,128)(2,1)}, u32[]{:S(2)}, u32[]{:S(2)}) async-start(bf16[4,528,512]{2,1,0:T(8,128)(2,1)} %shard_map.60), calls=%async_computation.3 | async-start | bytes 4325376 | tf_op jit(solution)/shard_map/all_to_all | solution.py:232
  76.0 0.0 collective-permute-done.2
  76.0 0.0 collective-permute-done.1
  76.0 1.0 pad_maximum_fusion.refs_0_
  77.0 2.2 %collective-permute-start.3 = (bf16[4,4,16,1024]{3,2,1,0:T(8,128)(2,1)S(1)}, bf16[4,4,16,1024]{3,2,1,0:T(8,128)(2,1)S(1)}, u32[]{:S(2)}, u32[]{:S(2)}) collective-permute-start(bf16[4,4,16,1024]{3,2,1,0:T(8,128)(2,1)S(1)} %pad_maximum_fusion.refs_0_), channel_id=1, source_target_pairs={{0,64},{4,20},{8,72},{12,28},{16,80},{20,4},{24,88},{28,12},{32,48... | collective-permute-start | bytes 1572872 | tf_op jit(solution)/shard_map/ppermute | solution.py:249
  79.2 3.7 %collective-permute-start.5 = (bf16[4,4,16,1024]{3,2,1,0:T(8,128)(2,1)S(1)}, bf16[4,4,16,1024]{3,2,1,0:T(8,128)(2,1)S(1)}, u32[]{:S(2)}, u32[]{:S(2)}) collective-permute-start(bf16[4,4,16,1024]{3,2,1,0:T(8,128)(2,1)S(1)} %pad_maximum_fusion.refs_0_), channel_id=1, source_target_pairs={{0,480},{4,28},{8,488},{12,4},{16,496},{20,12},{24,504},{28,20},{3... | collective-permute-start | bytes 1572872 | tf_op jit(solution)/shard_map/ppermute | solution.py:249
  83.0 1.9 %collective-permute-start.4 = (bf16[4,4,16,1024]{3,2,1,0:T(8,128)(2,1)S(1)}, bf16[4,4,16,1024]{3,2,1,0:T(8,128)(2,1)S(1)}, u32[]{:S(2)}, u32[]{:S(2)}) collective-permute-start(bf16[4,4,16,1024]{3,2,1,0:T(8,128)(2,1)S(1)} %pad_maximum_fusion.refs_0_), channel_id=1, source_target_pairs={{0,32},{4,12},{8,40},{12,20},{16,48},{20,28},{24,56},{28,4},{32,64... | collective-permute-start | bytes 1572872 | tf_op jit(solution)/shard_map/ppermute | solution.py:249
  84.9 4.0 %collective-permute-done.3.refs_1_ = bf16[4,4,16,1024]{3,2,1,0:T(8,128)(2,1)S(1)} collective-permute-done((bf16[4,4,16,1024]{3,2,1,0:T(8,128)(2,1)S(1)}, bf16[4,4,16,1024]{3,2,1,0:T(8,128)(2,1)S(1)}, u32[]{:S(2)}, u32[]{:S(2)}) %collective-permute-start.3) | collective-permute-done | bytes 524320 | tf_op jit(solution)/shard_map/ppermute | solution.py:249
  88.9 0.4 shard_map.61.refs_0_
  89.3 2.8 %collective-permute-start.6 = (bf16[2,4,4,16,1024]{4,3,2,1,0:T(8,128)(2,1)S(1)}, bf16[2,4,4,16,1024]{4,3,2,1,0:T(8,128)(2,1)S(1)}, u32[]{:S(2)}, u32[]{:S(2)}) collective-permute-start(bf16[2,4,4,16,1024]{4,3,2,1,0:T(8,128)(2,1)S(1)} %shard_map.61.refs_0_), channel_id=1, source_target_pairs={{0,4},{4,0},{1,5},{5,1},{2,6},{6,2},{3,7},{7,3},{8,12},{12,8},{9,1... | collective-permute-start | bytes 3145736 | tf_op jit(solution)/shard_map/ppermute | solution.py:315
  92.1 1.6 %collective-permute-done.5.refs_1_ = bf16[4,4,16,1024]{3,2,1,0:T(8,128)(2,1)S(1)} collective-permute-done((bf16[4,4,16,1024]{3,2,1,0:T(8,128)(2,1)S(1)}, bf16[4,4,16,1024]{3,2,1,0:T(8,128)(2,1)S(1)}, u32[]{:S(2)}, u32[]{:S(2)}) %collective-permute-start.5) | collective-permute-done | bytes 524320 | tf_op jit(solution)/shard_map/ppermute | solution.py:249
  93.6 0.9 collective-permute-done.4.refs_0_
  94.5 0.4 shard_map.62.refs_1_
  94.9 2.7 %collective-permute-start.7 = (bf16[2,4,4,16,1024]{4,3,2,1,0:T(8,128)(2,1)S(1)}, bf16[2,4,4,16,1024]{4,3,2,1,0:T(8,128)(2,1)}, u32[]{:S(2)}, u32[]{:S(2)}) collective-permute-start(bf16[2,4,4,16,1024]{4,3,2,1,0:T(8,128)(2,1)S(1)} %shard_map.62.refs_1_), channel_id=1, source_target_pairs={{0,4},{4,0},{1,5},{5,1},{2,6},{6,2},{3,7},{7,3},{8,12},{12,8},{9,1... | collective-permute-start | bytes 3145736 | tf_op jit(solution)/shard_map/ppermute | solution.py:315
  97.7 2.4 %collective-permute-done.7.refs_3_ = bf16[2,4,4,16,1024]{4,3,2,1,0:T(8,128)(2,1)} collective-permute-done((bf16[2,4,4,16,1024]{4,3,2,1,0:T(8,128)(2,1)S(1)}, bf16[2,4,4,16,1024]{4,3,2,1,0:T(8,128)(2,1)}, u32[]{:S(2)}, u32[]{:S(2)}) %collective-permute-start.7) | collective-permute-done | bytes 1048608 | tf_op jit(solution)/shard_map/ppermute | solution.py:315
  100.0 3.4 %all-to-all-done.3.h_hbm = bf16[4,528,512]{2,1,0:T(8,128)(2,1)} async-done(((bf16[4,528,512]{2,1,0:T(8,128)(2,1)}), bf16[4,528,512]{2,1,0:T(8,128)(2,1)}, u32[]{:S(2)}, u32[]{:S(2)}) %all-to-all-start.3) | async-done | bytes 2162720 | tf_op jit(solution)/shard_map/all_to_all | solution.py:232
  103.5 5.3 %shard_map.63 = bf16[512,1024]{1,0:T(8,128)(2,1)} custom-call(bf16[4,528,512]{2,1,0:T(8,128)(2,1)} %all-to-all-done.3.h_hbm, bf16[2,4,4,16,1024]{4,3,2,1,0:T(8,128)(2,1)} %copy-done, bf16[2,4,4,16,1024]{4,3,2,1,0:T(8,128)(2,1)} %copy-done.1, bf16[2,4,4,16,1024]{4,3,2,1,0:T(8,128)(2,1)} %copy-done.7, bf16[2,4,4,16,1024]{4,3,2,1,0:T(8,128)(2,1)} %collective-permute-done.7.refs_3_), custom_call_target="tpu_custom_call" | custom-call | flops 2000000000 | bytes 8388608 | tf_op jit(solution)/shard_map/pallas_call | solution.py:316
  (16 shorter events, 0.1 us)
Async XLA Ops:
  0.0 67.3 %copy-start.3 = (bf16[512,512]{1,0:T(8,128)(2,1)S(1)}, bf16[512,512]{1,0:T(8,128)(2,1)}, u32[]{:S(2)}) copy-start(bf16[512,512]{1,0:T(8,128)(2,1)} %k_ref.1) | copy-start | bytes 1572868
  0.0 67.0 %copy-start.5 = (bf16[512,512]{1,0:T(8,128)(2,1)S(1)}, bf16[512,512]{1,0:T(8,128)(2,1)}, u32[]{:S(2)}) copy-start(bf16[512,512]{1,0:T(8,128)(2,1)} %g_ref.1) | copy-start | bytes 1572868
  0.0 67.3 %copy-start.2 = (bf16[512,512]{1,0:T(8,128)(2,1)S(1)}, bf16[512,512]{1,0:T(8,128)(2,1)}, u32[]{:S(2)}) copy-start(bf16[512,512]{1,0:T(8,128)(2,1)} %q_ref.3) | copy-start | bytes 1572868
  20.8 0.8 copy-start.6
  46.5 23.3 %all-to-all-start.2 = ((bf16[32,16,128]{2,1,0:T(8,128)(2,1)}), bf16[32,16,128]{2,1,0:T(8,128)(2,1)S(1)}, u32[]{:S(2)}, u32[]{:S(2)}) async-start(bf16[32,16,128]{2,1,0:T(8,128)(2,1)} %get-tuple-element.19), calls=%async_computation.2 | async-start | bytes 262144 | tf_op jit(solution)/shard_map/all_to_all | solution.py:232
  57.7 18.3 %collective-permute-start.2 = (bf16[4,16,1024]{2,1,0:T(8,128)(2,1)S(1)}, bf16[4,16,1024]{2,1,0:T(8,128)(2,1)S(1)}, u32[]{:S(2)}, u32[]{:S(2)}) collective-permute-start(bf16[4,16,1024]{2,1,0:T(8,128)(2,1)S(1)} %get-tuple-element.21), channel_id=1, source_target_pairs={{0,16},{4,68},{8,24},{12,76},{16,0},{20,84},{24,8},{28,92},{32,48}... | collective-permute-start | bytes 393224 | tf_op jit(solution)/shard_map/ppermute | solution.py:249
  61.7 14.3 %collective-permute-start.1 = (bf16[4,16,1024]{2,1,0:T(8,128)(2,1)S(1)}, bf16[4,16,1024]{2,1,0:T(8,128)(2,1)}, u32[]{:S(2)}, u32[]{:S(2)}) collective-permute-start(bf16[4,16,1024]{2,1,0:T(8,128)(2,1)S(1)} %get-tuple-element.21), channel_id=1, source_target_pairs={{0,24},{4,484},{8,0},{12,492},{16,8},{20,500},{24,16},{28,508},{32... | collective-permute-start | bytes 393224 | tf_op jit(solution)/shard_map/ppermute | solution.py:249
  63.6 12.4 %collective-permute-start = (bf16[4,16,1024]{2,1,0:T(8,128)(2,1)S(1)}, bf16[4,16,1024]{2,1,0:T(8,128)(2,1)}, u32[]{:S(2)}, u32[]{:S(2)}) collective-permute-start(bf16[4,16,1024]{2,1,0:T(8,128)(2,1)S(1)} %get-tuple-element.21), channel_id=1, source_target_pairs={{0,8},{4,36},{8,16},{12,44},{16,24},{20,52},{24,0},{28,60},{32,40}... | collective-permute-start | bytes 393224 | tf_op jit(solution)/shard_map/ppermute | solution.py:249
  67.3 1.0 copy-start.4
  71.5 32.0 %all-to-all-start.3 = ((bf16[4,528,512]{2,1,0:T(8,128)(2,1)}), bf16[4,528,512]{2,1,0:T(8,128)(2,1)}, u32[]{:S(2)}, u32[]{:S(2)}) async-start(bf16[4,528,512]{2,1,0:T(8,128)(2,1)} %shard_map.60), calls=%async_computation.3 | async-start | bytes 4325376 | tf_op jit(solution)/shard_map/all_to_all | solution.py:232
  77.0 11.8 %collective-permute-start.3 = (bf16[4,4,16,1024]{3,2,1,0:T(8,128)(2,1)S(1)}, bf16[4,4,16,1024]{3,2,1,0:T(8,128)(2,1)S(1)}, u32[]{:S(2)}, u32[]{:S(2)}) collective-permute-start(bf16[4,4,16,1024]{3,2,1,0:T(8,128)(2,1)S(1)} %pad_maximum_fusion.refs_0_), channel_id=1, source_target_pairs={{0,64},{4,20},{8,72},{12,28},{16,80},{20,4},{24,88},{28,12},{32,48... | collective-permute-start | bytes 1572872 | tf_op jit(solution)/shard_map/ppermute | solution.py:249
  79.2 14.4 %collective-permute-start.5 = (bf16[4,4,16,1024]{3,2,1,0:T(8,128)(2,1)S(1)}, bf16[4,4,16,1024]{3,2,1,0:T(8,128)(2,1)S(1)}, u32[]{:S(2)}, u32[]{:S(2)}) collective-permute-start(bf16[4,4,16,1024]{3,2,1,0:T(8,128)(2,1)S(1)} %pad_maximum_fusion.refs_0_), channel_id=1, source_target_pairs={{0,480},{4,28},{8,488},{12,4},{16,496},{20,12},{24,504},{28,20},{3... | collective-permute-start | bytes 1572872 | tf_op jit(solution)/shard_map/ppermute | solution.py:249
  83.0 11.5 %collective-permute-start.4 = (bf16[4,4,16,1024]{3,2,1,0:T(8,128)(2,1)S(1)}, bf16[4,4,16,1024]{3,2,1,0:T(8,128)(2,1)S(1)}, u32[]{:S(2)}, u32[]{:S(2)}) collective-permute-start(bf16[4,4,16,1024]{3,2,1,0:T(8,128)(2,1)S(1)} %pad_maximum_fusion.refs_0_), channel_id=1, source_target_pairs={{0,32},{4,12},{8,40},{12,20},{16,48},{20,28},{24,56},{28,4},{32,64... | collective-permute-start | bytes 1572872 | tf_op jit(solution)/shard_map/ppermute | solution.py:249
  89.3 14.2 %copy-start = (bf16[2,4,4,16,1024]{4,3,2,1,0:T(8,128)(2,1)}, bf16[2,4,4,16,1024]{4,3,2,1,0:T(8,128)(2,1)S(1)}, u32[]{:S(2)}) copy-start(bf16[2,4,4,16,1024]{4,3,2,1,0:T(8,128)(2,1)S(1)} %shard_map.61.refs_0_) | copy-start | bytes 3145732
  89.3 8.4 %collective-permute-start.6 = (bf16[2,4,4,16,1024]{4,3,2,1,0:T(8,128)(2,1)S(1)}, bf16[2,4,4,16,1024]{4,3,2,1,0:T(8,128)(2,1)S(1)}, u32[]{:S(2)}, u32[]{:S(2)}) collective-permute-start(bf16[2,4,4,16,1024]{4,3,2,1,0:T(8,128)(2,1)S(1)} %shard_map.61.refs_0_), channel_id=1, source_target_pairs={{0,4},{4,0},{1,5},{5,1},{2,6},{6,2},{3,7},{7,3},{8,12},{12,8},{9,1... | collective-permute-start | bytes 3145736 | tf_op jit(solution)/shard_map/ppermute | solution.py:315
  94.9 8.6 %copy-start.1 = (bf16[2,4,4,16,1024]{4,3,2,1,0:T(8,128)(2,1)}, bf16[2,4,4,16,1024]{4,3,2,1,0:T(8,128)(2,1)S(1)}, u32[]{:S(2)}) copy-start(bf16[2,4,4,16,1024]{4,3,2,1,0:T(8,128)(2,1)S(1)} %shard_map.62.refs_1_) | copy-start | bytes 3145732
  94.9 5.1 %collective-permute-start.7 = (bf16[2,4,4,16,1024]{4,3,2,1,0:T(8,128)(2,1)S(1)}, bf16[2,4,4,16,1024]{4,3,2,1,0:T(8,128)(2,1)}, u32[]{:S(2)}, u32[]{:S(2)}) collective-permute-start(bf16[2,4,4,16,1024]{4,3,2,1,0:T(8,128)(2,1)S(1)} %shard_map.62.refs_1_), channel_id=1, source_target_pairs={{0,4},{4,0},{1,5},{5,1},{2,6},{6,2},{3,7},{7,3},{8,12},{12,8},{9,1... | collective-permute-start | bytes 3145736 | tf_op jit(solution)/shard_map/ppermute | solution.py:315
  97.7 5.8 %copy-start.7 = (bf16[2,4,4,16,1024]{4,3,2,1,0:T(8,128)(2,1)}, bf16[2,4,4,16,1024]{4,3,2,1,0:T(8,128)(2,1)S(1)}, u32[]{:S(2)}) copy-start(bf16[2,4,4,16,1024]{4,3,2,1,0:T(8,128)(2,1)S(1)} %collective-permute-done.6.refs_2_) | copy-start | bytes 3145732

commit v7 on v6

--- a/solution.py
+++ b/solution.py
@@ -162,39 +162,39 @@
     zl = lax.axis_index(ZL)
     y = lax.axis_index(Y)
     tile = 256
-    copies = []
+
+    def fetch(s, p, n, owner, along):
+        step = NEXT[PLACES[p % 2][n]]
+        if along:
+            to = w_ref.at[s, lax.rem(zl + step, 4), :, owner]
+        else:
+            to = w_ref.at[s, :, lax.rem(y + step, 4), owner]
+        return pltpu.make_async_copy(pieces[p].at[n, s], to, sem.at[s, 2 * p + n])
+
+    def part(s):
+        return pltpu.make_async_copy(h_hbm.at[s], h_ref.at[s], sem.at[s, 8])
+
+    def start(me):
+        for s in range(parts):
+            part(s).start()
+            for p in range(4):
+                owner = me if p < 2 else 1 - me
+                for n in range(2):
+                    fetch(s, p, n, owner, owner == 0).start()
+
+    @pl.when(core == 0)
+    def _():
+        start(0)
+
+    @pl.when(core == 1)
+    def _():
+        start(1)
+
     for s in range(parts):
-        copies.append([pltpu.make_async_copy(h_hbm.at[s], h_ref.at[s], sem.at[s, 16])])
-        copies[s][0].start()
-        for p, piece in enumerate(pieces):
-            owner = core if p < 2 else 1 - core
+        part(s).wait()
+        for p in range(4):
             for n in range(2):
-                step = NEXT[PLACES[p % 2][n]]
-                down = w_ref.at[s, :, lax.rem(y + step, 4), owner]
-                along = w_ref.at[s, lax.rem(zl + step, 4), :, owner]
-                by_y = pltpu.make_async_copy(piece.at[n, s], down, sem.at[s, 2 * p + n])
-                by_z = pltpu.make_async_copy(piece.at[n, s], along, sem.at[s, 8 + 2 * p + n])
-                copies[s].append((owner, by_y, by_z))
-
-                @pl.when(owner == 1)
-                def _():
-                    by_y.start()
-
-                @pl.when(owner == 0)
-                def _():
-                    by_z.start()
-
-    for s in range(parts):
-        copies[s][0].wait()
-        for owner, by_y, by_z in copies[s][1:]:
-            @pl.when(owner == 1)
-            def _():
-                by_y.wait()
-
-            @pl.when(owner == 0)
-            def _():
-                by_z.wait()
-
+                fetch(s, p, n, 0, True).wait()
         last = s == parts - 1
         if last:
             row = jnp.zeros((1, rows), F32)
@@ -322,7 +322,7 @@
             pltpu.VMEM((far, 4, 4, 2, *out_weight.shape), BF16),
             pltpu.VMEM((rows, cols), F32),
             pltpu.VMEM((rows, cols), BF16),
-            pltpu.SemaphoreType.DMA((group, 17)),
+            pltpu.SemaphoreType.DMA((group, 9)),
             pltpu.SemaphoreType.DMA((2,)),
         ],
         grant=60,

time: 110 us -> 109 us (level)
  no operation moved by 1% of the time
where the time goes in v7:
time: 109 us
  blocking collectives  42.6 us (39%)
  starting transfers between devices  38.2 us (35%)
  Pallas kernels  12.4 us (11%)
  waiting for transfers between devices  12.2 us (11%)
  local copies, waits for them, and re-layouts  1.82 us (2%)
    all_to_all x2, blocking collectives, swap(): return lax.all_to_all(array, axes, 0, 0, tiled=True)  42.6 us
    ppermute x6, starting transfers between devices, moved(): return lax.ppermute(array, SEQ, pairs)  17.1 us
    all_to_all x2, starting transfers between devices, swap(): return lax.all_to_all(array, axes, 0, 0, tiled=True)  15.6 us
    ppermute x6, waiting for transfers between devices, moved(): return lax.ppermute(array, SEQ, pairs)  6.42 us
    ppermute x2, starting transfers between devices, per_device(): halves.append(lax.ppermute(halves[n], C, ((0, 1), (1, 0))))  5.48 us
    pallas_call x1, Pallas kernels, per_device(): call(project_body, bf16((rows, cols)), 5, 2 * 10 ** 9, 8 * 2 ** 20, in_sp...  5.05 us
    all_to_all x2, waiting for transfers between devices, swap(): return lax.all_to_all(array, axes, 0, 0, tiled=True)  3.42 us
    pallas_call x1, Pallas kernels, per_device(): call(state_body, (f32((heads, HD, HD)), bf16(out_weight.shape)), 3, 10 **...  2.4 us
  transfers between devices with their start and end apart: 10, of which 5 were waited for; matrix products, arithmetic and copies ran while one was open for 1% of the time, Pallas kernels for 4%

profile of v7, /device:TPU:17, one launch (start us, length us, event | category | flops | bytes accessed | tf_op | source)
XLA Modules:
  0.0 108.5 jit_solution(9762818199656437879)
XLA Ops:
  0.0 2.4 %shard_map.55 = (f32[4,128,128]{2,1,0:T(8,128)}, bf16[16,1024]{1,0:T(8,128)(2,1)}) custom-call(bf16[512,512]{1,0:T(8,128)(2,1)} %k_ref.1, bf16[512,512]{1,0:T(8,128)(2,1)} %v_ref.1, bf16[16,1024]{1,0:T(8,128)(2,1)} %w_hbm.1), custom_call_target="tpu_custom_call" | custom-call | flops 100000000 | bytes 1048576 | tf_op jit(solution)/shard_map/pallas_call | solution.py:263
  2.4 18.4 %all_to_all.20.r_ref = f32[32,16,128]{2,1,0:T(8,128)S(1)} all-to-all(f32[32,16,128]{2,1,0:T(8,128)} %bitcast.8), channel_id=1, replica_groups=mesh['zh'=4,'zl'=4,'y'=4,'c'=2,'x'=4] {'zl','y','c'}, dimensions={0} | all-to-all | bytes 524288 | tf_op jit(solution)/shard_map/all_to_all | solution.py:232
  20.8 0.8 copy-done.6
  21.6 24.3 %all_to_all.21.t_ref = bf16[4,16,1280]{2,1,0:T(8,128)(2,1)S(1)} all-to-all(bf16[4,16,1280]{2,1,0:T(8,128)(2,1)S(1)} %get-tuple-element.18), channel_id=1, replica_groups=mesh['zh'=4,'zl'=4,'y'=4,'c'=2,'x'=4] {'zh'}, dimensions={0} | all-to-all | bytes 327680 | tf_op jit(solution)/shard_map/all_to_all | solution.py:232
  45.9 0.7 shard_map.57
  46.5 11.1 %all-to-all-start.2 = ((bf16[32,16,128]{2,1,0:T(8,128)(2,1)}), bf16[32,16,128]{2,1,0:T(8,128)(2,1)S(1)}, u32[]{:S(2)}, u32[]{:S(2)}) async-start(bf16[32,16,128]{2,1,0:T(8,128)(2,1)} %get-tuple-element.19), calls=%async_computation.2 | async-start | bytes 262144 | tf_op jit(solution)/shard_map/all_to_all | solution.py:232
  57.7 4.0 %collective-permute-start.2 = (bf16[4,16,1024]{2,1,0:T(8,128)(2,1)S(1)}, bf16[4,16,1024]{2,1,0:T(8,128)(2,1)S(1)}, u32[]{:S(2)}, u32[]{:S(2)}) collective-permute-start(bf16[4,16,1024]{2,1,0:T(8,128)(2,1)S(1)} %get-tuple-element.21), channel_id=1, source_target_pairs={{0,16},{4,68},{8,24},{12,76},{16,0},{20,84},{24,8},{28,92},{32,48}... | collective-permute-start | bytes 393224 | tf_op jit(solution)/shard_map/ppermute | solution.py:249
  61.7 1.9 %collective-permute-start.1 = (bf16[4,16,1024]{2,1,0:T(8,128)(2,1)S(1)}, bf16[4,16,1024]{2,1,0:T(8,128)(2,1)}, u32[]{:S(2)}, u32[]{:S(2)}) collective-permute-start(bf16[4,16,1024]{2,1,0:T(8,128)(2,1)S(1)} %get-tuple-element.21), channel_id=1, source_target_pairs={{0,24},{4,484},{8,0},{12,492},{16,8},{20,500},{24,16},{28,508},{32... | collective-permute-start | bytes 393224 | tf_op jit(solution)/shard_map/ppermute | solution.py:249
  63.6 3.4 %collective-permute-start = (bf16[4,16,1024]{2,1,0:T(8,128)(2,1)S(1)}, bf16[4,16,1024]{2,1,0:T(8,128)(2,1)}, u32[]{:S(2)}, u32[]{:S(2)}) collective-permute-start(bf16[4,16,1024]{2,1,0:T(8,128)(2,1)S(1)} %get-tuple-element.21), channel_id=1, source_target_pairs={{0,8},{4,36},{8,16},{12,44},{16,24},{20,52},{24,0},{28,60},{32,40}... | collective-permute-start | bytes 393224 | tf_op jit(solution)/shard_map/ppermute | solution.py:249
  67.0 0.3 shard_map.59.g_ref
  67.3 0.0 copy-start.4
  67.3 1.0 copy-done.4
  68.4 1.4 %shard_map.58.l_ref = f32[512,512]{1,0:T(8,128)S(1)} custom-call(bf16[512,512]{1,0:T(8,128)(2,1)S(1)} %copy-done.2, bf16[512,512]{1,0:T(8,128)(2,1)S(1)} %copy-done.3, bf16[512,512]{1,0:T(8,128)(2,1)S(1)} %copy-done.4), custom_call_target="tpu_custom_call" | custom-call | flops 500000000 | bytes 2097152 | tf_op jit(solution)/shard_map/pallas_call | solution.py:269
  69.8 0.0 all-to-all-done.2
  69.8 1.6 %shard_map.60 = bf16[4,528,512]{2,1,0:T(8,128)(2,1)} custom-call(bf16[512,512]{1,0:T(8,128)(2,1)S(1)} %copy-done.2, bf16[4,128,128]{2,1,0:T(8,128)(2,1)S(1)} %bitcast.6, f32[512,512]{1,0:T(8,128)S(1)} %shard_map.58.l_ref, f32[512,512]{1,0:T(8,128)S(1)} %shard_map.59.g_ref), custom_call_target="tpu_custom_call" | custom-call | flops 100000000 | bytes 4194304 | tf_op jit(solution)/shard_map/pallas_call | solution.py:286
  71.5 4.5 %all-to-all-start.3 = ((bf16[4,528,512]{2,1,0:T(8,128)(2,1)}), bf16[4,528,512]{2,1,0:T(8,128)(2,1)}, u32[]{:S(2)}, u32[]{:S(2)}) async-start(bf16[4,528,512]{2,1,0:T(8,128)(2,1)} %shard_map.60), calls=%async_computation.3 | async-start | bytes 4325376 | tf_op jit(solution)/shard_map/all_to_all | solution.py:232
  76.0 0.0 collective-permute-done.2
  76.0 0.0 collective-permute-done.1
  76.0 1.0 pad_maximum_fusion.refs_0_
  77.0 2.2 %collective-permute-start.3 = (bf16[4,4,16,1024]{3,2,1,0:T(8,128)(2,1)S(1)}, bf16[4,4,16,1024]{3,2,1,0:T(8,128)(2,1)S(1)}, u32[]{:S(2)}, u32[]{:S(2)}) collective-permute-start(bf16[4,4,16,1024]{3,2,1,0:T(8,128)(2,1)S(1)} %pad_maximum_fusion.refs_0_), channel_id=1, source_target_pairs={{0,64},{4,20},{8,72},{12,28},{16,80},{20,4},{24,88},{28,12},{32,48... | collective-permute-start | bytes 1572872 | tf_op jit(solution)/shard_map/ppermute | solution.py:249
  79.2 3.7 %collective-permute-start.5 = (bf16[4,4,16,1024]{3,2,1,0:T(8,128)(2,1)S(1)}, bf16[4,4,16,1024]{3,2,1,0:T(8,128)(2,1)S(1)}, u32[]{:S(2)}, u32[]{:S(2)}) collective-permute-start(bf16[4,4,16,1024]{3,2,1,0:T(8,128)(2,1)S(1)} %pad_maximum_fusion.refs_0_), channel_id=1, source_target_pairs={{0,480},{4,28},{8,488},{12,4},{16,496},{20,12},{24,504},{28,20},{3... | collective-permute-start | bytes 1572872 | tf_op jit(solution)/shard_map/ppermute | solution.py:249
  83.0 1.9 %collective-permute-start.4 = (bf16[4,4,16,1024]{3,2,1,0:T(8,128)(2,1)S(1)}, bf16[4,4,16,1024]{3,2,1,0:T(8,128)(2,1)S(1)}, u32[]{:S(2)}, u32[]{:S(2)}) collective-permute-start(bf16[4,4,16,1024]{3,2,1,0:T(8,128)(2,1)S(1)} %pad_maximum_fusion.refs_0_), channel_id=1, source_target_pairs={{0,32},{4,12},{8,40},{12,20},{16,48},{20,28},{24,56},{28,4},{32,64... | collective-permute-start | bytes 1572872 | tf_op jit(solution)/shard_map/ppermute | solution.py:249
  84.9 4.0 %collective-permute-done.3.refs_1_ = bf16[4,4,16,1024]{3,2,1,0:T(8,128)(2,1)S(1)} collective-permute-done((bf16[4,4,16,1024]{3,2,1,0:T(8,128)(2,1)S(1)}, bf16[4,4,16,1024]{3,2,1,0:T(8,128)(2,1)S(1)}, u32[]{:S(2)}, u32[]{:S(2)}) %collective-permute-start.3) | collective-permute-done | bytes 524320 | tf_op jit(solution)/shard_map/ppermute | solution.py:249
  88.9 0.4 shard_map.61.refs_0_
  89.3 2.8 %collective-permute-start.6 = (bf16[2,4,4,16,1024]{4,3,2,1,0:T(8,128)(2,1)S(1)}, bf16[2,4,4,16,1024]{4,3,2,1,0:T(8,128)(2,1)S(1)}, u32[]{:S(2)}, u32[]{:S(2)}) collective-permute-start(bf16[2,4,4,16,1024]{4,3,2,1,0:T(8,128)(2,1)S(1)} %shard_map.61.refs_0_), channel_id=1, source_target_pairs={{0,4},{4,0},{1,5},{5,1},{2,6},{6,2},{3,7},{7,3},{8,12},{12,8},{9,1... | collective-permute-start | bytes 3145736 | tf_op jit(solution)/shard_map/ppermute | solution.py:315
  92.1 1.6 %collective-permute-done.5.refs_1_ = bf16[4,4,16,1024]{3,2,1,0:T(8,128)(2,1)S(1)} collective-permute-done((bf16[4,4,16,1024]{3,2,1,0:T(8,128)(2,1)S(1)}, bf16[4,4,16,1024]{3,2,1,0:T(8,128)(2,1)S(1)}, u32[]{:S(2)}, u32[]{:S(2)}) %collective-permute-start.5) | collective-permute-done | bytes 524320 | tf_op jit(solution)/shard_map/ppermute | solution.py:249
  93.6 0.9 collective-permute-done.4.refs_0_
  94.5 0.4 shard_map.62.refs_1_
  94.9 2.7 %collective-permute-start.7 = (bf16[2,4,4,16,1024]{4,3,2,1,0:T(8,128)(2,1)S(1)}, bf16[2,4,4,16,1024]{4,3,2,1,0:T(8,128)(2,1)}, u32[]{:S(2)}, u32[]{:S(2)}) collective-permute-start(bf16[2,4,4,16,1024]{4,3,2,1,0:T(8,128)(2,1)S(1)} %shard_map.62.refs_1_), channel_id=1, source_target_pairs={{0,4},{4,0},{1,5},{5,1},{2,6},{6,2},{3,7},{7,3},{8,12},{12,8},{9,1... | collective-permute-start | bytes 3145736 | tf_op jit(solution)/shard_map/ppermute | solution.py:315
  97.7 2.4 %collective-permute-done.7.refs_3_ = bf16[2,4,4,16,1024]{4,3,2,1,0:T(8,128)(2,1)} collective-permute-done((bf16[2,4,4,16,1024]{4,3,2,1,0:T(8,128)(2,1)S(1)}, bf16[2,4,4,16,1024]{4,3,2,1,0:T(8,128)(2,1)}, u32[]{:S(2)}, u32[]{:S(2)}) %collective-permute-start.7) | collective-permute-done | bytes 1048608 | tf_op jit(solution)/shard_map/ppermute | solution.py:315
  100.0 3.4 %all-to-all-done.3.h_hbm = bf16[4,528,512]{2,1,0:T(8,128)(2,1)} async-done(((bf16[4,528,512]{2,1,0:T(8,128)(2,1)}), bf16[4,528,512]{2,1,0:T(8,128)(2,1)}, u32[]{:S(2)}, u32[]{:S(2)}) %all-to-all-start.3) | async-done | bytes 2162720 | tf_op jit(solution)/shard_map/all_to_all | solution.py:232
  103.5 5.0 %shard_map.63 = bf16[512,1024]{1,0:T(8,128)(2,1)} custom-call(bf16[4,528,512]{2,1,0:T(8,128)(2,1)} %all-to-all-done.3.h_hbm, bf16[2,4,4,16,1024]{4,3,2,1,0:T(8,128)(2,1)} %copy-done, bf16[2,4,4,16,1024]{4,3,2,1,0:T(8,128)(2,1)} %copy-done.1, bf16[2,4,4,16,1024]{4,3,2,1,0:T(8,128)(2,1)} %copy-done.7, bf16[2,4,4,16,1024]{4,3,2,1,0:T(8,128)(2,1)} %collective-permute-done.7.refs_3_), custom_call_target="tpu_custom_call" | custom-call | flops 2000000000 | bytes 8388608 | tf_op jit(solution)/shard_map/pallas_call | solution.py:316
  (16 shorter events, 0.1 us)
Async XLA Ops:
  0.0 67.3 %copy-start.3 = (bf16[512,512]{1,0:T(8,128)(2,1)S(1)}, bf16[512,512]{1,0:T(8,128)(2,1)}, u32[]{:S(2)}) copy-start(bf16[512,512]{1,0:T(8,128)(2,1)} %k_ref.1) | copy-start | bytes 1572868
  0.0 67.0 %copy-start.5 = (bf16[512,512]{1,0:T(8,128)(2,1)S(1)}, bf16[512,512]{1,0:T(8,128)(2,1)}, u32[]{:S(2)}) copy-start(bf16[512,512]{1,0:T(8,128)(2,1)} %g_ref.1) | copy-start | bytes 1572868
  0.0 67.3 %copy-start.2 = (bf16[512,512]{1,0:T(8,128)(2,1)S(1)}, bf16[512,512]{1,0:T(8,128)(2,1)}, u32[]{:S(2)}) copy-start(bf16[512,512]{1,0:T(8,128)(2,1)} %q_ref.3) | copy-start | bytes 1572868
  20.8 0.8 copy-start.6
  46.5 23.3 %all-to-all-start.2 = ((bf16[32,16,128]{2,1,0:T(8,128)(2,1)}), bf16[32,16,128]{2,1,0:T(8,128)(2,1)S(1)}, u32[]{:S(2)}, u32[]{:S(2)}) async-start(bf16[32,16,128]{2,1,0:T(8,128)(2,1)} %get-tuple-element.19), calls=%async_computation.2 | async-start | bytes 262144 | tf_op jit(solution)/shard_map/all_to_all | solution.py:232
  57.7 18.3 %collective-permute-start.2 = (bf16[4,16,1024]{2,1,0:T(8,128)(2,1)S(1)}, bf16[4,16,1024]{2,1,0:T(8,128)(2,1)S(1)}, u32[]{:S(2)}, u32[]{:S(2)}) collective-permute-start(bf16[4,16,1024]{2,1,0:T(8,128)(2,1)S(1)} %get-tuple-element.21), channel_id=1, source_target_pairs={{0,16},{4,68},{8,24},{12,76},{16,0},{20,84},{24,8},{28,92},{32,48}... | collective-permute-start | bytes 393224 | tf_op jit(solution)/shard_map/ppermute | solution.py:249
  61.7 14.3 %collective-permute-start.1 = (bf16[4,16,1024]{2,1,0:T(8,128)(2,1)S(1)}, bf16[4,16,1024]{2,1,0:T(8,128)(2,1)}, u32[]{:S(2)}, u32[]{:S(2)}) collective-permute-start(bf16[4,16,1024]{2,1,0:T(8,128)(2,1)S(1)} %get-tuple-element.21), channel_id=1, source_target_pairs={{0,24},{4,484},{8,0},{12,492},{16,8},{20,500},{24,16},{28,508},{32... | collective-permute-start | bytes 393224 | tf_op jit(solution)/shard_map/ppermute | solution.py:249
  63.6 12.4 %collective-permute-start = (bf16[4,16,1024]{2,1,0:T(8,128)(2,1)S(1)}, bf16[4,16,1024]{2,1,0:T(8,128)(2,1)}, u32[]{:S(2)}, u32[]{:S(2)}) collective-permute-start(bf16[4,16,1024]{2,1,0:T(8,128)(2,1)S(1)} %get-tuple-element.21), channel_id=1, source_target_pairs={{0,8},{4,36},{8,16},{12,44},{16,24},{20,52},{24,0},{28,60},{32,40}... | collective-permute-start | bytes 393224 | tf_op jit(solution)/shard_map/ppermute | solution.py:249
  67.3 1.0 copy-start.4
  71.5 32.0 %all-to-all-start.3 = ((bf16[4,528,512]{2,1,0:T(8,128)(2,1)}), bf16[4,528,512]{2,1,0:T(8,128)(2,1)}, u32[]{:S(2)}, u32[]{:S(2)}) async-start(bf16[4,528,512]{2,1,0:T(8,128)(2,1)} %shard_map.60), calls=%async_computation.3 | async-start | bytes 4325376 | tf_op jit(solution)/shard_map/all_to_all | solution.py:232
  77.0 11.8 %collective-permute-start.3 = (bf16[4,4,16,1024]{3,2,1,0:T(8,128)(2,1)S(1)}, bf16[4,4,16,1024]{3,2,1,0:T(8,128)(2,1)S(1)}, u32[]{:S(2)}, u32[]{:S(2)}) collective-permute-start(bf16[4,4,16,1024]{3,2,1,0:T(8,128)(2,1)S(1)} %pad_maximum_fusion.refs_0_), channel_id=1, source_target_pairs={{0,64},{4,20},{8,72},{12,28},{16,80},{20,4},{24,88},{28,12},{32,48... | collective-permute-start | bytes 1572872 | tf_op jit(solution)/shard_map/ppermute | solution.py:249
  79.2 14.4 %collective-permute-start.5 = (bf16[4,4,16,1024]{3,2,1,0:T(8,128)(2,1)S(1)}, bf16[4,4,16,1024]{3,2,1,0:T(8,128)(2,1)S(1)}, u32[]{:S(2)}, u32[]{:S(2)}) collective-permute-start(bf16[4,4,16,1024]{3,2,1,0:T(8,128)(2,1)S(1)} %pad_maximum_fusion.refs_0_), channel_id=1, source_target_pairs={{0,480},{4,28},{8,488},{12,4},{16,496},{20,12},{24,504},{28,20},{3... | collective-permute-start | bytes 1572872 | tf_op jit(solution)/shard_map/ppermute | solution.py:249
  83.0 11.5 %collective-permute-start.4 = (bf16[4,4,16,1024]{3,2,1,0:T(8,128)(2,1)S(1)}, bf16[4,4,16,1024]{3,2,1,0:T(8,128)(2,1)S(1)}, u32[]{:S(2)}, u32[]{:S(2)}) collective-permute-start(bf16[4,4,16,1024]{3,2,1,0:T(8,128)(2,1)S(1)} %pad_maximum_fusion.refs_0_), channel_id=1, source_target_pairs={{0,32},{4,12},{8,40},{12,20},{16,48},{20,28},{24,56},{28,4},{32,64... | collective-permute-start | bytes 1572872 | tf_op jit(solution)/shard_map/ppermute | solution.py:249
  89.3 14.2 %copy-start = (bf16[2,4,4,16,1024]{4,3,2,1,0:T(8,128)(2,1)}, bf16[2,4,4,16,1024]{4,3,2,1,0:T(8,128)(2,1)S(1)}, u32[]{:S(2)}) copy-start(bf16[2,4,4,16,1024]{4,3,2,1,0:T(8,128)(2,1)S(1)} %shard_map.61.refs_0_) | copy-start | bytes 3145732
  89.3 8.4 %collective-permute-start.6 = (bf16[2,4,4,16,1024]{4,3,2,1,0:T(8,128)(2,1)S(1)}, bf16[2,4,4,16,1024]{4,3,2,1,0:T(8,128)(2,1)S(1)}, u32[]{:S(2)}, u32[]{:S(2)}) collective-permute-start(bf16[2,4,4,16,1024]{4,3,2,1,0:T(8,128)(2,1)S(1)} %shard_map.61.refs_0_), channel_id=1, source_target_pairs={{0,4},{4,0},{1,5},{5,1},{2,6},{6,2},{3,7},{7,3},{8,12},{12,8},{9,1... | collective-permute-start | bytes 3145736 | tf_op jit(solution)/shard_map/ppermute | solution.py:315
  94.9 8.6 %copy-start.1 = (bf16[2,4,4,16,1024]{4,3,2,1,0:T(8,128)(2,1)}, bf16[2,4,4,16,1024]{4,3,2,1,0:T(8,128)(2,1)S(1)}, u32[]{:S(2)}) copy-start(bf16[2,4,4,16,1024]{4,3,2,1,0:T(8,128)(2,1)S(1)} %shard_map.62.refs_1_) | copy-start | bytes 3145732
  94.9 5.1 %collective-permute-start.7 = (bf16[2,4,4,16,1024]{4,3,2,1,0:T(8,128)(2,1)S(1)}, bf16[2,4,4,16,1024]{4,3,2,1,0:T(8,128)(2,1)}, u32[]{:S(2)}, u32[]{:S(2)}) collective-permute-start(bf16[2,4,4,16,1024]{4,3,2,1,0:T(8,128)(2,1)S(1)} %shard_map.62.refs_1_), channel_id=1, source_target_pairs={{0,4},{4,0},{1,5},{5,1},{2,6},{6,2},{3,7},{7,3},{8,12},{12,8},{9,1... | collective-permute-start | bytes 3145736 | tf_op jit(solution)/shard_map/ppermute | solution.py:315
  97.7 5.8 %copy-start.7 = (bf16[2,4,4,16,1024]{4,3,2,1,0:T(8,128)(2,1)}, bf16[2,4,4,16,1024]{4,3,2,1,0:T(8,128)(2,1)S(1)}, u32[]{:S(2)}) copy-start(bf16[2,4,4,16,1024]{4,3,2,1,0:T(8,128)(2,1)S(1)} %collective-permute-done.6.refs_2_) | copy-start | bytes 3145732
